TPU v7x, 32 devices: a whole 2x2x4 slice. The times are simulated.
32 devices in a mesh: groups: 2 (over y), seg: 4 (over z), bin: 4 (over x, core).
Axes of the slice: x: 2, y: 2, z: 4, core: 2. Of those that a mesh axis runs over, the one named last changes fastest.
Arguments:
- start_factors: float32 [4096, 128], P(('groups', 'seg', 'bin')), parts along dimension 0, may hold values from -6 to 6
- bin_factors: bfloat16 [8192, 128], P(('groups', 'bin')), parts along dimension 0, may hold values from -0.5 to 0.5
- tile_speed: bfloat16 [8, 4, 12, 128, 128], P(('groups', 'seg'), 'bin'), parts along dimension 0, may hold values from -6 to 6
- tile_weight: bfloat16 [8, 4, 12, 128, 128], P(('groups', 'seg'), 'bin'), parts along dimension 0, may hold values from 0.099609375 to 2
- tile_cells: int32 [8, 4, 12, 2], P(('groups', 'seg'), 'bin'), parts along dimension 0, may hold values from 0 to 7, as said below
- tile_count: int32 [8, 4], P(('groups', 'seg'), 'bin'), parts along dimension 0, may hold values from 1 to 12, as said below
- inner_pairs: int32 [8, 4, 2, 2], P(('groups', 'seg'), 'bin'), parts along dimension 0, may hold values from 0 to 3, as said below
- inner_weight: float32 [8, 4, 2, 128, 128], P(('groups', 'seg'), 'bin'), parts along dimension 0, may hold values from 0 to 0.00390625
- face_rows: int32 [8, 4, 2, 256], P(('groups', 'seg'), 'bin'), parts along dimension 0, may hold values from 0 to 511, as said below
- face_count: int32 [8, 4, 2], P(('groups', 'seg'), 'bin'), parts along dimension 0, may hold values from 128 to 256, as said below
- face_weight: float32 [8, 4, 256, 256], P(('groups', 'seg'), 'bin'), parts along dimension 0, may hold values from 0 to 0.00390625
Outputs:
- solution_factors: float32 [4096, 128], P(('groups', 'seg', 'bin')), parts along dimension 0
- residual: float32 [4096, 128], P(('groups', 'seg', 'bin')), parts along dimension 0
There are 2 independent parts, one for each index of `groups`. A program takes and returns all parts, laid end to end along the dimension named above; each array names one. Nothing has to cross between parts.
Inputs may be any that keep to these rules, and one draw needn't show every extreme that they name: `tile_cells`: the 12 slots of one device name different pairs; the first entry is a segment block of the partition, the second a bin block of the device's bins. `tile_count`: some device of every draw has all 12 slots live. `inner_pairs`: the two blocks of a pair differ; both are segment blocks of the partition. `face_rows`: row numbers within the partition, different within each face list. `face_count`: some face list of every draw has all 256 rows live.
All inputs are finite; a program needn't handle non-finite values.
Results may differ from a plain program's by a relative error of at most 0.0024.
Values sent between devices are 32-bit elements; how exact they have to be, the bound alone decides.
No kernel may reach another device: no remote copies, remote signals or barrier semaphores. Data moves between devices by JAX's collectives and lax.ppermute only.
A program may use at most 64 MiB of HBM per device.

v0:
```python
import jax
import jax.numpy as jnp
from jax import lax
from jax.sharding import PartitionSpec as P

ITERS = 2


highest = lax.Precision.HIGHEST
ridge_weight = 0.5


def from_behind(x, axis, by):
    devices = lax.axis_size(axis)
    pairs = [(i, i + by) for i in range(devices) if 0 <= i + by < devices]
    return lax.ppermute(x, axis, pairs)


def shards(
    start_factors,
    bin_factors,
    tile_speed,
    tile_weight,
    tile_cells,
    tile_count,
    inner_pairs,
    inner_weight,
    face_rows,
    face_count,
    face_weight,
):
    speeds = tile_speed[0, 0]
    weights = tile_weight[0, 0]
    cells = tile_cells[0, 0]
    n_tiles = speeds.shape[0]
    tile_size = speeds.shape[1]
    own_rows = start_factors.shape[0]
    width = start_factors.shape[1]
    part_rows = own_rows * lax.axis_size("bin")
    part_blocks = part_rows // tile_size
    block_ids = jnp.arange(part_blocks, dtype=jnp.int32)
    live_tiles = (jnp.arange(n_tiles, dtype=jnp.int32) < tile_count[0, 0]).astype(jnp.float32)
    tile_bins = bin_factors.reshape(-1, tile_size, width)[cells[:, 1]]
    bins_wide = tile_bins.astype(jnp.float32)
    tile_gain = weights.astype(jnp.float32) * live_tiles[:, None, None]
    tile_onehot = (cells[:, 0][:, None] == block_ids[None, :]).astype(jnp.float32)
    weighted = (weights.astype(jnp.float32) * speeds.astype(jnp.float32)).astype(jnp.bfloat16)
    rhs_terms = jnp.einsum("kij,kjr->kir", weighted, tile_bins, preferred_element_type=jnp.float32)
    rhs_terms = rhs_terms * live_tiles[:, None, None]
    rhs_part = jnp.einsum("kb,kir->bir", tile_onehot, rhs_terms, precision=highest).reshape(
        part_rows, width
    )
    pairs = inner_pairs[0, 0]
    pair_weight = inner_weight[0, 0]
    left_onehot = (pairs[:, 0][:, None] == block_ids[None, :]).astype(jnp.float32)
    right_onehot = (pairs[:, 1][:, None] == block_ids[None, :]).astype(jnp.float32)
    left_degree = pair_weight.sum(2)
    right_degree = pair_weight.sum(1)
    rows_low = face_rows[0, 0, 0]
    rows_up = face_rows[0, 0, 1]
    face_slots = jnp.arange(rows_low.shape[0], dtype=jnp.int32)
    mask_low = (face_slots < face_count[0, 0, 0]).astype(jnp.float32)
    mask_up = (face_slots < face_count[0, 0, 1]).astype(jnp.float32)
    upper_count = face_count[0, 0, 1:2]
    face_block = face_weight[0, 0]

    def apply_local(whole_rows):
        blocks = whole_rows.reshape(part_blocks, tile_size, width)
        picked = blocks[cells[:, 0]]
        scores = jnp.einsum("kir,kjr->kij", picked, bins_wide, precision=highest) * tile_gain
        pulled = jnp.einsum("kij,kjr->kir", scores, bins_wide, precision=highest)
        left = blocks[pairs[:, 0]]
        right = blocks[pairs[:, 1]]
        to_left = left_degree[..., None] * left - jnp.einsum(
            "kij,kjr->kir", pair_weight, right, precision=highest
        )
        to_right = right_degree[..., None] * right - jnp.einsum(
            "kij,kir->kjr", pair_weight, left, precision=highest
        )
        summed = jnp.einsum("kb,kir->bir", tile_onehot, pulled, precision=highest)
        summed = summed + jnp.einsum("kb,kir->bir", left_onehot, to_left, precision=highest)
        summed = summed + jnp.einsum("kb,kir->bir", right_onehot, to_right, precision=highest)
        summed = summed.reshape(part_rows, width)
        own_face = whole_rows[rows_low] * mask_low[:, None]
        upper_face = whole_rows[rows_up] * mask_up[:, None]
        lower_face, lower_count = from_behind((upper_face, upper_count), "seg", 1)
        lower_mask = (face_slots < lower_count[0]).astype(jnp.float32)
        coupling = face_block * mask_low[:, None] * lower_mask[None, :]
        own_term = coupling.sum(1)[:, None] * own_face - jnp.dot(
            coupling, lower_face, precision=highest
        )
        answer = coupling.sum(0)[:, None] * lower_face - jnp.dot(
            coupling.T, own_face, precision=highest
        )
        returned = from_behind(answer, "seg", -1)
        return summed.at[rows_low].add(own_term).at[rows_up].add(returned)

    def reduce_rows(partial_value):
        reduced = lax.psum_scatter(partial_value, "bin", scatter_dimension=0, tiled=True)
        return reduced

    def spread(vector):
        whole_rows = lax.all_gather(vector, "bin", axis=0, tiled=True)
        return whole_rows

    def fold_sum(values):
        folded = lax.psum((values[0], values[1]), ("seg", "bin"))
        return folded

    def image_of(vector):
        return reduce_rows(apply_local(spread(vector))) + ridge_weight * vector

    start_whole = lax.all_gather(start_factors, "bin", axis=0, tiled=True)
    residual = reduce_rows(rhs_part - apply_local(start_whole)) - ridge_weight * start_factors
    solution = start_factors
    images = image_of(residual)
    norm_now, product = fold_sum((jnp.sum(residual * residual), jnp.sum(residual * images)))
    step_size = norm_now / product
    direction = residual
    along = images
    for iteration in range(ITERS):
        solution = solution + step_size * direction
        residual = residual - step_size * along
        if iteration + 1 < ITERS:
            images = image_of(residual)
            norm_next, product = fold_sum(
                (jnp.sum(residual * residual), jnp.sum(residual * images))
            )
            beta_ratio = norm_next / norm_now
            step_size = norm_next / (product - beta_ratio * norm_next / step_size)
            direction = residual + beta_ratio * direction
            along = images + beta_ratio * along
            norm_now = norm_next
    outputs = (solution, residual)
    return outputs


def solution(mesh):
    return jax.shard_map(
        shards,
        mesh=mesh,
        in_specs=(
            P(("groups", "seg", "bin"), None),
            P(("groups", "bin"), None),
            P(("groups", "seg"), "bin", None, None, None),
            P(("groups", "seg"), "bin", None, None, None),
            P(("groups", "seg"), "bin", None, None),
            P(("groups", "seg"), "bin"),
            P(("groups", "seg"), "bin", None, None),
            P(("groups", "seg"), "bin", None, None, None),
            P(("groups", "seg"), "bin", None, None),
            P(("groups", "seg"), "bin", None),
            P(("groups", "seg"), "bin", None, None),
        ),
        out_specs=(P(("groups", "seg", "bin"), None), P(("groups", "seg", "bin"), None)),
        check_vma=False,
    )
```

profile of v0, /device:TPU:0, one launch (start us, length us, event | category | flops | bytes accessed | tf_op | source)
XLA Modules:
  0.0 242.0 jit_solution(7704379374900717921)
XLA Ops:
  7.2 1.4 fusion.76
  8.6 5.6 %collective-permute-start = (s32[1]{0:T(128)}, s32[1]{0:T(128)}, u32[]{:S(2)}, u32[]{:S(2)}) collective-permute-start(s32[1]{0:T(128)} %bitcast.23), channel_id=1, source_target_pairs={{0,4},{4,8},{8,12},{1,5},{5,9},{9,13},{2,6},{6,10},{10,14},{3,7},{... | collective-permute-start | bytes 20 | tf_op jit(solution)/shard_map/ppermute | solution.py:16
  14.2 6.0 %all_gather.9 = f32[512,128]{1,0:T(8,128)S(1)} all-gather(f32[128,128]{1,0:T(8,128)} %param.11), channel_id=1, replica_groups=mesh['groups'=2,'seg'=4,'bin'=4] {'bin'}, dimensions={0}, use_global_device_ids=true | all-gather | bytes 327680 | tf_op jit(solution)/shard_map/all_gather | solution.py:113
  21.7 3.0 %collective-permute-start.1 = (f32[256,128]{1,0:T(8,128)S(1)}, f32[256,128]{1,0:T(8,128)S(1)}, u32[]{:S(2)}, u32[]{:S(2)}) collective-permute-start(f32[256,128]{1,0:T(8,128)S(1)} %broadcast_multiply_fusion.2), channel_id=1, source_target_pairs={{0,4},{4,8},{8,12},{1,5},{5,9},{9,13},{2,6},{6,10},{10,14},{3,7},{... | collective-permute-start | bytes 393224 | tf_op jit(solution)/shard_map/ppermute | solution.py:16
  40.1 2.0 scatter_fusion
  42.2 3.6 %collective-permute-done.2 = f32[256,128]{1,0:T(8,128)S(1)} collective-permute-done((f32[256,128]{1,0:T(8,128)S(1)}, f32[256,128]{1,0:T(8,128)S(1)}, u32[]{:S(2)}, u32[]{:S(2)}) %collective-permute-start.2) | collective-permute-done | bytes 131104 | tf_op jit(solution)/shard_map/ppermute | solution.py:16
  45.8 2.0 scatter_fusion.1
  48.6 19.4 %reduce-scatter.4.cloned.1.call-done = f32[128,128]{1,0:T(8,128)} async-done(((f32[512,128]{1,0:T(8,128)}), f32[128,128]{1,0:T(8,128)}) %reduce-scatter.4.cloned.1.call-update) | async-done | bytes 65552 | tf_op jit(solution)/shard_map/reduce_scatter | solution.py:99
  68.9 5.8 %all_gather.10 = f32[512,128]{1,0:T(8,128)S(1)} all-gather(f32[128,128]{1,0:T(8,128)S(1)} %multiply_subtract_fusion.5), channel_id=1, replica_groups=mesh['groups'=2,'seg'=4,'bin'=4] {'bin'}, dimensions={0}, use_global_device_ids=true | all-gather | bytes 327680 | tf_op jit(solution)/shard_map/all_gather | solution.py:103
  78.6 3.6 %collective-permute-start.3 = (f32[256,128]{1,0:T(8,128)S(1)}, f32[256,128]{1,0:T(8,128)S(1)}, u32[]{:S(2)}, u32[]{:S(2)}) collective-permute-start(f32[256,128]{1,0:T(8,128)S(1)} %broadcast_multiply_fusion.1), channel_id=1, source_target_pairs={{0,4},{4,8},{8,12},{1,5},{5,9},{9,13},{2,6},{6,10},{10,14},{3,7},{... | collective-permute-start | bytes 393224 | tf_op jit(solution)/shard_map/ppermute | solution.py:16
  88.1 2.0 scatter_fusion.2
  90.2 3.6 %collective-permute-done.4 = f32[256,128]{1,0:T(8,128)S(1)} collective-permute-done((f32[256,128]{1,0:T(8,128)S(1)}, f32[256,128]{1,0:T(8,128)S(1)}, u32[]{:S(2)}, u32[]{:S(2)}) %collective-permute-start.4) | collective-permute-done | bytes 131104 | tf_op jit(solution)/shard_map/ppermute | solution.py:16
  93.7 2.0 scatter_fusion.3
  96.5 19.3 %reduce-scatter.6.cloned.1.call-done = f32[128,128]{1,0:T(8,128)} async-done(((f32[512,128]{1,0:T(8,128)}), f32[128,128]{1,0:T(8,128)}) %reduce-scatter.6.cloned.1.call-update) | async-done | bytes 65552 | tf_op jit(solution)/shard_map/reduce_scatter | solution.py:99
  115.8 1.5 multiply_reduce_fusion.2
  117.4 32.6 %all-reduce.1 = (f32[]{:T(128)}, f32[]{:T(128)}) all-reduce(f32[]{:T(128)} %get-tuple-element.9, f32[]{:T(128)} %get-tuple-element.8), channel_id=1, replica_groups=mesh['groups'=2,'seg'=4,'bin'=4] {'seg','bin'}, use_global_device_ids=true, to_apply=%region_8.0 | all-reduce | flops 2 | bytes 16 | tf_op jit(solution)/shard_map/psum | solution.py:107
  151.4 5.8 %all_gather.11 = f32[512,128]{1,0:T(8,128)S(1)} all-gather(f32[128,128]{1,0:T(8,128)S(1)} %multiply_subtract_fusion.4), channel_id=1, replica_groups=mesh['groups'=2,'seg'=4,'bin'=4] {'bin'}, dimensions={0}, use_global_device_ids=true | all-gather | bytes 327680 | tf_op jit(solution)/shard_map/all_gather | solution.py:103
  166.6 1.5 collective-permute-start.6
  168.6 2.0 scatter_fusion.4
  170.7 3.8 %collective-permute-done.6 = f32[256,128]{1,0:T(8,128)S(1)} collective-permute-done((f32[256,128]{1,0:T(8,128)S(1)}, f32[256,128]{1,0:T(8,128)S(1)}, u32[]{:S(2)}, u32[]{:S(2)}) %collective-permute-start.6) | collective-permute-done | bytes 131104 | tf_op jit(solution)/shard_map/ppermute | solution.py:16
  174.5 2.0 scatter_fusion.5
  177.2 18.6 %reduce-scatter.8.cloned.1.call-done = f32[128,128]{1,0:T(8,128)} async-done(((f32[512,128]{1,0:T(8,128)}), f32[128,128]{1,0:T(8,128)}) %reduce-scatter.8.cloned.1.call-update) | async-done | bytes 65552 | tf_op jit(solution)/shard_map/reduce_scatter | solution.py:99
  195.8 1.6 multiply_reduce_fusion
  197.4 32.7 %all-reduce = (f32[]{:T(128)}, f32[]{:T(128)}) all-reduce(f32[]{:T(128)} %get-tuple-element.7, f32[]{:T(128)} %get-tuple-element.6), channel_id=1, replica_groups=mesh['groups'=2,'seg'=4,'bin'=4] {'seg','bin'}, use_global_device_ids=true, to_apply=%region_15.0 | all-reduce | flops 2 | bytes 16 | tf_op jit(solution)/shard_map/psum | solution.py:107
  (108 shorter events, 39.4 us)
Async XLA Ops:
  7.2 18.9 %copy-start = (bf16[1024,128]{1,0:T(8,128)(2,1)S(1)}, bf16[1024,128]{1,0:T(8,128)(2,1)}, u32[]{:S(2)}) copy-start(bf16[1024,128]{1,0:T(8,128)(2,1)} %param.12) | copy-start | bytes 786436
  7.2 60.8 %reduce-scatter.4.cloned.1.call-start = ((), (), s32[]{:S(2)}) async-start(), calls=%async_computation.3 | async-start | bytes 327680 | tf_op jit(solution)/shard_map/reduce_scatter | solution.py:99
  8.6 11.6 %copy-start.11 = (s32[1,1,2,256]{3,2,1,0:T(2,128)S(1)}, s32[1,1,2,256]{3,2,1,0:T(2,128)}, u32[]{:S(2)}) copy-start(s32[1,1,2,256]{3,2,1,0:T(2,128)} %param.19) | copy-start | bytes 6148
  8.6 28.0 %collective-permute-start = (s32[1]{0:T(128)}, s32[1]{0:T(128)}, u32[]{:S(2)}, u32[]{:S(2)}) collective-permute-start(s32[1]{0:T(128)} %bitcast.23), channel_id=1, source_target_pairs={{0,4},{4,8},{8,12},{1,5},{5,9},{9,13},{2,6},{6,10},{10,14},{3,7},{... | collective-permute-start | bytes 20 | tf_op jit(solution)/shard_map/ppermute | solution.py:16
  21.7 3.0 %copy-start.12 = (s32[1,1,12,2]{2,3,1,0:T(2,128)S(1)}, s32[1,1,12,2]{2,3,1,0:T(2,128)}, u32[]{:S(2)}) copy-start(s32[1,1,12,2]{2,3,1,0:T(2,128)} %param.15) | copy-start | bytes 292
  21.7 16.0 %collective-permute-start.1 = (f32[256,128]{1,0:T(8,128)S(1)}, f32[256,128]{1,0:T(8,128)S(1)}, u32[]{:S(2)}, u32[]{:S(2)}) collective-permute-start(f32[256,128]{1,0:T(8,128)S(1)} %broadcast_multiply_fusion.2), channel_id=1, source_target_pairs={{0,4},{4,8},{8,12},{1,5},{5,9},{9,13},{2,6},{6,10},{10,14},{3,7},{... | collective-permute-start | bytes 393224 | tf_op jit(solution)/shard_map/ppermute | solution.py:16
  26.1 1.0 copy-start.5
  28.5 0.7 copy-start.10
  30.0 0.9 copy-start.4
  34.4 1.0 copy-start.8
  36.6 1.0 copy-start.3
  38.4 7.4 %collective-permute-start.2 = (f32[256,128]{1,0:T(8,128)S(1)}, f32[256,128]{1,0:T(8,128)S(1)}, u32[]{:S(2)}, u32[]{:S(2)}) collective-permute-start(f32[256,128]{1,0:T(8,128)S(1)} %multiply_subtract_fusion.2), channel_id=1, source_target_pairs={{4,0},{8,4},{12,8},{5,1},{9,5},{13,9},{6,2},{10,6},{14,10},{7,3},{... | collective-permute-start | bytes 393224 | tf_op jit(solution)/shard_map/ppermute | solution.py:16
  48.5 19.5 %copy-start.6 = (f32[128,128]{1,0:T(8,128)S(1)}, f32[128,128]{1,0:T(8,128)}, u32[]{:S(2)}) copy-start(f32[128,128]{1,0:T(8,128)} %param.11) | copy-start | bytes 196612
  48.6 67.3 %reduce-scatter.6.cloned.1.call-start = ((), (), s32[]{:S(2)}) async-start(), calls=%async_computation.4 | async-start | bytes 327680 | tf_op jit(solution)/shard_map/reduce_scatter | solution.py:99
  78.6 7.1 %collective-permute-start.3 = (f32[256,128]{1,0:T(8,128)S(1)}, f32[256,128]{1,0:T(8,128)S(1)}, u32[]{:S(2)}, u32[]{:S(2)}) collective-permute-start(f32[256,128]{1,0:T(8,128)S(1)} %broadcast_multiply_fusion.1), channel_id=1, source_target_pairs={{0,4},{4,8},{8,12},{1,5},{5,9},{9,13},{2,6},{6,10},{10,14},{3,7},{... | collective-permute-start | bytes 393224 | tf_op jit(solution)/shard_map/ppermute | solution.py:16
  86.4 7.4 %collective-permute-start.4 = (f32[256,128]{1,0:T(8,128)S(1)}, f32[256,128]{1,0:T(8,128)S(1)}, u32[]{:S(2)}, u32[]{:S(2)}) collective-permute-start(f32[256,128]{1,0:T(8,128)S(1)} %multiply_subtract_fusion.1), channel_id=1, source_target_pairs={{4,0},{8,4},{12,8},{5,1},{9,5},{13,9},{6,2},{10,6},{14,10},{7,3},{... | collective-permute-start | bytes 393224 | tf_op jit(solution)/shard_map/ppermute | solution.py:16
  95.8 0.7 copy-start.2
  96.5 99.3 %reduce-scatter.8.cloned.1.call-start = ((), (), s32[]{:S(2)}) async-start(), calls=%async_computation.5 | async-start | bytes 327680 | tf_op jit(solution)/shard_map/reduce_scatter | solution.py:99
  115.8 35.5 %copy-start.7 = (f32[128,128]{1,0:T(8,128)S(1)}, f32[128,128]{1,0:T(8,128)}, u32[]{:S(2)}) copy-start(f32[128,128]{1,0:T(8,128)} %reduce-scatter.6.cloned.1.call-done) | copy-start | bytes 196612
  161.1 4.8 %collective-permute-start.5 = (f32[256,128]{1,0:T(8,128)S(1)}, f32[256,128]{1,0:T(8,128)S(1)}, u32[]{:S(2)}, u32[]{:S(2)}) collective-permute-start(f32[256,128]{1,0:T(8,128)S(1)} %broadcast_multiply_fusion), channel_id=1, source_target_pairs={{0,4},{4,8},{8,12},{1,5},{5,9},{9,13},{2,6},{6,10},{10,14},{3,7},{... | collective-permute-start | bytes 393224 | tf_op jit(solution)/shard_map/ppermute | solution.py:16
  166.6 7.8 %collective-permute-start.6 = (f32[256,128]{1,0:T(8,128)S(1)}, f32[256,128]{1,0:T(8,128)S(1)}, u32[]{:S(2)}, u32[]{:S(2)}) collective-permute-start(f32[256,128]{1,0:T(8,128)S(1)} %multiply_subtract_fusion), channel_id=1, source_target_pairs={{4,0},{8,4},{12,8},{5,1},{9,5},{13,9},{6,2},{10,6},{14,10},{7,3},{... | collective-permute-start | bytes 393224 | tf_op jit(solution)/shard_map/ppermute | solution.py:16
  176.5 0.7 copy-start.1
  195.8 38.9 %copy-start.9 = (f32[128,128]{1,0:T(8,128)S(1)}, f32[128,128]{1,0:T(8,128)}, u32[]{:S(2)}) copy-start(f32[128,128]{1,0:T(8,128)} %reduce-scatter.8.cloned.1.call-done) | copy-start | bytes 196612
Sparse Core Ops, SparseCore 0:
  48.7 19.2 reduce-scatter.3
  96.6 19.1 reduce-scatter.5
  177.3 18.4 reduce-scatter.7
where the time goes:
time: 243 us; the launch traced here: 242 us
  blocking collectives  82.9 us (34%)
  waiting for transfers between devices  68.3 us (28%)
  between operations  20.9 us (9%)
  other arithmetic  20.5 us (8%)
  starting transfers between devices  17.7 us (7%)
  matrix products  16.7 us (7%)
  local copies, waits for them, and re-layouts  14.9 us (6%)
    psum x2, blocking collectives, fold_sum(): folded = lax.psum((values[0], values[1]), ('seg', 'bin'))  65.4 us
    reduce_scatter x3, waiting for transfers between devices, reduce_rows(): lax.psum_scatter(partial_value, 'bin', scatter_dimension=0, tiled=True)  57.3 us
    ppermute x7, starting transfers between devices, from_behind(): return lax.ppermute(x, axis, pairs)  17.6 us
    scatter-add x6, other arithmetic, apply_local(): return summed.at[rows_low].add(own_term).at[rows_up].add(returned)  12.3 us
    all_gather x2, blocking collectives, spread(): whole_rows = lax.all_gather(vector, 'bin', axis=0, tiled=True)  11.6 us
    ppermute x7, waiting for transfers between devices, from_behind(): return lax.ppermute(x, axis, pairs)  11 us
    all_gather x1, blocking collectives, shards(): start_whole = lax.all_gather(start_factors, 'bin', axis=0, tiled=True)  5.97 us
  transfers between devices with their start and end apart: 10, of which 6 were waited for; matrix products, arithmetic and copies ran while one was open for 11% of the time, Pallas kernels for 0%

commit v1 on v0

v1 whole, which is shorter than its diff:
```python
import jax
import jax.numpy as jnp
from jax import lax
from jax.sharding import PartitionSpec as P

ITERS = 2
PAD = 8

highest = lax.Precision.HIGHEST
ridge_weight = 0.5


def is_power_of_two(n):
    return n & (n - 1) == 0


def swap(x, axis, mask):
    n = lax.axis_size(axis)
    return lax.ppermute(x, axis, [(i, i ^ mask) for i in range(n)])


def bit_of(axis, mask):
    return (lax.axis_index(axis) & mask) != 0


def ordered(bit, mine, other, dim):
    first = jnp.where(bit, other, mine)
    second = jnp.where(bit, mine, other)
    return jnp.stack([first, second], dim)


def gather_rows(own):
    n = lax.axis_size("bin")
    if not is_power_of_two(n):
        return lax.all_gather(own, "bin", axis=0, tiled=True)
    held = own[None]
    mask = n // 2
    while mask:
        held = ordered(bit_of("bin", mask), held, swap(held, "bin", mask), 1)
        held = held.reshape((-1,) + own.shape)
        mask //= 2
    return held.reshape(-1, own.shape[-1])


def reduce_all(partial_rows):
    n = lax.axis_size("bin")
    if n == 1:
        return partial_rows
    if not is_power_of_two(n):
        return lax.psum(partial_rows, "bin")
    half = partial_rows.shape[0] // 2
    odd = bit_of("bin", 1)
    low, high = partial_rows[:half], partial_rows[half:]
    kept = jnp.where(odd, high, low) + swap(jnp.where(odd, low, high), "bin", 1)
    mask = 2
    while mask < n:
        kept = kept + swap(kept, "bin", mask)
        mask *= 2
    return ordered(odd, kept, swap(kept, "bin", 1), 0).reshape(partial_rows.shape)


def reduce_own(partial_rows, sums):
    n = lax.axis_size("bin")
    width = partial_rows.shape[1]
    if not is_power_of_two(n):
        own = lax.psum_scatter(partial_rows, "bin", scatter_dimension=0, tiled=True)
        return own, lax.psum(sums, "bin")
    blocks = partial_rows.reshape(n, -1, width)
    mask = 1
    while mask < n:
        split = blocks.reshape(-1, 2, blocks.shape[1], width)
        bit = bit_of("bin", mask)
        sent = jnp.where(bit, split[:, 0], split[:, 1])
        kept = jnp.where(bit, split[:, 1], split[:, 0])
        count = sent.shape[0] * sent.shape[1]
        message = jnp.concatenate([sent.reshape(count, width), sums], 0)
        got = swap(message, "bin", mask)
        blocks = kept + got[:count].reshape(kept.shape)
        sums = sums + got[count:]
        mask *= 2
    return blocks.reshape(-1, width), sums


def reduce_seg(sums):
    n = lax.axis_size("seg")
    if not is_power_of_two(n):
        return lax.psum(sums, "seg")
    mask = 1
    while mask < n:
        if mask * 2 < n:
            sums = sums + swap(sums, "seg", mask) + swap(sums, "seg", 2 * mask) + swap(sums, "seg", 3 * mask)
            mask *= 4
        else:
            sums = sums + swap(sums, "seg", mask)
            mask *= 2
    return sums


def pack(values, width):
    rows = [jnp.full((1, width), value, jnp.float32) for value in values]
    rows.append(jnp.zeros((PAD - len(values), width), jnp.float32))
    return jnp.concatenate(rows, 0)


def exchange_faces(low, up):
    n = lax.axis_size("seg")
    odd = bit_of("seg", 1)
    pairs_even = [(i, i + 1) for i in range(0, n - 1, 2)]
    pairs_odd = [(i, i + 1) for i in range(1, n - 1, 2)]
    both = lambda pairs: pairs + [(b, a) for a, b in pairs]
    first = lax.ppermute(jnp.where(odd, low, up), "seg", both(pairs_even))
    second = lax.ppermute(jnp.where(odd, up, low), "seg", both(pairs_odd))
    return jnp.where(odd, first, second), jnp.where(odd, second, first)


def shards(
    start_factors,
    bin_factors,
    tile_speed,
    tile_weight,
    tile_cells,
    tile_count,
    inner_pairs,
    inner_weight,
    face_rows,
    face_count,
    face_weight,
):
    speeds = tile_speed[0, 0]
    weights = tile_weight[0, 0]
    cells = tile_cells[0, 0]
    n_tiles = speeds.shape[0]
    tile_size = speeds.shape[1]
    own_rows = start_factors.shape[0]
    width = start_factors.shape[1]
    n_bin = lax.axis_size("bin")
    n_seg = lax.axis_size("seg")
    part_rows = own_rows * n_bin
    part_blocks = part_rows // tile_size

    start_whole = gather_rows(start_factors)

    rows_low = face_rows[0, 0, 0]
    rows_up = face_rows[0, 0, 1]
    faces = rows_low.shape[0]
    face_slots = jnp.arange(faces, dtype=jnp.int32)
    mask_low = (face_slots < face_count[0, 0, 0]).astype(jnp.float32)
    mask_up = (face_slots < face_count[0, 0, 1]).astype(jnp.float32)
    count_up = face_count[0, 0, 1].astype(jnp.float32)
    block_low = face_weight[0, 0] * mask_low[:, None]
    block_next = lax.ppermute(block_low, "seg", [(i, i - 1) for i in range(1, n_seg)])

    block_ids = jnp.arange(part_blocks, dtype=jnp.int32)
    live_tiles = (jnp.arange(n_tiles, dtype=jnp.int32) < tile_count[0, 0]).astype(jnp.float32)
    tile_bins = bin_factors.reshape(-1, tile_size, width)[cells[:, 1]]
    bins_wide = tile_bins.astype(jnp.float32)
    tile_gain = weights.astype(jnp.float32) * live_tiles[:, None, None]
    tile_onehot = (cells[:, 0][:, None] == block_ids[None, :]).astype(jnp.float32)
    weighted = (weights.astype(jnp.float32) * speeds.astype(jnp.float32)).astype(jnp.bfloat16)
    rhs_terms = jnp.einsum("kij,kjr->kir", weighted, tile_bins, preferred_element_type=jnp.float32)
    rhs_terms = rhs_terms * live_tiles[:, None, None]
    rhs_part = jnp.einsum("kb,kir->bir", tile_onehot, rhs_terms, precision=highest).reshape(
        part_rows, width
    )
    pairs = inner_pairs[0, 0]
    pair_weight = inner_weight[0, 0]
    left_onehot = (pairs[:, 0][:, None] == block_ids[None, :]).astype(jnp.float32)
    right_onehot = (pairs[:, 1][:, None] == block_ids[None, :]).astype(jnp.float32)
    left_degree = pair_weight.sum(2)
    right_degree = pair_weight.sum(1)

    coupling = []

    def apply_local(whole_rows, extra):
        own_low = whole_rows[rows_low] * mask_low[:, None]
        own_up = whole_rows[rows_up] * mask_up[:, None]
        low_message = jnp.concatenate([own_low, extra], 0)
        up_message = jnp.concatenate([own_up, extra], 0)
        up_previous, low_next = exchange_faces(low_message, up_message)

        blocks = whole_rows.reshape(part_blocks, tile_size, width)
        picked = blocks[cells[:, 0]]
        scores = jnp.einsum("kir,kjr->kij", picked, bins_wide, precision=highest) * tile_gain
        pulled = jnp.einsum("kij,kjr->kir", scores, bins_wide, precision=highest)
        left = blocks[pairs[:, 0]]
        right = blocks[pairs[:, 1]]
        to_left = left_degree[..., None] * left - jnp.einsum(
            "kij,kjr->kir", pair_weight, right, precision=highest
        )
        to_right = right_degree[..., None] * right - jnp.einsum(
            "kij,kir->kjr", pair_weight, left, precision=highest
        )
        summed = jnp.einsum("kb,kir->bir", tile_onehot, pulled, precision=highest)
        summed = summed + jnp.einsum("kb,kir->bir", left_onehot, to_left, precision=highest)
        summed = summed + jnp.einsum("kb,kir->bir", right_onehot, to_right, precision=highest)
        summed = summed.reshape(part_rows, width)

        if not coupling:
            live_previous = (face_slots.astype(jnp.float32) < up_previous[faces, 0]).astype(jnp.float32)
            coupling.append(block_low * live_previous[None, :])
            coupling.append(block_next * mask_up[None, :])
        down, up = coupling
        low_term = down.sum(1)[:, None] * own_low - jnp.dot(
            down, up_previous[:faces], precision=highest
        )
        up_term = up.sum(0)[:, None] * own_up - jnp.dot(
            up.T, low_next[:faces], precision=highest
        )
        return summed.at[rows_low].add(low_term).at[rows_up].add(up_term)

    counts = pack([count_up], width)
    partial_zero = rhs_part - apply_local(start_whole, counts)
    first = reduce_all(partial_zero) - ridge_weight * start_whole
    second = reduce_all(apply_local(first, counts)) + ridge_weight * first
    early = reduce_seg(pack([jnp.sum(first * first), jnp.sum(first * second)], width))
    norm_zero, product_zero = early[0, 0], early[1, 0]
    step_zero = norm_zero / product_zero
    partial_two = apply_local(second, counts)
    residual_whole = first - step_zero * second
    late_part = pack([jnp.sum(residual_whole * partial_two)], width)
    third, late = reduce_own(partial_two, late_part)
    with_second = jnp.sum(residual_whole * second)
    product_part = with_second - step_zero * (late[0, 0] + ridge_weight * with_second)
    final = reduce_seg(pack([jnp.sum(residual_whole * residual_whole), product_part], width))
    norm_one, product_one = final[0, 0], final[1, 0]
    beta = norm_one / norm_zero
    step_one = norm_one / (product_one - beta * norm_one / step_zero)

    offset = lax.axis_index("bin") * own_rows
    own = lambda whole: lax.dynamic_slice(whole, (offset, 0), (own_rows, width))
    first, second = own(first), own(second)
    third = third + ridge_weight * second
    residual = first - step_zero * second
    image = second - step_zero * third
    direction = residual + beta * first
    along = image + beta * second
    solution_factors = start_factors + step_zero * first + step_one * direction
    residual = residual - step_one * along
    return solution_factors, residual


def solution(mesh):
    return jax.shard_map(
        shards,
        mesh=mesh,
        in_specs=(
            P(("groups", "seg", "bin"), None),
            P(("groups", "bin"), None),
            P(("groups", "seg"), "bin", None, None, None),
            P(("groups", "seg"), "bin", None, None, None),
            P(("groups", "seg"), "bin", None, None),
            P(("groups", "seg"), "bin"),
            P(("groups", "seg"), "bin", None, None),
            P(("groups", "seg"), "bin", None, None, None),
            P(("groups", "seg"), "bin", None, None),
            P(("groups", "seg"), "bin", None),
            P(("groups", "seg"), "bin", None, None),
        ),
        out_specs=(P(("groups", "seg", "bin"), None), P(("groups", "seg", "bin"), None)),
        check_vma=False,
    )
```

time: 243 us -> 143 us (0.59)
  blocking collectives: 82.9 us -> 0 us
  waiting for transfers between devices: 68.3 us -> 30.1 us
  local copies, waits for them, and re-layouts: 14.9 us -> 28.1 us
  between operations: 20.9 us -> 10.6 us
  other arithmetic: 20.5 us -> 27.8 us
  starting transfers between devices: 17.7 us -> 24.3 us
  matrix products: 16.7 us -> 20.6 us
    psum x2 -> x0, blocking collectives: 65.4 us -> none  [fold_sum(): folded = lax.psum((values[0], values[1]), ('seg', 'bin'))]
    reduce_scatter x3 -> x0, waiting for transfers between devices: 57.3 us -> none  [reduce_rows(): lax.psum_scatter(partial_value, 'bin', scatter_dimension=0, tiled=True)]
    ppermute x7 -> x23, waiting for transfers between devices: 11 us -> 30.1 us  [the longest x16 22.4 us: swap(): return lax.ppermute(x, axis, [(i, i ^ mask) for i in range(n)])]
    all_gather x3 -> x0, blocking collectives: 17.5 us -> none  [the longest x2 11.6 us: spread(): whole_rows = lax.all_gather(vector, 'bin', axis=0, tiled=True)]
    ppermute x7 -> x23, starting transfers between devices: 17.6 us -> 24.3 us  [the longest x16 15.3 us: swap(): return lax.ppermute(x, axis, [(i, i ^ mask) for i in range(n)])]
    unnamed x26 -> x116, local copies, waits for them, and re-layouts: 3.33 us -> 9.77 us
    dot_general x6, matrix products: 3.31 us -> 6.68 us  [the longest x3 4.63 us: apply_local(): jnp.dot(up.T, low_next[:faces], precision=highest)]
    select_n x1 -> x11, other arithmetic: 0.01 us -> 2.92 us  [the longest x2 0.99 us: exchange_faces(): first = lax.ppermute(jnp.where(odd, low, up), 'seg', both(pairs_even))]
  transfers between devices with their start and end apart: 10 -> 23, of which waited for: 6 -> 11; matrix products, arithmetic and copies ran while one was open for 11% -> 21% of each run, Pallas kernels for 0% -> 0%
where the time goes in v1:
time: 143 us; the launch traced here: 142 us
  waiting for transfers between devices  30.1 us (21%)
  local copies, waits for them, and re-layouts  28.1 us (20%)
  other arithmetic  27.8 us (19%)
  starting transfers between devices  24.3 us (17%)
  matrix products  20.6 us (14%)
  between operations  10.6 us (7%)
    ppermute x16, waiting for transfers between devices, swap(): return lax.ppermute(x, axis, [(i, i ^ mask) for i in range(n)])  22.4 us
    ppermute x16, starting transfers between devices, swap(): return lax.ppermute(x, axis, [(i, i ^ mask) for i in range(n)])  15.3 us
    scatter-add x6, other arithmetic, apply_local(): return summed.at[rows_low].add(low_term).at[rows_up].add(up_term)  13.2 us
    unnamed x116, local copies, waits for them, and re-layouts  9.77 us
    ppermute x1, waiting for transfers between devices, shards(): lax.ppermute(block_low, 'seg', [(i, i - 1) for i in range(1, n_seg)])  7.72 us
    dot_general x3, matrix products, apply_local(): jnp.dot(up.T, low_next[:faces], precision=highest)  4.63 us
    ppermute x3, starting transfers between devices, exchange_faces(): first = lax.ppermute(jnp.where(odd, low, up), 'seg', both(pairs_even))  4.49 us
    gather x3, local copies, waits for them, and re-layouts, apply_local(): picked = blocks[cells[:, 0]]  3.96 us
  transfers between devices with their start and end apart: 23, of which 11 were waited for; matrix products, arithmetic and copies ran while one was open for 21% of the time, Pallas kernels for 0%

profile of v1, /device:TPU:0, one launch (start us, length us, event | category | flops | bytes accessed | tf_op | source)
XLA Modules:
  0.0 141.6 jit_solution(1020759965107714658)
XLA Ops:
  0.6 3.0 %collective-permute-start = (f32[1,128,128]{2,1,0:T(8,128)}, f32[1,128,128]{2,1,0:T(8,128)S(1)}, u32[]{:S(2)}, u32[]{:S(2)}) collective-permute-start(f32[1,128,128]{2,1,0:T(8,128)} %bitcast.214), channel_id=1, source_target_pairs={{0,2},{1,3},{2,0},{3,1},{4,6},{5,7},{6,4},{7,5},{8,10},{9,11},{10,... | collective-permute-start | bytes 196616 | tf_op jit(solution)/shard_map/ppermute | solution.py:19
  18.2 1.6 %collective-permute-start.2 = (f32[264,128]{1,0:T(8,128)}, f32[264,128]{1,0:T(8,128)}, u32[]{:S(2)}, u32[]{:S(2)}) collective-permute-start(f32[264,128]{1,0:T(8,128)} %get-tuple-element.22), channel_id=1, source_target_pairs={{0,4},{8,12},{4,0},{12,8},{1,5},{9,13},{5,1},{13,9},{2,6},{10,14},... | collective-permute-start | bytes 405512 | tf_op jit(solution)/shard_map/ppermute | solution.py:111
  32.7 2.0 %scatter_fusion = f32[512,128]{1,0:T(8,128)S(1)} fusion(f32[512,128]{1,0:T(8,128)S(1)} %bitcast.199, s32[256]{0:T(256)S(1)} %bitcast.216, f32[256,128]{1,0:T(8,128)S(1)} %convolution_subtract_fusion.2), kind=kCustom, calls=%fused_computation.16 | custom fusion | flops 32768 | bytes 394240 | tf_op jit(solution)/shard_map/scatter-add | solution.py:209
  34.7 7.7 %collective-permute-done.4 = f32[256,256]{1,0:T(8,128)S(1)} collective-permute-done((f32[256,256]{1,0:T(8,128)S(1)}, f32[256,256]{1,0:T(8,128)S(1)}, u32[]{:S(2)}, u32[]{:S(2)}) %collective-permute-start.4) | collective-permute-done | bytes 262176 | tf_op jit(solution)/shard_map/ppermute | solution.py:151
  42.5 1.6 %fusion.19 = f32[256,128]{1,0:T(8,128)S(1)} fusion(f32[256,256]{1,0:T(8,128)S(1)} %collective-permute-done.4, f32[264,128]{1,0:T(8,128)} %collective-permute-done.2, f32[264,128]{1,0:T(8,128)} %collective-permute-done.3, f32[256]{0:T(256)S(1)} %compare_convert_fusion.1, pred[]{:T(512)S(6)} %ne.8), kind=kOutput, calls=%fused_computation.78 | convolution fusion | flops 100761600 | bytes 656385 | tf_op jit(solution)/shard_map/dot_general | solution.py:206
  44.1 2.5 %scatter_custom_fusion.1 = f32[512,128]{1,0:T(8,128)S(1)} fusion(f32[512,128]{1,0:T(8,128)S(1)} %scatter_fusion, s32[256]{0:T(256)} %bitcast.221, f32[256,128]{1,0:T(8,128)S(1)} %fusion.19, f32[256,128]{1,0:T(8,128)S(1)} %get-tuple-element.46, f32[256]{0:T(256)S(1)} %multiply_reduce_fusion.5), kind=kCustom, calls=%fused_computation.126 | custom fusion | flops 98304 | bytes 525312 | tf_op jit(solution)/shard_map/scatter-add | solution.py:209
  48.7 5.0 %collective-permute-done.6 = f32[256,128]{1,0:T(8,128)S(1)} collective-permute-done((f32[256,128]{1,0:T(8,128)S(1)}, f32[256,128]{1,0:T(8,128)S(1)}, u32[]{:S(2)}, u32[]{:S(2)}) %collective-permute-start.6) | collective-permute-done | bytes 131104 | tf_op jit(solution)/shard_map/ppermute | solution.py:19
  56.1 1.5 %gather_fusion.9 = f32[256,128]{1,0:T(8,128)} fusion(f32[512,128]{1,0:T(8,128)S(1)} %bitcast_subtract_fusion, s32[1024]{0:T(1024)} %copy-done.35), kind=kCustom, calls=%fused_computation.9 | custom fusion | bytes 263168 | tf_op jit(solution)/shard_map/gather | solution.py:175
  59.0 1.6 %gather_fusion.6 = f32[12,128,128]{2,1,0:T(8,128)} fusion(f32[4,128,128]{2,1,0:T(8,128)S(1)} %multiply_subtract_fusion.1, s32[1024]{0:T(1024)} %get-tuple-element.44), kind=kCustom, calls=%fused_computation.6 | custom fusion | bytes 1572912 | tf_op jit(solution)/shard_map/gather | solution.py:182
  62.4 1.8 %collective-permute-start.8 = (f32[264,128]{1,0:T(8,128)S(1)}, f32[264,128]{1,0:T(8,128)S(1)}, u32[]{:S(2)}, u32[]{:S(2)}) collective-permute-start(f32[264,128]{1,0:T(8,128)S(1)} %get-tuple-element.19), channel_id=1, source_target_pairs={{0,4},{8,12},{4,0},{12,8},{1,5},{9,13},{5,1},{13,9},{2,6},{10,14},... | collective-permute-start | bytes 405512 | tf_op jit(solution)/shard_map/ppermute | solution.py:111
  69.9 2.0 %scatter_fusion.1 = f32[512,128]{1,0:T(8,128)S(1)} fusion(f32[512,128]{1,0:T(8,128)S(1)} %bitcast.198, s32[256]{0:T(256)S(1)} %bitcast.217, f32[256,128]{1,0:T(8,128)S(1)} %convolution_subtract_fusion.1), kind=kCustom, calls=%fused_computation.18 | custom fusion | flops 32768 | bytes 394240 | tf_op jit(solution)/shard_map/scatter-add | solution.py:209
  72.0 1.6 %fusion.17 = f32[256,128]{1,0:T(8,128)S(1)} fusion(f32[256,256]{1,0:T(8,128)S(1)} %collective-permute-done.4, f32[256]{0:T(256)S(1)} %compare_convert_fusion.1, f32[264,128]{1,0:T(8,128)} %copy-done.8, f32[264,128]{1,0:T(8,128)} %copy-done.7, pred[]{:T(512)S(6)} %ne.8), kind=kOutput, calls=%fused_computation.76 | convolution fusion | flops 100761600 | bytes 656385 | tf_op jit(solution)/shard_map/dot_general | solution.py:206
  73.5 2.3 %scatter_custom_fusion.3 = f32[512,128]{1,0:T(8,128)S(1)} fusion(f32[512,128]{1,0:T(8,128)S(1)} %scatter_fusion.1, s32[256]{0:T(256)} %bitcast.222, f32[256,128]{1,0:T(8,128)S(1)} %fusion.17, f32[256]{0:T(256)S(1)} %copy-done.29, f32[256,128]{1,0:T(8,128)S(1)} %gather_fusion.10, f32[256]{0:T(256)S(1)} %compare_convert_fusion.1), kind=kCustom, calls=%fused_computation.120 | custom fusion | flops 131072 | bytes 526336 | tf_op jit(solution)/shard_map/scatter-add | solution.py:209
  77.9 5.0 %collective-permute-done.11 = f32[256,128]{1,0:T(8,128)S(1)} collective-permute-done((f32[256,128]{1,0:T(8,128)S(1)}, f32[256,128]{1,0:T(8,128)S(1)}, u32[]{:S(2)}, u32[]{:S(2)}) %collective-permute-start.11) | collective-permute-done | bytes 131104 | tf_op jit(solution)/shard_map/ppermute | solution.py:19
  87.8 2.5 %collective-permute-start.13 = (f32[8,128]{1,0:T(8,128)}, f32[8,128]{1,0:T(8,128)}, u32[]{:S(2)}, u32[]{:S(2)}) collective-permute-start(f32[8,128]{1,0:T(8,128)} %broadcast.192), channel_id=1, source_target_pairs={{0,4},{4,0},{8,12},{12,8},{1,5},{5,1},{9,13},{13,9},{2,6},{6,2},{1... | collective-permute-start | bytes 12296 | tf_op jit(solution)/shard_map/ppermute | solution.py:19
  90.8 1.9 %collective-permute-start.15 = (f32[8,128]{1,0:T(8,128)}, f32[8,128]{1,0:T(8,128)}, u32[]{:S(2)}, u32[]{:S(2)}) collective-permute-start(f32[8,128]{1,0:T(8,128)} %broadcast.192), channel_id=1, source_target_pairs={{0,12},{4,8},{8,4},{12,0},{1,13},{5,9},{9,5},{13,1},{2,14},{6,10},... | collective-permute-start | bytes 12296 | tf_op jit(solution)/shard_map/ppermute | solution.py:19
  95.9 1.6 %gather_fusion.11 = f32[12,128,128]{2,1,0:T(8,128)} fusion(f32[4,128,128]{2,1,0:T(8,128)S(1)} %multiply_add_fusion, s32[1024]{0:T(1024)} %get-tuple-element.44), kind=kCustom, calls=%fused_computation.11 | custom fusion | bytes 1572912 | tf_op jit(solution)/shard_map/gather | solution.py:182
  111.3 2.0 %scatter_fusion.2 = f32[512,128]{1,0:T(8,128)S(1)} fusion(f32[512,128]{1,0:T(8,128)S(1)} %bitcast.195, s32[256]{0:T(256)S(1)} %bitcast.218, f32[256,128]{1,0:T(8,128)S(1)} %convolution_subtract_fusion), kind=kCustom, calls=%fused_computation.20 | custom fusion | flops 32768 | bytes 394240 | tf_op jit(solution)/shard_map/scatter-add | solution.py:209
  113.3 1.5 %fusion.15 = f32[256,128]{1,0:T(8,128)S(1)} fusion(f32[256,256]{1,0:T(8,128)S(1)} %collective-permute-done.4, f32[256]{0:T(256)S(1)} %compare_convert_fusion.1, f32[264,128]{1,0:T(8,128)} %collective-permute-done.17, f32[264,128]{1,0:T(8,128)S(1)} %collective-permute-done.16, pred[]{:T(512)S(6)} %ne.8), kind=kOutput, calls=%fused_computation.74 | convolution fusion | flops 100761600 | bytes 656385 | tf_op jit(solution)/shard_map/dot_general | solution.py:206
  114.8 2.3 %scatter_custom_fusion.5 = f32[512,128]{1,0:T(8,128)S(1)} fusion(f32[512,128]{1,0:T(8,128)S(1)} %scatter_fusion.2, s32[256]{0:T(256)} %bitcast.223, f32[256,128]{1,0:T(8,128)S(1)} %fusion.15, f32[256]{0:T(256)S(1)} %copy-done.30, f32[256,128]{1,0:T(8,128)S(1)} %gather_fusion.15, f32[256]{0:T(256)S(1)} %compare_convert_fusion.1), kind=kCustom, calls=%fused_computation.114 | custom fusion | flops 131072 | bytes 526336 | tf_op jit(solution)/shard_map/scatter-add | solution.py:209
  122.5 2.2 %collective-permute-done.19 = f32[136,128]{1,0:T(8,128)S(1)} collective-permute-done((f32[136,128]{1,0:T(8,128)S(1)}, f32[136,128]{1,0:T(8,128)S(1)}, u32[]{:S(2)}, u32[]{:S(2)}) %collective-permute-start.19) | collective-permute-done | bytes 69664 | tf_op jit(solution)/shard_map/ppermute | solution.py:19
  127.2 2.8 %collective-permute-start.20 = (f32[8,128]{1,0:T(8,128)S(1)}, f32[8,128]{1,0:T(8,128)S(1)}, u32[]{:S(2)}, u32[]{:S(2)}) collective-permute-start(f32[8,128]{1,0:T(8,128)S(1)} %broadcast.194), channel_id=1, source_target_pairs={{0,4},{4,0},{8,12},{12,8},{1,5},{5,1},{9,13},{13,9},{2,6},{6,2},{1... | collective-permute-start | bytes 12296 | tf_op jit(solution)/shard_map/ppermute | solution.py:19
  130.5 1.9 %collective-permute-start.22 = (f32[8,128]{1,0:T(8,128)S(1)}, f32[8,128]{1,0:T(8,128)S(1)}, u32[]{:S(2)}, u32[]{:S(2)}) collective-permute-start(f32[8,128]{1,0:T(8,128)S(1)} %broadcast.194), channel_id=1, source_target_pairs={{0,12},{4,8},{8,4},{12,0},{1,13},{5,9},{9,5},{13,1},{2,14},{6,10},... | collective-permute-start | bytes 12296 | tf_op jit(solution)/shard_map/ppermute | solution.py:19
  132.4 2.1 %collective-permute-done.21 = f32[8,128]{1,0:T(8,128)S(1)} collective-permute-done((f32[8,128]{1,0:T(8,128)S(1)}, f32[8,128]{1,0:T(8,128)S(1)}, u32[]{:S(2)}, u32[]{:S(2)}) %collective-permute-start.21) | collective-permute-done | bytes 4128 | tf_op jit(solution)/shard_map/ppermute | solution.py:19
  (263 shorter events, 70.9 us)
Async XLA Ops:
  0.6 12.0 %collective-permute-start = (f32[1,128,128]{2,1,0:T(8,128)}, f32[1,128,128]{2,1,0:T(8,128)S(1)}, u32[]{:S(2)}, u32[]{:S(2)}) collective-permute-start(f32[1,128,128]{2,1,0:T(8,128)} %bitcast.214), channel_id=1, source_target_pairs={{0,2},{1,3},{2,0},{3,1},{4,6},{5,7},{6,4},{7,5},{8,10},{9,11},{10,... | collective-permute-start | bytes 196616 | tf_op jit(solution)/shard_map/ppermute | solution.py:19
  12.7 3.0 %collective-permute-start.1 = (f32[2,128,128]{2,1,0:T(8,128)S(1)}, f32[2,128,128]{2,1,0:T(8,128)S(1)}, u32[]{:S(2)}, u32[]{:S(2)}) collective-permute-start(f32[2,128,128]{2,1,0:T(8,128)S(1)} %maximum_bitcast_fusion), channel_id=1, source_target_pairs={{0,1},{1,0},{2,3},{3,2},{4,5},{5,4},{6,7},{7,6},{8,9},{9,8},{10,11... | collective-permute-start | bytes 393224 | tf_op jit(solution)/shard_map/ppermute | solution.py:19
  18.2 9.8 %collective-permute-start.2 = (f32[264,128]{1,0:T(8,128)}, f32[264,128]{1,0:T(8,128)}, u32[]{:S(2)}, u32[]{:S(2)}) collective-permute-start(f32[264,128]{1,0:T(8,128)} %get-tuple-element.22), channel_id=1, source_target_pairs={{0,4},{8,12},{4,0},{12,8},{1,5},{9,13},{5,1},{13,9},{2,6},{10,14},... | collective-permute-start | bytes 405512 | tf_op jit(solution)/shard_map/ppermute | solution.py:111
  19.8 8.2 %collective-permute-start.3 = (f32[264,128]{1,0:T(8,128)}, f32[264,128]{1,0:T(8,128)}, u32[]{:S(2)}, u32[]{:S(2)}) collective-permute-start(f32[264,128]{1,0:T(8,128)} %get-tuple-element.21), channel_id=1, source_target_pairs={{4,8},{8,4},{5,9},{9,5},{6,10},{10,6},{7,11},{11,7},{20,24},{24,20... | collective-permute-start | bytes 405512 | tf_op jit(solution)/shard_map/ppermute | solution.py:112
  30.4 12.0 %collective-permute-start.4 = (f32[256,256]{1,0:T(8,128)S(1)}, f32[256,256]{1,0:T(8,128)S(1)}, u32[]{:S(2)}, u32[]{:S(2)}) collective-permute-start(f32[256,256]{1,0:T(8,128)S(1)} %get-tuple-element.14), channel_id=1, source_target_pairs={{4,0},{8,4},{12,8},{5,1},{9,5},{13,9},{6,2},{10,6},{14,10},{7,3},{... | collective-permute-start | bytes 786440 | tf_op jit(solution)/shard_map/ppermute | solution.py:151
  46.6 1.4 collective-permute-start.5
  48.1 5.6 %collective-permute-start.6 = (f32[256,128]{1,0:T(8,128)S(1)}, f32[256,128]{1,0:T(8,128)S(1)}, u32[]{:S(2)}, u32[]{:S(2)}) collective-permute-start(f32[256,128]{1,0:T(8,128)S(1)} %select_add_fusion.1), channel_id=1, source_target_pairs={{0,2},{1,3},{2,0},{3,1},{4,6},{5,7},{6,4},{7,5},{8,10},{9,11},{10,... | collective-permute-start | bytes 393224 | tf_op jit(solution)/shard_map/ppermute | solution.py:19
  53.7 1.4 collective-permute-start.7
  62.4 6.2 %collective-permute-start.8 = (f32[264,128]{1,0:T(8,128)S(1)}, f32[264,128]{1,0:T(8,128)S(1)}, u32[]{:S(2)}, u32[]{:S(2)}) collective-permute-start(f32[264,128]{1,0:T(8,128)S(1)} %get-tuple-element.19), channel_id=1, source_target_pairs={{0,4},{8,12},{4,0},{12,8},{1,5},{9,13},{5,1},{13,9},{2,6},{10,14},... | collective-permute-start | bytes 405512 | tf_op jit(solution)/shard_map/ppermute | solution.py:111
  64.2 4.4 %collective-permute-start.9 = (f32[264,128]{1,0:T(8,128)S(1)}, f32[264,128]{1,0:T(8,128)S(1)}, u32[]{:S(2)}, u32[]{:S(2)}) collective-permute-start(f32[264,128]{1,0:T(8,128)S(1)} %get-tuple-element.20), channel_id=1, source_target_pairs={{4,8},{8,4},{5,9},{9,5},{6,10},{10,6},{7,11},{11,7},{20,24},{24,20... | collective-permute-start | bytes 405512 | tf_op jit(solution)/shard_map/ppermute | solution.py:112
  75.9 1.4 collective-permute-start.10
  77.3 5.6 %collective-permute-start.11 = (f32[256,128]{1,0:T(8,128)S(1)}, f32[256,128]{1,0:T(8,128)S(1)}, u32[]{:S(2)}, u32[]{:S(2)}) collective-permute-start(f32[256,128]{1,0:T(8,128)S(1)} %select_add_fusion), channel_id=1, source_target_pairs={{0,2},{1,3},{2,0},{3,1},{4,6},{5,7},{6,4},{7,5},{8,10},{9,11},{10,... | collective-permute-start | bytes 393224 | tf_op jit(solution)/shard_map/ppermute | solution.py:19
  83.0 1.4 collective-permute-start.12
  87.8 18.9 %collective-permute-start.13 = (f32[8,128]{1,0:T(8,128)}, f32[8,128]{1,0:T(8,128)}, u32[]{:S(2)}, u32[]{:S(2)}) collective-permute-start(f32[8,128]{1,0:T(8,128)} %broadcast.192), channel_id=1, source_target_pairs={{0,4},{4,0},{8,12},{12,8},{1,5},{5,1},{9,13},{13,9},{2,6},{6,2},{1... | collective-permute-start | bytes 12296 | tf_op jit(solution)/shard_map/ppermute | solution.py:19
  90.3 16.4 %collective-permute-start.14 = (f32[8,128]{1,0:T(8,128)}, f32[8,128]{1,0:T(8,128)}, u32[]{:S(2)}, u32[]{:S(2)}) collective-permute-start(f32[8,128]{1,0:T(8,128)} %broadcast.192), channel_id=1, source_target_pairs={{0,8},{4,12},{8,0},{12,4},{1,9},{5,13},{9,1},{13,5},{2,10},{6,14},... | collective-permute-start | bytes 12296 | tf_op jit(solution)/shard_map/ppermute | solution.py:19
  90.8 15.9 %collective-permute-start.15 = (f32[8,128]{1,0:T(8,128)}, f32[8,128]{1,0:T(8,128)}, u32[]{:S(2)}, u32[]{:S(2)}) collective-permute-start(f32[8,128]{1,0:T(8,128)} %broadcast.192), channel_id=1, source_target_pairs={{0,12},{4,8},{8,4},{12,0},{1,13},{5,9},{9,5},{13,1},{2,14},{6,10},... | collective-permute-start | bytes 12296 | tf_op jit(solution)/shard_map/ppermute | solution.py:19
  100.5 9.4 %collective-permute-start.16 = (f32[264,128]{1,0:T(8,128)}, f32[264,128]{1,0:T(8,128)S(1)}, u32[]{:S(2)}, u32[]{:S(2)}) collective-permute-start(f32[264,128]{1,0:T(8,128)} %get-tuple-element.17), channel_id=1, source_target_pairs={{0,4},{8,12},{4,0},{12,8},{1,5},{9,13},{5,1},{13,9},{2,6},{10,14},... | collective-permute-start | bytes 405512 | tf_op jit(solution)/shard_map/ppermute | solution.py:111
  101.6 8.3 %collective-permute-start.17 = (f32[264,128]{1,0:T(8,128)}, f32[264,128]{1,0:T(8,128)}, u32[]{:S(2)}, u32[]{:S(2)}) collective-permute-start(f32[264,128]{1,0:T(8,128)} %get-tuple-element.18), channel_id=1, source_target_pairs={{4,8},{8,4},{5,9},{9,5},{6,10},{10,6},{7,11},{11,7},{20,24},{24,20... | collective-permute-start | bytes 405512 | tf_op jit(solution)/shard_map/ppermute | solution.py:112
  118.7 1.4 %collective-permute-start.18 = (f32[264,128]{1,0:T(8,128)S(1)}, f32[264,128]{1,0:T(8,128)S(1)}, u32[]{:S(2)}, u32[]{:S(2)}) collective-permute-start(f32[264,128]{1,0:T(8,128)S(1)} %maximum_maximum_fusion.6), channel_id=1, source_target_pairs={{0,1},{1,0},{2,3},{3,2},{4,5},{5,4},{6,7},{7,6},{8,9},{9,8},{10,11... | collective-permute-start | bytes 405512 | tf_op jit(solution)/shard_map/ppermute | solution.py:19
  120.3 4.4 %collective-permute-start.19 = (f32[136,128]{1,0:T(8,128)S(1)}, f32[136,128]{1,0:T(8,128)S(1)}, u32[]{:S(2)}, u32[]{:S(2)}) collective-permute-start(f32[136,128]{1,0:T(8,128)S(1)} %pad_maximum_fusion.3), channel_id=1, source_target_pairs={{0,2},{1,3},{2,0},{3,1},{4,6},{5,7},{6,4},{7,5},{8,10},{9,11},{10,... | collective-permute-start | bytes 208904 | tf_op jit(solution)/shard_map/ppermute | solution.py:19
  121.9 19.0 %copy-start.12 = (f32[128,128]{1,0:T(8,128)S(1)}, f32[128,128]{1,0:T(8,128)}, u32[]{:S(2)}) copy-start(f32[128,128]{1,0:T(8,128)} %param.11) | copy-start | bytes 196612
  127.2 5.1 %collective-permute-start.20 = (f32[8,128]{1,0:T(8,128)S(1)}, f32[8,128]{1,0:T(8,128)S(1)}, u32[]{:S(2)}, u32[]{:S(2)}) collective-permute-start(f32[8,128]{1,0:T(8,128)S(1)} %broadcast.194), channel_id=1, source_target_pairs={{0,4},{4,0},{8,12},{12,8},{1,5},{5,1},{9,13},{13,9},{2,6},{6,2},{1... | collective-permute-start | bytes 12296 | tf_op jit(solution)/shard_map/ppermute | solution.py:19
  130.0 4.5 %collective-permute-start.21 = (f32[8,128]{1,0:T(8,128)S(1)}, f32[8,128]{1,0:T(8,128)S(1)}, u32[]{:S(2)}, u32[]{:S(2)}) collective-permute-start(f32[8,128]{1,0:T(8,128)S(1)} %broadcast.194), channel_id=1, source_target_pairs={{0,8},{4,12},{8,0},{12,4},{1,9},{5,13},{9,1},{13,5},{2,10},{6,14},... | collective-permute-start | bytes 12296 | tf_op jit(solution)/shard_map/ppermute | solution.py:19
  130.5 5.4 %collective-permute-start.22 = (f32[8,128]{1,0:T(8,128)S(1)}, f32[8,128]{1,0:T(8,128)S(1)}, u32[]{:S(2)}, u32[]{:S(2)}) collective-permute-start(f32[8,128]{1,0:T(8,128)S(1)} %broadcast.194), channel_id=1, source_target_pairs={{0,12},{4,8},{8,4},{12,0},{1,13},{5,9},{9,5},{13,1},{2,14},{6,10},... | collective-permute-start | bytes 12296 | tf_op jit(solution)/shard_map/ppermute | solution.py:19
  (57 other events, 136.3 us)

commit v2 on v1

v2 whole, which is shorter than its diff:
```python
import functools

import jax
import jax.numpy as jnp
from jax import lax
from jax.experimental import pallas as pl
from jax.experimental.pallas import tpu as pltpu
from jax.sharding import PartitionSpec as P

ITERS = 2
PAD = 8
VMEM_BYTES = 16 << 20

f32 = jnp.float32
bf16 = jnp.bfloat16
ridge_weight = 0.5


def is_power_of_two(n):
    return n & (n - 1) == 0


def swap(x, axis, mask):
    n = lax.axis_size(axis)
    return lax.ppermute(x, axis, [(i, i ^ mask) for i in range(n)])


def bit_of(axis, mask):
    return (lax.axis_index(axis) & mask) != 0


def ordered(bit, mine, other, dim):
    first = jnp.where(bit, other, mine)
    second = jnp.where(bit, mine, other)
    return jnp.stack([first, second], dim)


def gather_rows(own):
    n = lax.axis_size("bin")
    if not is_power_of_two(n):
        return lax.all_gather(own, "bin", axis=0, tiled=True)
    held = own[None]
    mask = n // 2
    while mask:
        held = ordered(bit_of("bin", mask), held, swap(held, "bin", mask), 1)
        held = held.reshape((-1,) + own.shape)
        mask //= 2
    return held.reshape(-1, own.shape[-1])


def reduce_all(partial_rows):
    n = lax.axis_size("bin")
    if n == 1:
        return partial_rows
    if not is_power_of_two(n):
        return lax.psum(partial_rows, "bin")
    half = partial_rows.shape[0] // 2
    odd = bit_of("bin", 1)
    low, high = partial_rows[:half], partial_rows[half:]
    kept = jnp.where(odd, high, low) + swap(jnp.where(odd, low, high), "bin", 1)
    mask = 2
    while mask < n:
        kept = kept + swap(kept, "bin", mask)
        mask *= 2
    return ordered(odd, kept, swap(kept, "bin", 1), 0).reshape(partial_rows.shape)


def reduce_own(partial_rows, sums):
    n = lax.axis_size("bin")
    width = partial_rows.shape[1]
    if not is_power_of_two(n):
        own = lax.psum_scatter(partial_rows, "bin", scatter_dimension=0, tiled=True)
        return own, lax.psum(sums, "bin")
    blocks = partial_rows.reshape(n, -1, width)
    mask = 1
    while mask < n:
        split = blocks.reshape(-1, 2, blocks.shape[1], width)
        bit = bit_of("bin", mask)
        sent = jnp.where(bit, split[:, 0], split[:, 1])
        kept = jnp.where(bit, split[:, 1], split[:, 0])
        count = sent.shape[0] * sent.shape[1]
        message = jnp.concatenate([sent.reshape(count, width), sums], 0)
        got = swap(message, "bin", mask)
        blocks = kept + got[:count].reshape(kept.shape)
        sums = sums + got[count:]
        mask *= 2
    return blocks.reshape(-1, width), sums


def reduce_seg(sums):
    n = lax.axis_size("seg")
    if not is_power_of_two(n):
        return lax.psum(sums, "seg")
    mask = 1
    while mask < n:
        if mask * 2 < n:
            sums = sums + swap(sums, "seg", mask) + swap(sums, "seg", 2 * mask) + swap(sums, "seg", 3 * mask)
            mask *= 4
        else:
            sums = sums + swap(sums, "seg", mask)
            mask *= 2
    return sums


def exchange_pairs(n, first):
    pairs = [(i, i + 1) for i in range(first, n - 1, 2)]
    return pairs + [(b, a) for a, b in pairs]


def exchange_faces(message_even, message_odd):
    n = lax.axis_size("seg")
    got_even = lax.ppermute(message_even, "seg", exchange_pairs(n, 0))
    got_odd = lax.ppermute(message_odd, "seg", exchange_pairs(n, 1))
    return got_even, got_odd


def split(x):
    high = x.astype(bf16)
    return high, (x - high.astype(f32)).astype(bf16)


def dot(a, b):
    return lax.dot_general(a, b, (((1,), (0,)), ((), ())), preferred_element_type=f32)


def along(x):
    high, low = split(x)
    return jnp.concatenate([high, high, low], 1)


def stacked(x):
    high, low = split(x)
    return jnp.concatenate([high, low, high], 0)


class Info:
    def __init__(self, n_tiles, n_inner):
        self.cells = 0
        self.count = 2 * n_tiles
        self.pairs = self.count + 1
        self.faces = self.pairs + 2 * n_inner
        self.odd = self.faces + 2
        self.index = self.odd + 1


def call(kernel, outs, *operands, scratch=(), flops=0):
    smem = pl.BlockSpec(memory_space=pltpu.SMEM)
    vmem = pl.BlockSpec(memory_space=pltpu.VMEM)
    nbytes = sum(o.size * o.dtype.itemsize for o in operands)
    return pl.pallas_call(
        kernel,
        out_shape=[jax.ShapeDtypeStruct(shape, kind) for shape, kind in outs],
        in_specs=[smem] + [vmem] * (len(operands) - 1),
        out_specs=[vmem] * len(outs),
        scratch_shapes=scratch,
        compiler_params=pltpu.CompilerParams(vmem_limit_bytes=VMEM_BYTES),
        cost_estimate=pl.CostEstimate(flops=flops, bytes_accessed=nbytes, transcendentals=0),
    )(*operands)


def prep_kernel(at, n_bin, info, weights, speeds, bins, inner, rows, face,
                rhs, gain, bins_t, bins_s, inner_cat, diag, pick_hot, scatter_hot, down_cat):
    n_tiles, tile, _ = weights.shape
    width = bins.shape[1]
    part_rows = rhs.shape[0]
    for k in range(bins.shape[0] // tile):
        block = bins[k * tile:(k + 1) * tile, :]
        flipped = block.astype(f32).T.astype(bf16)
        bins_t[k] = jnp.concatenate([flipped, flipped], 0)
        bins_s[k] = jnp.concatenate([block, block], 0)
    rhs[...] = jnp.zeros_like(rhs)
    for k in range(n_tiles):
        wide = weights[k].astype(f32)
        live = jnp.where(k < info[at.count], 1.0, 0.0).astype(f32)
        gain[k] = wide * live
        weighted = (wide * speeds[k].astype(f32)).astype(bf16)
        terms = dot(weighted, bins_s[info[at.cells + 2 * k + 1], 0:tile, :]) * live
        place = pl.ds(pl.multiple_of(info[at.cells + 2 * k] * tile, tile), tile)
        rhs[place, :] += terms
    diag[...] = jnp.full(diag.shape, ridge_weight / n_bin, f32)
    for j in range(inner.shape[0]):
        block = inner[j]
        flipped = block.T
        inner_cat[j, 0] = along(block)
        inner_cat[j, 1] = along(flipped)
        for side, matrix in enumerate((block, flipped)):
            place = pl.ds(pl.multiple_of(info[at.pairs + 2 * j + side] * tile, tile), tile)
            degree = jnp.sum(matrix, axis=1, keepdims=True)
            diag[place, :] += jnp.broadcast_to(degree, (tile, width))
    n_face = rows.shape[1]
    for side in range(2):
        live = info[at.faces + side]
        listed = rows[side:side + 1, :]
        slots = lax.broadcasted_iota(jnp.int32, (1, n_face), 1)
        listed = jnp.where(slots < live, listed, -1)
        ids = lax.broadcasted_iota(jnp.int32, (part_rows, n_face), 0)
        hot = (ids == listed).astype(f32)
        scatter_hot[:, side * n_face:(side + 1) * n_face] = hot.astype(bf16)
        pick_hot[side * n_face:(side + 1) * n_face, :] = hot.T.astype(bf16)
    high, low = split(face[...])
    hot = scatter_hot[:, 0:n_face]
    high = dot(hot, high).astype(bf16)
    low = dot(hot, low).astype(bf16)
    down_cat[...] = jnp.concatenate([high, high, low], 1)


def up_kernel(info, face_next, scatter_hot, up_cat):
    n_face = face_next.shape[0]
    high, low = split(face_next[...].T)
    hot = scatter_hot[:, n_face:2 * n_face]
    high = dot(hot, high).astype(bf16)
    low = dot(hot, low).astype(bf16)
    up_cat[...] = jnp.concatenate([high, high, low], 1)


def pick_kernel(at, count_row, info, whole, pick_hot, *refs):
    if count_row:
        whole_cat, even, odd = refs
        extra = jnp.full((PAD, whole.shape[1]), info[at.faces + 1], jnp.int32).astype(f32)
    else:
        before, whole_cat, even, odd, sums = refs
        extra = None
    high, low = split(whole[...])
    cat = jnp.concatenate([high, low], 1)
    whole_cat[...] = cat
    width = whole.shape[1]
    picked = dot(pick_hot[...], cat)
    picked = picked[:, :width] + picked[:, width:]
    n_face = picked.shape[0] // 2
    low_rows, up_rows = picked[:n_face], picked[n_face:]
    is_odd = info[at.odd] == 1
    even[0:n_face, :] = jnp.where(is_odd, low_rows, up_rows)
    odd[0:n_face, :] = jnp.where(is_odd, up_rows, low_rows)
    if count_row:
        even[n_face:, :] = extra
        odd[n_face:, :] = extra
    else:
        now, old = whole[...], before[...]
        sums[...] = jnp.zeros_like(sums)
        sums[0:1, :] = jnp.sum(old * old, axis=0, keepdims=True)
        sums[1:2, :] = jnp.sum(old * now, axis=0, keepdims=True)


def main_kernel(at, info, whole, whole_cat, bins_t, bins_s, gain, inner_cat, diag, out, terms):
    n_tiles, tile, _ = gain.shape
    width = whole.shape[1]
    for k in range(n_tiles):
        place = pl.ds(pl.multiple_of(info[at.cells + 2 * k] * tile, tile), tile)
        column = info[at.cells + 2 * k + 1]
        scores = dot(whole_cat[place, :], bins_t[column]) * gain[k]
        high, low = split(scores)
        terms[k] = dot(jnp.concatenate([high, low], 1), bins_s[column])
    n_inner = inner_cat.shape[0]
    for j in range(n_inner):
        for side in range(2):
            place = pl.ds(pl.multiple_of(info[at.pairs + 2 * j + 1 - side] * tile, tile), tile)
            other = whole_cat[place, :]
            high, low = other[:, :width], other[:, width:]
            terms[n_tiles + 2 * j + side] = -dot(inner_cat[j, side], jnp.concatenate([high, low, high], 0))
    out[...] = diag[...] * whole[...]
    for k in range(n_tiles):
        place = pl.ds(pl.multiple_of(info[at.cells + 2 * k] * tile, tile), tile)
        out[place, :] += terms[k]
    for j in range(n_inner):
        for side in range(2):
            place = pl.ds(pl.multiple_of(info[at.pairs + 2 * j + side] * tile, tile), tile)
            out[place, :] += terms[n_tiles + 2 * j + side]


def neighbours(at, info, even, odd, n_face):
    is_odd = info[at.odd] == 1
    first, second = even[0:n_face, :], odd[0:n_face, :]
    return jnp.where(is_odd, first, second), jnp.where(is_odd, second, first)


def first_face_kernel(at, info, even, odd, down_cat, up_cat, part, whole, diag, rhs, out, diag_all):
    n_face = down_cat.shape[1] // 3
    width = part.shape[1]
    previous, following = neighbours(at, info, even, odd, n_face)
    is_odd = info[at.odd] == 1
    count = jnp.where(is_odd, even[n_face:n_face + 1, :], odd[n_face:n_face + 1, :])
    slots = lax.broadcasted_iota(jnp.int32, (n_face, width), 0).astype(f32)
    live = jnp.where(slots < count, 1.0, 0.0).astype(bf16)
    zero, one = jnp.zeros_like(live), jnp.ones_like(live)
    down = jnp.concatenate([stacked(previous), jnp.concatenate([live, zero, live], 0)], 1)
    up = jnp.concatenate([stacked(following), jnp.concatenate([one, zero, one], 0)], 1)
    both = dot(down_cat[...], down) + dot(up_cat[...], up)
    degree = both[:, width:]
    diag_all[...] = diag[...] + degree
    out[...] = rhs[...] - (part[...] + degree * whole[...] - both[:, :width])


def face_kernel(at, info, even, odd, down_cat, up_cat, part, out):
    n_face = down_cat.shape[1] // 3
    previous, following = neighbours(at, info, even, odd, n_face)
    out[...] = part[...] - dot(down_cat[...], stacked(previous)) - dot(up_cat[...], stacked(following))


def row_sum(values):
    return jnp.sum(values, axis=1, keepdims=True)


def last_face_kernel(at, info, even, odd, down_cat, up_cat, part, first, second, early, out, sums, known):
    n_face = down_cat.shape[1] // 3
    previous, following = neighbours(at, info, even, odd, n_face)
    image = part[...] - dot(down_cat[...], stacked(previous)) - dot(up_cat[...], stacked(following))
    out[...] = image
    step = row_sum(early[0:1, :]) / row_sum(early[1:2, :])
    residual = first[...] - step * second[...]
    sums[...] = jnp.zeros_like(sums)
    sums[0:1, :] = jnp.sum(residual * image, axis=0, keepdims=True)
    known[...] = jnp.zeros_like(known)
    known[0:1, :] = jnp.sum(residual * residual, axis=0, keepdims=True)
    known[1:2, :] = jnp.sum(residual * second[...], axis=0, keepdims=True)


def step_kernel(info, early, known, late, out):
    step = row_sum(early[0:1, :]) / row_sum(early[1:2, :])
    out[...] = jnp.zeros_like(out)
    out[0:1, :] = known[0:1, :]
    out[1:2, :] = known[1:2, :] - step * late[0:1, :]


def last_kernel(at, info, start, first, second, third, early, final, solution, residual):
    own_rows = start.shape[0]
    place = pl.ds(pl.multiple_of(info[at.index] * own_rows, own_rows), own_rows)
    norm_zero, product_zero = row_sum(early[0:1, :]), row_sum(early[1:2, :])
    norm_one, product_one = row_sum(final[0:1, :]), row_sum(final[1:2, :])
    step_zero = norm_zero / product_zero
    beta = norm_one / norm_zero
    step_one = norm_one / (product_one - beta * norm_one / step_zero)
    zeroth, once, twice = first[place, :], second[place, :], third[...]
    after = zeroth - step_zero * once
    image = once - step_zero * twice
    direction = after + beta * zeroth
    moved = image + beta * once
    solution[...] = start[...] + step_zero * zeroth + step_one * direction
    residual[...] = after - step_one * moved


def shards(
    start_factors,
    bin_factors,
    tile_speed,
    tile_weight,
    tile_cells,
    tile_count,
    inner_pairs,
    inner_weight,
    face_rows,
    face_count,
    face_weight,
):
    start_whole = gather_rows(start_factors)
    weights = tile_weight[0, 0]
    n_tiles, tile, _ = weights.shape
    inner = inner_weight[0, 0]
    n_inner = inner.shape[0]
    rows = face_rows[0, 0]
    n_face = rows.shape[1]
    own_rows, width = start_factors.shape
    n_bin = lax.axis_size("bin")
    n_seg = lax.axis_size("seg")
    part_rows = own_rows * n_bin
    bin_blocks = bin_factors.shape[0] // tile
    at = Info(n_tiles, n_inner)
    info = jnp.concatenate(
        [
            tile_cells.reshape(-1),
            tile_count.reshape(-1),
            inner_pairs.reshape(-1),
            face_count.reshape(-1),
            (lax.axis_index("seg") % 2).reshape(1),
            lax.axis_index("bin").reshape(1),
        ]
    ).astype(jnp.int32)

    face = face_weight[0, 0]
    live_low = (jnp.arange(n_face, dtype=jnp.int32) < face_count[0, 0, 0]).astype(f32)
    face_next = lax.ppermute(
        face * live_low[:, None], "seg", [(i, i - 1) for i in range(1, n_seg)]
    )

    rows_shape = (part_rows, width)
    tile_flops = 2 * tile * tile * width
    rhs, gain, bins_t, bins_s, inner_cat, diag, pick_hot, scatter_hot, down_cat = call(
        functools.partial(prep_kernel, at, n_bin),
        [
            (rows_shape, f32),
            ((n_tiles, tile, tile), f32),
            ((bin_blocks, 2 * width, tile), bf16),
            ((bin_blocks, 2 * tile, width), bf16),
            ((n_inner, 2, tile, 3 * tile), bf16),
            (rows_shape, f32),
            ((2 * n_face, part_rows), bf16),
            ((part_rows, 2 * n_face), bf16),
            ((part_rows, 3 * n_face), bf16),
        ],
        info,
        weights,
        tile_speed[0, 0],
        bin_factors,
        inner,
        rows,
        face,
        flops=n_tiles * tile_flops,
    )
    (up_cat,) = call(
        up_kernel, [((part_rows, 3 * n_face), bf16)], info, face_next, scatter_hot, flops=tile_flops
    )

    message = ((n_face + PAD, width), f32)
    cat = ((part_rows, 2 * width), bf16)
    sums = ((PAD, width), f32)

    def main(whole, whole_cat, diagonal):
        (part,) = call(
            functools.partial(main_kernel, at),
            [(rows_shape, f32)],
            info,
            whole,
            whole_cat,
            bins_t,
            bins_s,
            gain,
            inner_cat,
            diagonal,
            scratch=[pltpu.VMEM((n_tiles + 2 * n_inner, tile, width), f32)],
            flops=6 * n_tiles * tile_flops,
        )
        return part

    start_cat, even, odd = call(
        functools.partial(pick_kernel, at, True), [cat, message, message], info, start_whole, pick_hot
    )
    even, odd = exchange_faces(even, odd)
    part = main(start_whole, start_cat, diag)
    part, diag_all = call(
        functools.partial(first_face_kernel, at),
        [(rows_shape, f32), (rows_shape, f32)],
        info, even, odd, down_cat, up_cat, part, start_whole, diag, rhs,
    )
    first = reduce_all(part)

    first_cat, even, odd = call(
        functools.partial(pick_kernel, at, True), [cat, message, message], info, first, pick_hot
    )
    even, odd = exchange_faces(even, odd)
    part = main(first, first_cat, diag_all)
    (part,) = call(
        functools.partial(face_kernel, at), [(rows_shape, f32)], info, even, odd, down_cat, up_cat, part
    )
    second = reduce_all(part)

    face_message = ((n_face, width), f32)
    second_cat, even, odd, early = call(
        functools.partial(pick_kernel, at, False),
        [cat, face_message, face_message, sums], info, second, pick_hot, first,
    )
    even, odd = exchange_faces(even, odd)
    early = reduce_seg(early)
    part = main(second, second_cat, diag_all)
    part, late, known = call(
        functools.partial(last_face_kernel, at),
        [(rows_shape, f32), sums, sums],
        info, even, odd, down_cat, up_cat, part, first, second, early,
    )
    third, late = reduce_own(part, late)
    (final,) = call(step_kernel, [sums], info, early, known, late)
    final = reduce_seg(final)
    return tuple(
        call(
            functools.partial(last_kernel, at),
            [(start_factors.shape, f32), (start_factors.shape, f32)],
            info, start_factors, first, second, third, early, final,
        )
    )


def solution(mesh):
    return jax.shard_map(
        shards,
        mesh=mesh,
        in_specs=(
            P(("groups", "seg", "bin"), None),
            P(("groups", "bin"), None),
            P(("groups", "seg"), "bin", None, None, None),
            P(("groups", "seg"), "bin", None, None, None),
            P(("groups", "seg"), "bin", None, None),
            P(("groups", "seg"), "bin"),
            P(("groups", "seg"), "bin", None, None),
            P(("groups", "seg"), "bin", None, None, None),
            P(("groups", "seg"), "bin", None, None),
            P(("groups", "seg"), "bin", None),
            P(("groups", "seg"), "bin", None, None),
        ),
        out_specs=(P(("groups", "seg", "bin"), None), P(("groups", "seg", "bin"), None)),
        check_vma=False,
    )
```

time: 143 us -> 82.1 us (0.57)
  other arithmetic: 27.8 us -> 1.33 us
  local copies, waits for them, and re-layouts: 28.1 us -> 4.18 us
  matrix products: 20.6 us -> 0 us
  Pallas kernels: 0 us -> 14.2 us
  between operations: 10.6 us -> 1.72 us
  starting transfers between devices: 24.3 us -> 32 us
  waiting for transfers between devices: 30.1 us -> 28.4 us
    dot_general x29 -> x0, matrix products: 20.6 us -> none  [the longest x3 4.63 us: apply_local(): jnp.dot(up.T, low_next[:faces], precision=highest)]
    pallas_call x0 -> x13, Pallas kernels: none -> 14.2 us  [call(): pl.pallas_call(kernel, out_shape=[jax.ShapeDtypeStruct(shape, kind) for s...]
    gather x16 -> x0, local copies, waits for them, and re-layouts: 13.9 us -> none  [the longest x3 3.96 us: apply_local(): picked = blocks[cells[:, 0]]]
    scatter-add x6 -> x0, other arithmetic: 13.2 us -> none  [apply_local(): return summed.at[rows_low].add(low_term).at[rows_up].add(up_term)]
    unnamed x116 -> x21, local copies, waits for them, and re-layouts: 9.77 us -> 3.91 us
    ppermute x16, starting transfers between devices: 15.3 us -> 19.1 us  [swap(): return lax.ppermute(x, axis, [(i, i ^ mask) for i in range(n)])]
    ppermute x7, starting transfers between devices: 9.06 us -> 12.9 us  [the longest x3 9.6 us: exchange_faces(): got_even = lax.ppermute(message_even, 'seg', exchange_pairs(n, 0))]
    reduce_sum x6 -> x0, other arithmetic: 3.79 us -> none  [the longest x1 1.43 us: shards(): jnp.sum(first * first)]
  transfers between devices with their start and end apart: 23 -> 23, of which waited for: 11 -> 14; matrix products, arithmetic and copies ran while one was open for 21% -> 1% of each run, Pallas kernels for 0% -> 9%
where the time goes in v2:
time: 82.1 us; the launch traced here: 81.8 us
  starting transfers between devices  32 us (39%)
  waiting for transfers between devices  28.4 us (35%)
  Pallas kernels  14.2 us (17%)
  local copies, waits for them, and re-layouts  4.18 us (5%)
  between operations  1.72 us (2%)
  other arithmetic  1.33 us (2%)
    ppermute x16, waiting for transfers between devices, swap(): return lax.ppermute(x, axis, [(i, i ^ mask) for i in range(n)])  22.8 us
    ppermute x16, starting transfers between devices, swap(): return lax.ppermute(x, axis, [(i, i ^ mask) for i in range(n)])  19.1 us
    pallas_call x13, Pallas kernels, call(): pl.pallas_call(kernel, out_shape=[jax.ShapeDtypeStruct(shape, kind) for s...  14.2 us
    ppermute x3, starting transfers between devices, exchange_faces(): got_even = lax.ppermute(message_even, 'seg', exchange_pairs(n, 0))  9.6 us
    ppermute x3, waiting for transfers between devices, exchange_faces(): got_even = lax.ppermute(message_even, 'seg', exchange_pairs(n, 0))  5.63 us
    unnamed x21, local copies, waits for them, and re-layouts  3.91 us
    ppermute x3, starting transfers between devices, exchange_faces(): got_odd = lax.ppermute(message_odd, 'seg', exchange_pairs(n, 1))  1.97 us
  transfers between devices with their start and end apart: 23, of which 14 were waited for; matrix products, arithmetic and copies ran while one was open for 1% of the time, Pallas kernels for 9%

profile of v2, /device:TPU:0, one launch (start us, length us, event | category | flops | bytes accessed | tf_op | source)
XLA Modules:
  0.0 81.8 jit_solution(13754363595869715142)
XLA Ops:
  0.6 3.0 %collective-permute-start = (f32[1,128,128]{2,1,0:T(8,128)}, f32[1,128,128]{2,1,0:T(8,128)S(1)}, u32[]{:S(2)}, u32[]{:S(2)}) collective-permute-start(f32[1,128,128]{2,1,0:T(8,128)} %bitcast.79), channel_id=1, source_target_pairs={{0,2},{1,3},{2,0},{3,1},{4,6},{5,7},{6,4},{7,5},{8,10},{9,11},{10,... | collective-permute-start | bytes 196616 | tf_op jit(solution)/shard_map/ppermute | solution.py:25
  4.4 1.7 %collective-permute-done = f32[1,128,128]{2,1,0:T(8,128)S(1)} collective-permute-done((f32[1,128,128]{2,1,0:T(8,128)}, f32[1,128,128]{2,1,0:T(8,128)S(1)}, u32[]{:S(2)}, u32[]{:S(2)}) %collective-permute-start) | collective-permute-done | bytes 65568 | tf_op jit(solution)/shard_map/ppermute | solution.py:25
  14.9 2.8 %collective-permute-start.2 = (f32[264,128]{1,0:T(8,128)S(1)}, f32[264,128]{1,0:T(8,128)S(1)}, u32[]{:S(2)}, u32[]{:S(2)}) collective-permute-start(f32[264,128]{1,0:T(8,128)S(1)} %get-tuple-element.27), channel_id=1, source_target_pairs={{0,4},{8,12},{4,0},{12,8},{1,5},{9,13},{5,1},{13,9},{2,6},{10,14},... | collective-permute-start | bytes 405512 | tf_op jit(solution)/shard_map/ppermute | solution.py:112
  18.4 1.4 %shard_map.125.part = f32[512,128]{1,0:T(8,128)S(1)} custom-call(s32[33]{0:T(128)S(1)} %concatenate.9.info, f32[512,128]{1,0:T(8,128)S(1)} %bitcast.72, bf16[512,256]{1,0:T(8,128)(2,1)S(1)} %get-tuple-element.31.whole_cat, bf16[8,256,128]{2,1,0:T(8,128)(2,1)S(1)} %get-tuple-element.32.bins_t, bf16[8,256,128]{2,1,0:T(8,128)(2,1)S(1)} %get-tuple-element.33.bins_s, ...), custom_call_target="tpu_custom_call" | custom-call | flops 301989888 | bytes 3014788 | tf_op jit(solution)/shard_map/pallas_call | solution.py:150
  23.2 1.3 %collective-permute-done.5 = f32[256,128]{1,0:T(8,128)S(1)} collective-permute-done((f32[256,128]{1,0:T(8,128)S(1)}, f32[256,128]{1,0:T(8,128)S(1)}, u32[]{:S(2)}, u32[]{:S(2)}) %collective-permute-start.5) | collective-permute-done | bytes 131104 | tf_op jit(solution)/shard_map/ppermute | solution.py:25
  24.5 1.7 %collective-permute-start.6 = (f32[256,128]{1,0:T(8,128)S(1)}, f32[256,128]{1,0:T(8,128)S(1)}, u32[]{:S(2)}, u32[]{:S(2)}) collective-permute-start(f32[256,128]{1,0:T(8,128)S(1)} %select_add_fusion.1), channel_id=1, source_target_pairs={{0,2},{1,3},{2,0},{3,1},{4,6},{5,7},{6,4},{7,5},{8,10},{9,11},{10,... | collective-permute-start | bytes 393224 | tf_op jit(solution)/shard_map/ppermute | solution.py:25
  26.3 3.9 %collective-permute-done.6 = f32[256,128]{1,0:T(8,128)S(1)} collective-permute-done((f32[256,128]{1,0:T(8,128)S(1)}, f32[256,128]{1,0:T(8,128)S(1)}, u32[]{:S(2)}, u32[]{:S(2)}) %collective-permute-start.6) | collective-permute-done | bytes 131104 | tf_op jit(solution)/shard_map/ppermute | solution.py:25
  32.5 5.0 %collective-permute-start.8 = (f32[264,128]{1,0:T(8,128)S(1)}, f32[264,128]{1,0:T(8,128)S(1)}, u32[]{:S(2)}, u32[]{:S(2)}) collective-permute-start(f32[264,128]{1,0:T(8,128)S(1)} %get-tuple-element.39), channel_id=1, source_target_pairs={{0,4},{8,12},{4,0},{12,8},{1,5},{9,13},{5,1},{13,9},{2,6},{10,14},... | collective-permute-start | bytes 405512 | tf_op jit(solution)/shard_map/ppermute | solution.py:112
  38.2 1.4 %shard_map.128.part = f32[512,128]{1,0:T(8,128)S(1)} custom-call(s32[33]{0:T(128)S(1)} %concatenate.9.info, f32[512,128]{1,0:T(8,128)S(1)} %bitcast.63, bf16[512,256]{1,0:T(8,128)(2,1)S(1)} %get-tuple-element.41.whole_cat, bf16[8,256,128]{2,1,0:T(8,128)(2,1)S(1)} %get-tuple-element.32.bins_t, bf16[8,256,128]{2,1,0:T(8,128)(2,1)S(1)} %get-tuple-element.33.bins_s, ...), custom_call_target="tpu_custom_call" | custom-call | flops 301989888 | bytes 3014788 | tf_op jit(solution)/shard_map/pallas_call | solution.py:150
  39.5 1.9 %collective-permute-done.8.even = f32[264,128]{1,0:T(8,128)S(1)} collective-permute-done((f32[264,128]{1,0:T(8,128)S(1)}, f32[264,128]{1,0:T(8,128)S(1)}, u32[]{:S(2)}, u32[]{:S(2)}) %collective-permute-start.8) | collective-permute-done | bytes 135200 | tf_op jit(solution)/shard_map/ppermute | solution.py:112
  44.0 1.6 %collective-permute-start.11 = (f32[256,128]{1,0:T(8,128)S(1)}, f32[256,128]{1,0:T(8,128)S(1)}, u32[]{:S(2)}, u32[]{:S(2)}) collective-permute-start(f32[256,128]{1,0:T(8,128)S(1)} %select_add_fusion), channel_id=1, source_target_pairs={{0,2},{1,3},{2,0},{3,1},{4,6},{5,7},{6,4},{7,5},{8,10},{9,11},{10,... | collective-permute-start | bytes 393224 | tf_op jit(solution)/shard_map/ppermute | solution.py:25
  45.5 4.1 %collective-permute-done.11 = f32[256,128]{1,0:T(8,128)S(1)} collective-permute-done((f32[256,128]{1,0:T(8,128)S(1)}, f32[256,128]{1,0:T(8,128)S(1)}, u32[]{:S(2)}, u32[]{:S(2)}) %collective-permute-start.11) | collective-permute-done | bytes 131104 | tf_op jit(solution)/shard_map/ppermute | solution.py:25
  52.0 2.7 %collective-permute-start.17 = (f32[8,128]{1,0:T(8,128)S(1)}, f32[8,128]{1,0:T(8,128)S(1)}, u32[]{:S(2)}, u32[]{:S(2)}) collective-permute-start(f32[8,128]{1,0:T(8,128)S(1)} %get-tuple-element.46), channel_id=1, source_target_pairs={{0,12},{4,8},{8,4},{12,0},{1,13},{5,9},{9,5},{13,1},{2,14},{6,10},... | collective-permute-start | bytes 12296 | tf_op jit(solution)/shard_map/ppermute | solution.py:25
  54.7 2.5 %collective-permute-start.16 = (f32[8,128]{1,0:T(8,128)S(1)}, f32[8,128]{1,0:T(8,128)S(1)}, u32[]{:S(2)}, u32[]{:S(2)}) collective-permute-start(f32[8,128]{1,0:T(8,128)S(1)} %get-tuple-element.46), channel_id=1, source_target_pairs={{0,8},{4,12},{8,0},{12,4},{1,9},{5,13},{9,1},{13,5},{2,10},{6,14},... | collective-permute-start | bytes 12296 | tf_op jit(solution)/shard_map/ppermute | solution.py:25
  57.4 1.4 %shard_map.131.part = f32[512,128]{1,0:T(8,128)S(1)} custom-call(s32[33]{0:T(128)S(1)} %concatenate.9.info, f32[512,128]{1,0:T(8,128)S(1)} %bitcast.68, bf16[512,256]{1,0:T(8,128)(2,1)S(1)} %get-tuple-element.45.whole_cat, bf16[8,256,128]{2,1,0:T(8,128)(2,1)S(1)} %get-tuple-element.32.bins_t, bf16[8,256,128]{2,1,0:T(8,128)(2,1)S(1)} %get-tuple-element.33.bins_s, ...), custom_call_target="tpu_custom_call" | custom-call | flops 301989888 | bytes 3014788 | tf_op jit(solution)/shard_map/pallas_call | solution.py:150
  58.8 1.8 %collective-permute-start.13 = (f32[256,128]{1,0:T(8,128)S(1)}, f32[256,128]{1,0:T(8,128)S(1)}, u32[]{:S(2)}, u32[]{:S(2)}) collective-permute-start(f32[256,128]{1,0:T(8,128)S(1)} %get-tuple-element.43), channel_id=1, source_target_pairs={{0,4},{8,12},{4,0},{12,8},{1,5},{9,13},{5,1},{13,9},{2,6},{10,14},... | collective-permute-start | bytes 393224 | tf_op jit(solution)/shard_map/ppermute | solution.py:112
  61.3 2.5 %collective-permute-done.13.even = f32[256,128]{1,0:T(8,128)S(1)} collective-permute-done((f32[256,128]{1,0:T(8,128)S(1)}, f32[256,128]{1,0:T(8,128)S(1)}, u32[]{:S(2)}, u32[]{:S(2)}) %collective-permute-start.13) | collective-permute-done | bytes 131104 | tf_op jit(solution)/shard_map/ppermute | solution.py:112
  65.1 1.3 %collective-permute-done.18 = f32[264,128]{1,0:T(8,128)S(1)} collective-permute-done((f32[264,128]{1,0:T(8,128)S(1)}, f32[264,128]{1,0:T(8,128)S(1)}, u32[]{:S(2)}, u32[]{:S(2)}) %collective-permute-start.18) | collective-permute-done | bytes 135200 | tf_op jit(solution)/shard_map/ppermute | solution.py:25
  66.5 1.6 %collective-permute-start.19 = (f32[136,128]{1,0:T(8,128)S(1)}, f32[136,128]{1,0:T(8,128)S(1)}, u32[]{:S(2)}, u32[]{:S(2)}) collective-permute-start(f32[136,128]{1,0:T(8,128)S(1)} %pad_maximum_fusion.4), channel_id=1, source_target_pairs={{0,2},{1,3},{2,0},{3,1},{4,6},{5,7},{6,4},{7,5},{8,10},{9,11},{10,... | collective-permute-start | bytes 208904 | tf_op jit(solution)/shard_map/ppermute | solution.py:25
  68.1 2.8 %collective-permute-done.19 = f32[136,128]{1,0:T(8,128)S(1)} collective-permute-done((f32[136,128]{1,0:T(8,128)S(1)}, f32[136,128]{1,0:T(8,128)S(1)}, u32[]{:S(2)}, u32[]{:S(2)}) %collective-permute-start.19) | collective-permute-done | bytes 69664 | tf_op jit(solution)/shard_map/ppermute | solution.py:25
  71.5 2.4 %collective-permute-start.22 = (f32[8,128]{1,0:T(8,128)S(1)}, f32[8,128]{1,0:T(8,128)S(1)}, u32[]{:S(2)}, u32[]{:S(2)}) collective-permute-start(f32[8,128]{1,0:T(8,128)S(1)} %shard_map.133), channel_id=1, source_target_pairs={{0,12},{4,8},{8,4},{12,0},{1,13},{5,9},{9,5},{13,1},{2,14},{6,10},... | collective-permute-start | bytes 12296 | tf_op jit(solution)/shard_map/ppermute | solution.py:25
  73.9 3.0 %collective-permute-start.21 = (f32[8,128]{1,0:T(8,128)S(1)}, f32[8,128]{1,0:T(8,128)S(1)}, u32[]{:S(2)}, u32[]{:S(2)}) collective-permute-start(f32[8,128]{1,0:T(8,128)S(1)} %shard_map.133), channel_id=1, source_target_pairs={{0,8},{4,12},{8,0},{12,4},{1,9},{5,13},{9,1},{13,5},{2,10},{6,14},... | collective-permute-start | bytes 12296 | tf_op jit(solution)/shard_map/ppermute | solution.py:25
  76.9 1.6 %collective-permute-done.21 = f32[8,128]{1,0:T(8,128)S(1)} collective-permute-done((f32[8,128]{1,0:T(8,128)S(1)}, f32[8,128]{1,0:T(8,128)S(1)}, u32[]{:S(2)}, u32[]{:S(2)}) %collective-permute-start.21) | collective-permute-done | bytes 4128 | tf_op jit(solution)/shard_map/ppermute | solution.py:25
  78.5 2.0 %collective-permute-done.20 = f32[8,128]{1,0:T(8,128)S(1)} collective-permute-done((f32[8,128]{1,0:T(8,128)S(1)}, f32[8,128]{1,0:T(8,128)S(1)}, u32[]{:S(2)}, u32[]{:S(2)}) %collective-permute-start.20) | collective-permute-done | bytes 4128 | tf_op jit(solution)/shard_map/ppermute | solution.py:25
  (87 shorter events, 24.9 us)
Async XLA Ops:
  0.6 5.5 %collective-permute-start = (f32[1,128,128]{2,1,0:T(8,128)}, f32[1,128,128]{2,1,0:T(8,128)S(1)}, u32[]{:S(2)}, u32[]{:S(2)}) collective-permute-start(f32[1,128,128]{2,1,0:T(8,128)} %bitcast.79), channel_id=1, source_target_pairs={{0,2},{1,3},{2,0},{3,1},{4,6},{5,7},{6,4},{7,5},{8,10},{9,11},{10,... | collective-permute-start | bytes 196616 | tf_op jit(solution)/shard_map/ppermute | solution.py:25
  7.0 6.9 %collective-permute-start.1 = (f32[2,128,128]{2,1,0:T(8,128)S(1)}, f32[2,128,128]{2,1,0:T(8,128)S(1)}, u32[]{:S(2)}, u32[]{:S(2)}) collective-permute-start(f32[2,128,128]{2,1,0:T(8,128)S(1)} %maximum_bitcast_fusion), channel_id=1, source_target_pairs={{0,1},{1,0},{2,3},{3,2},{4,5},{5,4},{6,7},{7,6},{8,9},{9,8},{10,11... | collective-permute-start | bytes 393224 | tf_op jit(solution)/shard_map/ppermute | solution.py:25
  7.2 12.5 %collective-permute-start.4 = (f32[256,256]{1,0:T(8,128)S(1)}, f32[256,256]{1,0:T(8,128)S(1)}, u32[]{:S(2)}, u32[]{:S(2)}) collective-permute-start(f32[256,256]{1,0:T(8,128)S(1)} %broadcast_multiply_fusion), channel_id=1, source_target_pairs={{4,0},{8,4},{12,8},{5,1},{9,5},{13,9},{6,2},{10,6},{14,10},{7,3},{... | collective-permute-start | bytes 786440 | tf_op jit(solution)/shard_map/ppermute | solution.py:380
  14.9 7.0 %collective-permute-start.2 = (f32[264,128]{1,0:T(8,128)S(1)}, f32[264,128]{1,0:T(8,128)S(1)}, u32[]{:S(2)}, u32[]{:S(2)}) collective-permute-start(f32[264,128]{1,0:T(8,128)S(1)} %get-tuple-element.27), channel_id=1, source_target_pairs={{0,4},{8,12},{4,0},{12,8},{1,5},{9,13},{5,1},{13,9},{2,6},{10,14},... | collective-permute-start | bytes 405512 | tf_op jit(solution)/shard_map/ppermute | solution.py:112
  17.7 4.2 %collective-permute-start.3 = (f32[264,128]{1,0:T(8,128)S(1)}, f32[264,128]{1,0:T(8,128)S(1)}, u32[]{:S(2)}, u32[]{:S(2)}) collective-permute-start(f32[264,128]{1,0:T(8,128)S(1)} %get-tuple-element.28), channel_id=1, source_target_pairs={{4,8},{8,4},{5,9},{9,5},{6,10},{10,6},{7,11},{11,7},{20,24},{24,20... | collective-permute-start | bytes 405512 | tf_op jit(solution)/shard_map/ppermute | solution.py:113
  23.1 1.4 %collective-permute-start.5 = (f32[256,128]{1,0:T(8,128)S(1)}, f32[256,128]{1,0:T(8,128)S(1)}, u32[]{:S(2)}, u32[]{:S(2)}) collective-permute-start(f32[256,128]{1,0:T(8,128)S(1)} %slice_select_fusion.1), channel_id=1, source_target_pairs={{0,1},{1,0},{2,3},{3,2},{4,5},{5,4},{6,7},{7,6},{8,9},{9,8},{10,11... | collective-permute-start | bytes 393224 | tf_op jit(solution)/shard_map/ppermute | solution.py:25
  24.5 5.6 %collective-permute-start.6 = (f32[256,128]{1,0:T(8,128)S(1)}, f32[256,128]{1,0:T(8,128)S(1)}, u32[]{:S(2)}, u32[]{:S(2)}) collective-permute-start(f32[256,128]{1,0:T(8,128)S(1)} %select_add_fusion.1), channel_id=1, source_target_pairs={{0,2},{1,3},{2,0},{3,1},{4,6},{5,7},{6,4},{7,5},{8,10},{9,11},{10,... | collective-permute-start | bytes 393224 | tf_op jit(solution)/shard_map/ppermute | solution.py:25
  30.2 1.4 %collective-permute-start.7 = (f32[256,128]{1,0:T(8,128)S(1)}, f32[256,128]{1,0:T(8,128)S(1)}, u32[]{:S(2)}, u32[]{:S(2)}) collective-permute-start(f32[256,128]{1,0:T(8,128)S(1)} %add.56), channel_id=1, source_target_pairs={{0,1},{1,0},{2,3},{3,2},{4,5},{5,4},{6,7},{7,6},{8,9},{9,8},{10,11... | collective-permute-start | bytes 393224 | tf_op jit(solution)/shard_map/ppermute | solution.py:25
  32.5 8.9 %collective-permute-start.8 = (f32[264,128]{1,0:T(8,128)S(1)}, f32[264,128]{1,0:T(8,128)S(1)}, u32[]{:S(2)}, u32[]{:S(2)}) collective-permute-start(f32[264,128]{1,0:T(8,128)S(1)} %get-tuple-element.39), channel_id=1, source_target_pairs={{0,4},{8,12},{4,0},{12,8},{1,5},{9,13},{5,1},{13,9},{2,6},{10,14},... | collective-permute-start | bytes 405512 | tf_op jit(solution)/shard_map/ppermute | solution.py:112
  37.5 3.9 %collective-permute-start.9 = (f32[264,128]{1,0:T(8,128)S(1)}, f32[264,128]{1,0:T(8,128)S(1)}, u32[]{:S(2)}, u32[]{:S(2)}) collective-permute-start(f32[264,128]{1,0:T(8,128)S(1)} %get-tuple-element.40), channel_id=1, source_target_pairs={{4,8},{8,4},{5,9},{9,5},{6,10},{10,6},{7,11},{11,7},{20,24},{24,20... | collective-permute-start | bytes 405512 | tf_op jit(solution)/shard_map/ppermute | solution.py:113
  42.6 1.4 %collective-permute-start.10 = (f32[256,128]{1,0:T(8,128)S(1)}, f32[256,128]{1,0:T(8,128)S(1)}, u32[]{:S(2)}, u32[]{:S(2)}) collective-permute-start(f32[256,128]{1,0:T(8,128)S(1)} %slice_select_fusion), channel_id=1, source_target_pairs={{0,1},{1,0},{2,3},{3,2},{4,5},{5,4},{6,7},{7,6},{8,9},{9,8},{10,11... | collective-permute-start | bytes 393224 | tf_op jit(solution)/shard_map/ppermute | solution.py:25
  44.0 5.6 %collective-permute-start.11 = (f32[256,128]{1,0:T(8,128)S(1)}, f32[256,128]{1,0:T(8,128)S(1)}, u32[]{:S(2)}, u32[]{:S(2)}) collective-permute-start(f32[256,128]{1,0:T(8,128)S(1)} %select_add_fusion), channel_id=1, source_target_pairs={{0,2},{1,3},{2,0},{3,1},{4,6},{5,7},{6,4},{7,5},{8,10},{9,11},{10,... | collective-permute-start | bytes 393224 | tf_op jit(solution)/shard_map/ppermute | solution.py:25
  49.6 1.4 %collective-permute-start.12 = (f32[256,128]{1,0:T(8,128)S(1)}, f32[256,128]{1,0:T(8,128)S(1)}, u32[]{:S(2)}, u32[]{:S(2)}) collective-permute-start(f32[256,128]{1,0:T(8,128)S(1)} %add.58), channel_id=1, source_target_pairs={{0,1},{1,0},{2,3},{3,2},{4,5},{5,4},{6,7},{7,6},{8,9},{9,8},{10,11... | collective-permute-start | bytes 393224 | tf_op jit(solution)/shard_map/ppermute | solution.py:25
  52.0 9.3 %collective-permute-start.17 = (f32[8,128]{1,0:T(8,128)S(1)}, f32[8,128]{1,0:T(8,128)S(1)}, u32[]{:S(2)}, u32[]{:S(2)}) collective-permute-start(f32[8,128]{1,0:T(8,128)S(1)} %get-tuple-element.46), channel_id=1, source_target_pairs={{0,12},{4,8},{8,4},{12,0},{1,13},{5,9},{9,5},{13,1},{2,14},{6,10},... | collective-permute-start | bytes 12296 | tf_op jit(solution)/shard_map/ppermute | solution.py:25
  54.7 6.6 %collective-permute-start.16 = (f32[8,128]{1,0:T(8,128)S(1)}, f32[8,128]{1,0:T(8,128)S(1)}, u32[]{:S(2)}, u32[]{:S(2)}) collective-permute-start(f32[8,128]{1,0:T(8,128)S(1)} %get-tuple-element.46), channel_id=1, source_target_pairs={{0,8},{4,12},{8,0},{12,4},{1,9},{5,13},{9,1},{13,5},{2,10},{6,14},... | collective-permute-start | bytes 12296 | tf_op jit(solution)/shard_map/ppermute | solution.py:25
  57.1 4.1 %collective-permute-start.15 = (f32[8,128]{1,0:T(8,128)S(1)}, f32[8,128]{1,0:T(8,128)S(1)}, u32[]{:S(2)}, u32[]{:S(2)}) collective-permute-start(f32[8,128]{1,0:T(8,128)S(1)} %get-tuple-element.46), channel_id=1, source_target_pairs={{0,4},{4,0},{8,12},{12,8},{1,5},{5,1},{9,13},{13,9},{2,6},{6,2},{1... | collective-permute-start | bytes 12296 | tf_op jit(solution)/shard_map/ppermute | solution.py:25
  58.8 5.1 %collective-permute-start.13 = (f32[256,128]{1,0:T(8,128)S(1)}, f32[256,128]{1,0:T(8,128)S(1)}, u32[]{:S(2)}, u32[]{:S(2)}) collective-permute-start(f32[256,128]{1,0:T(8,128)S(1)} %get-tuple-element.43), channel_id=1, source_target_pairs={{0,4},{8,12},{4,0},{12,8},{1,5},{9,13},{5,1},{13,9},{2,6},{10,14},... | collective-permute-start | bytes 393224 | tf_op jit(solution)/shard_map/ppermute | solution.py:112
  60.6 3.2 %collective-permute-start.14 = (f32[256,128]{1,0:T(8,128)S(1)}, f32[256,128]{1,0:T(8,128)S(1)}, u32[]{:S(2)}, u32[]{:S(2)}) collective-permute-start(f32[256,128]{1,0:T(8,128)S(1)} %get-tuple-element.44), channel_id=1, source_target_pairs={{4,8},{8,4},{5,9},{9,5},{6,10},{10,6},{7,11},{11,7},{20,24},{24,20... | collective-permute-start | bytes 393224 | tf_op jit(solution)/shard_map/ppermute | solution.py:113
  65.0 1.4 %collective-permute-start.18 = (f32[264,128]{1,0:T(8,128)S(1)}, f32[264,128]{1,0:T(8,128)S(1)}, u32[]{:S(2)}, u32[]{:S(2)}) collective-permute-start(f32[264,128]{1,0:T(8,128)S(1)} %pad_maximum_fusion.3), channel_id=1, source_target_pairs={{0,1},{1,0},{2,3},{3,2},{4,5},{5,4},{6,7},{7,6},{8,9},{9,8},{10,11... | collective-permute-start | bytes 405512 | tf_op jit(solution)/shard_map/ppermute | solution.py:25
  66.5 4.4 %collective-permute-start.19 = (f32[136,128]{1,0:T(8,128)S(1)}, f32[136,128]{1,0:T(8,128)S(1)}, u32[]{:S(2)}, u32[]{:S(2)}) collective-permute-start(f32[136,128]{1,0:T(8,128)S(1)} %pad_maximum_fusion.4), channel_id=1, source_target_pairs={{0,2},{1,3},{2,0},{3,1},{4,6},{5,7},{6,4},{7,5},{8,10},{9,11},{10,... | collective-permute-start | bytes 208904 | tf_op jit(solution)/shard_map/ppermute | solution.py:25
  71.5 9.0 %copy-start.3 = (f32[128,128]{1,0:T(8,128)S(1)}, f32[128,128]{1,0:T(8,128)}, u32[]{:S(2)}) copy-start(f32[128,128]{1,0:T(8,128)} %start.1) | copy-start | bytes 196612
  71.5 5.4 %collective-permute-start.22 = (f32[8,128]{1,0:T(8,128)S(1)}, f32[8,128]{1,0:T(8,128)S(1)}, u32[]{:S(2)}, u32[]{:S(2)}) collective-permute-start(f32[8,128]{1,0:T(8,128)S(1)} %shard_map.133), channel_id=1, source_target_pairs={{0,12},{4,8},{8,4},{12,0},{1,13},{5,9},{9,5},{13,1},{2,14},{6,10},... | collective-permute-start | bytes 12296 | tf_op jit(solution)/shard_map/ppermute | solution.py:25
  73.9 4.6 %collective-permute-start.21 = (f32[8,128]{1,0:T(8,128)S(1)}, f32[8,128]{1,0:T(8,128)S(1)}, u32[]{:S(2)}, u32[]{:S(2)}) collective-permute-start(f32[8,128]{1,0:T(8,128)S(1)} %shard_map.133), channel_id=1, source_target_pairs={{0,8},{4,12},{8,0},{12,4},{1,9},{5,13},{9,1},{13,5},{2,10},{6,14},... | collective-permute-start | bytes 12296 | tf_op jit(solution)/shard_map/ppermute | solution.py:25
  76.9 3.6 %collective-permute-start.20 = (f32[8,128]{1,0:T(8,128)S(1)}, f32[8,128]{1,0:T(8,128)S(1)}, u32[]{:S(2)}, u32[]{:S(2)}) collective-permute-start(f32[8,128]{1,0:T(8,128)S(1)} %shard_map.133), channel_id=1, source_target_pairs={{0,4},{4,0},{8,12},{12,8},{1,5},{5,1},{9,13},{13,9},{2,6},{6,2},{1... | collective-permute-start | bytes 12296 | tf_op jit(solution)/shard_map/ppermute | solution.py:25
  (9 other events, 13.7 us)

commit v3 on v2

v3 whole, which is shorter than its diff:
```python
import functools

import jax
import jax.numpy as jnp
from jax import lax
from jax.experimental import pallas as pl
from jax.experimental.pallas import tpu as pltpu
from jax.sharding import PartitionSpec as P

ITERS = 2
PAD = 8
VMEM_BYTES = 16 << 20

f32 = jnp.float32
bf16 = jnp.bfloat16
ridge_weight = 0.5


def is_power_of_two(n):
    return n & (n - 1) == 0


def swap(x, axis, mask):
    n = lax.axis_size(axis)
    return lax.ppermute(x, axis, [(i, i ^ mask) for i in range(n)])


def bit_of(axis, mask):
    return (lax.axis_index(axis) & mask) != 0


def ordered(bit, mine, other, dim):
    first = jnp.where(bit, other, mine)
    second = jnp.where(bit, mine, other)
    return jnp.stack([first, second], dim)


def gather_rows(own, copy):
    n = lax.axis_size("bin")
    if not is_power_of_two(n):
        return lax.all_gather(own, "bin", axis=0, tiled=True)
    sent, held = own[None], copy[None]
    mask = n // 2
    while mask:
        held = ordered(bit_of("bin", mask), held, swap(sent, "bin", mask), 1)
        held = held.reshape((-1,) + own.shape)
        sent = held
        mask //= 2
    return held.reshape(-1, own.shape[-1])


def reduce_all(partial_rows):
    n = lax.axis_size("bin")
    if n == 1:
        return partial_rows
    if not is_power_of_two(n):
        return lax.psum(partial_rows, "bin")
    half = partial_rows.shape[0] // 2
    odd = bit_of("bin", 1)
    low, high = partial_rows[:half], partial_rows[half:]
    kept = jnp.where(odd, high, low) + swap(jnp.where(odd, low, high), "bin", 1)
    mask = 2
    while mask < n:
        kept = kept + swap(kept, "bin", mask)
        mask *= 2
    return ordered(odd, kept, swap(kept, "bin", 1), 0).reshape(partial_rows.shape)


def reduce_own(partial_rows, sums):
    n = lax.axis_size("bin")
    width = partial_rows.shape[1]
    if not is_power_of_two(n):
        own = lax.psum_scatter(partial_rows, "bin", scatter_dimension=0, tiled=True)
        return own, lax.psum(sums, "bin")
    blocks = partial_rows.reshape(n, -1, width)
    mask = 1
    while mask < n:
        split = blocks.reshape(-1, 2, blocks.shape[1], width)
        bit = bit_of("bin", mask)
        sent = jnp.where(bit, split[:, 0], split[:, 1])
        kept = jnp.where(bit, split[:, 1], split[:, 0])
        count = sent.shape[0] * sent.shape[1]
        message = jnp.concatenate([sent.reshape(count, width), sums], 0)
        got = swap(message, "bin", mask)
        blocks = kept + got[:count].reshape(kept.shape)
        sums = sums + got[count:]
        mask *= 2
    return blocks.reshape(-1, width), sums


def reduce_seg(sums):
    n = lax.axis_size("seg")
    if not is_power_of_two(n):
        return lax.psum(sums, "seg")
    mask = 1
    while mask < n:
        if mask * 2 < n:
            sums = sums + swap(sums, "seg", mask) + swap(sums, "seg", 2 * mask) + swap(sums, "seg", 3 * mask)
            mask *= 4
        else:
            sums = sums + swap(sums, "seg", mask)
            mask *= 2
    return sums


def face_pairs(first):
    n_seg, n_bin = lax.axis_size("seg"), lax.axis_size("bin")
    pairs = []
    for s in range(n_seg):
        other = s + 1 if (s - first) % 2 == 0 else s - 1
        for t in range(n_bin):
            if 0 <= other < n_seg:
                pairs.append((s * n_bin + t, other * n_bin + t))
            elif n_bin % 2 == 0:
                pairs.append((s * n_bin + t, s * n_bin + (t ^ 1)))
    return pairs


def exchange_faces(message_even, message_odd):
    got_even = lax.ppermute(message_even, ("seg", "bin"), face_pairs(0))
    got_odd = lax.ppermute(message_odd, ("seg", "bin"), face_pairs(1))
    return got_even, got_odd


def split(x):
    high = x.astype(bf16)
    return high, (x - high.astype(f32)).astype(bf16)


def dot(a, b):
    return lax.dot_general(a, b, (((1,), (0,)), ((), ())), preferred_element_type=f32)


def along(x):
    high, low = split(x)
    return jnp.concatenate([high, high, low], 1)


def stacked(x):
    high, low = split(x)
    return jnp.concatenate([high, low, high], 0)


def call(kernel, outs, *operands, smem=(), hbm=False, scratch=(), flops=0):
    in_smem = pl.BlockSpec(memory_space=pltpu.SMEM)
    in_vmem = pl.BlockSpec(memory_space=pltpu.VMEM)
    given = pl.BlockSpec(memory_space=pltpu.HBM) if hbm else in_vmem
    nbytes = sum(o.size * o.dtype.itemsize for o in operands)
    return pl.pallas_call(
        kernel,
        out_shape=[jax.ShapeDtypeStruct(shape, kind) for shape, kind in outs],
        in_specs=[in_smem] * len(smem) + [given] * len(operands),
        out_specs=[in_vmem] * len(outs),
        scratch_shapes=scratch,
        compiler_params=pltpu.CompilerParams(vmem_limit_bytes=VMEM_BYTES),
        cost_estimate=pl.CostEstimate(flops=flops, bytes_accessed=nbytes, transcendentals=0),
    )(*smem, *operands)


def block_at(index, size):
    return pl.ds(pl.multiple_of(index * size, size), size)


def prep_kernel(n_bin, cells, count, pairs, faces,
                start_hbm, bins_hbm, rows_hbm, face_hbm, inner_hbm, weights_hbm, speeds_hbm,
                start, rhs, gain, bins_t, bins_s, inner_cat, diag, pick_hot, scatter_up, down_cat,
                bins, rows, face, inner, weights, speeds, sems):
    moves = [
        pltpu.make_async_copy(source, target, sems.at[i])
        for i, (source, target) in enumerate([
            (rows_hbm, rows), (face_hbm, face), (start_hbm, start), (bins_hbm, bins),
            (inner_hbm, inner), (weights_hbm, weights), (speeds_hbm, speeds),
        ])
    ]
    for move in moves:
        move.start()
    n_tiles, tile, _ = weights.shape
    width = bins.shape[1]
    part_rows = rhs.shape[0]
    n_face = rows.shape[1]
    is_odd = lax.axis_index("seg") % 2 == 1
    is_first = lax.axis_index("seg") == 0
    rhs[...] = jnp.zeros_like(rhs)
    diag[...] = jnp.full(diag.shape, ridge_weight / n_bin, f32)
    slots = lax.broadcasted_iota(jnp.int32, (1, n_face), 1)
    ids = lax.broadcasted_iota(jnp.int32, (part_rows, n_face), 0)
    moves[0].wait()
    hots = []
    for side in range(2):
        listed = jnp.where(slots < faces[0, side], rows[side:side + 1, :], -1)
        hots.append((ids == listed).astype(f32))
    scatter_up[...] = hots[1].astype(bf16)
    low_t, up_t = hots[0].T.astype(bf16), hots[1].T.astype(bf16)
    pick_hot[0:n_face, :] = jnp.where(is_odd, low_t, up_t)
    pick_hot[n_face:, :] = jnp.where(is_odd, up_t, low_t)
    moves[1].wait()
    high, low = split(jnp.where(is_first, 0.0, face[...]))
    hot = hots[0].astype(bf16)
    high = dot(hot, high).astype(bf16)
    low = dot(hot, low).astype(bf16)
    down_cat[...] = jnp.concatenate([high, high, low], 1)
    moves[2].wait()
    moves[3].wait()
    for k in range(bins.shape[0] // tile):
        block = bins[k * tile:(k + 1) * tile, :]
        flipped = block.astype(f32).T.astype(bf16)
        bins_t[k] = jnp.concatenate([flipped, flipped], 0)
        bins_s[k] = jnp.concatenate([block, block], 0)
    moves[4].wait()
    for j in range(inner.shape[0]):
        block = inner[j]
        flipped = block.T
        inner_cat[j, 0] = along(block)
        inner_cat[j, 1] = along(flipped)
        for side, matrix in enumerate((block, flipped)):
            degree = jnp.sum(matrix, axis=1, keepdims=True)
            diag[block_at(pairs[j, side], tile), :] += jnp.broadcast_to(degree, (tile, width))
    moves[5].wait()
    moves[6].wait()
    for k in range(n_tiles):
        wide = weights[k].astype(f32)
        live = jnp.where(k < count[0, 0], 1.0, 0.0).astype(f32)
        gain[k] = wide * live
        weighted = (wide * speeds[k].astype(f32)).astype(bf16)
        terms = dot(weighted, bins[block_at(cells[1, k], tile), :]) * live
        rhs[block_at(cells[0, k], tile), :] += terms


def up_kernel(face_even, face_odd, scatter_up, down_cat, cat_even, cat_odd):
    index = lax.axis_index("seg")
    is_odd = index % 2 == 1
    is_last = index == lax.axis_size("seg") - 1
    following = jnp.where(is_odd, face_odd[...], face_even[...])
    high, low = split(jnp.where(is_last, 0.0, following).T)
    hot = scatter_up[...]
    high = dot(hot, high).astype(bf16)
    low = dot(hot, low).astype(bf16)
    up = jnp.concatenate([high, high, low], 1)
    down = down_cat[...]
    cat_even[...] = jnp.where(is_odd, down, up)
    cat_odd[...] = jnp.where(is_odd, up, down)


def pick(whole, pick_hot, whole_cat):
    width = whole.shape[1]
    high, low = split(whole[...])
    cat = jnp.concatenate([high, low], 1)
    whole_cat[...] = cat
    picked = dot(pick_hot[...], cat)
    return picked[:, :width] + picked[:, width:]


def first_pick_kernel(whole, pick_hot, counts, whole_cat, even, odd):
    picked = pick(whole, pick_hot, whole_cat)
    n_face = picked.shape[0] // 2
    even[0:n_face, :] = picked[:n_face]
    odd[0:n_face, :] = picked[n_face:]
    even[n_face:, :] = counts[0:PAD, :]
    odd[n_face:, :] = counts[PAD:, :]


def pick_kernel(whole, pick_hot, whole_cat, even, odd):
    picked = pick(whole, pick_hot, whole_cat)
    n_face = picked.shape[0] // 2
    even[...] = picked[:n_face]
    odd[...] = picked[n_face:]


def main_kernel(cells, pairs, whole, whole_cat, bins_t, bins_s, gain, inner_cat, diag, *refs):
    if len(refs) == 4:
        before, out, sums, terms = refs
        now, old = whole[...], before[...]
        sums[...] = jnp.zeros_like(sums)
        sums[0:1, :] = jnp.sum(old * old, axis=0, keepdims=True)
        sums[1:2, :] = jnp.sum(old * now, axis=0, keepdims=True)
    else:
        out, terms = refs
    n_tiles, tile, _ = gain.shape
    width = whole.shape[1]
    for k in range(n_tiles):
        scores = dot(whole_cat[block_at(cells[0, k], tile), :], bins_t[cells[1, k]]) * gain[k]
        high, low = split(scores)
        terms[k] = dot(jnp.concatenate([high, low], 1), bins_s[cells[1, k]])
    n_inner = inner_cat.shape[0]
    for j in range(n_inner):
        for side in range(2):
            other = whole_cat[block_at(pairs[j, 1 - side], tile), :]
            high, low = other[:, :width], other[:, width:]
            terms[n_tiles + 2 * j + side] = -dot(inner_cat[j, side], jnp.concatenate([high, low, high], 0))
    out[...] = diag[...] * whole[...]
    for k in range(n_tiles):
        out[block_at(cells[0, k], tile), :] += terms[k]
    for j in range(n_inner):
        for side in range(2):
            out[block_at(pairs[j, side], tile), :] += terms[n_tiles + 2 * j + side]


def first_face_kernel(even, odd, cat_even, cat_odd, part, whole, diag, rhs, out, diag_all):
    n_face = cat_even.shape[1] // 3
    width = part.shape[1]
    slots = lax.broadcasted_iota(jnp.int32, (n_face, width), 0).astype(f32)
    both = jnp.zeros((part.shape[0], 2 * width), f32)
    for got, cat in ((even, cat_even), (odd, cat_odd)):
        live = jnp.where(slots < got[n_face:n_face + 1, :], 1.0, 0.0).astype(bf16)
        seen = jnp.concatenate([live, jnp.zeros_like(live), live], 0)
        both = both + dot(cat[...], jnp.concatenate([stacked(got[0:n_face, :]), seen], 1))
    degree = both[:, width:]
    diag_all[...] = diag[...] + degree
    out[...] = rhs[...] - (part[...] + degree * whole[...] - both[:, :width])


def face_image(even, odd, cat_even, cat_odd, part):
    return part[...] - dot(cat_even[...], stacked(even[...])) - dot(cat_odd[...], stacked(odd[...]))


def face_kernel(even, odd, cat_even, cat_odd, part, out):
    out[...] = face_image(even, odd, cat_even, cat_odd, part)


def row_sum(values):
    return jnp.sum(values, axis=1, keepdims=True)


def last_face_kernel(even, odd, cat_even, cat_odd, part, first, second, early, out, sums, known):
    image = face_image(even, odd, cat_even, cat_odd, part)
    out[...] = image
    step = row_sum(early[0:1, :]) / row_sum(early[1:2, :])
    residual = first[...] - step * second[...]
    sums[...] = jnp.zeros_like(sums)
    sums[0:1, :] = jnp.sum(residual * image, axis=0, keepdims=True)
    known[...] = jnp.zeros_like(known)
    known[0:1, :] = jnp.sum(residual * residual, axis=0, keepdims=True)
    known[1:2, :] = jnp.sum(residual * second[...], axis=0, keepdims=True)


def step_kernel(early, known, late, out):
    step = row_sum(early[0:1, :]) / row_sum(early[1:2, :])
    out[...] = jnp.zeros_like(out)
    out[0:1, :] = known[0:1, :]
    out[1:2, :] = known[1:2, :] - step * late[0:1, :]


def last_kernel(start, first, second, third, early, final, solution, residual):
    norm_zero, product_zero = row_sum(early[0:1, :]), row_sum(early[1:2, :])
    norm_one, product_one = row_sum(final[0:1, :]), row_sum(final[1:2, :])
    step_zero = norm_zero / product_zero
    beta = norm_one / norm_zero
    step_one = norm_one / (product_one - beta * norm_one / step_zero)
    zeroth, once, twice = first[...], second[...], third[...]
    after = zeroth - step_zero * once
    image = once - step_zero * twice
    direction = after + beta * zeroth
    moved = image + beta * once
    solution[...] = start[...] + step_zero * zeroth + step_one * direction
    residual[...] = after - step_one * moved


def shards(
    start_factors,
    bin_factors,
    tile_speed,
    tile_weight,
    tile_cells,
    tile_count,
    inner_pairs,
    inner_weight,
    face_rows,
    face_count,
    face_weight,
):
    weights = tile_weight[0, 0]
    n_tiles, tile, _ = weights.shape
    inner = inner_weight[0, 0]
    n_inner = inner.shape[0]
    rows = face_rows[0, 0]
    n_face = rows.shape[1]
    own_rows, width = start_factors.shape
    n_bin = lax.axis_size("bin")
    part_rows = own_rows * n_bin
    bin_blocks = bin_factors.shape[0] // tile
    cells = tile_cells[0, 0].T
    pairs = inner_pairs[0, 0]

    face = face_weight[0, 0]
    face_even, face_odd = exchange_faces(face, face)

    rows_shape = (part_rows, width)
    tile_flops = 2 * tile * tile * width
    own_start, rhs, gain, bins_t, bins_s, inner_cat, diag, pick_hot, scatter_up, down_cat = call(
        functools.partial(prep_kernel, n_bin),
        [
            (start_factors.shape, f32),
            (rows_shape, f32),
            ((n_tiles, tile, tile), f32),
            ((bin_blocks, 2 * width, tile), bf16),
            ((bin_blocks, 2 * tile, width), bf16),
            ((n_inner, 2, tile, 3 * tile), bf16),
            (rows_shape, f32),
            ((2 * n_face, part_rows), bf16),
            ((part_rows, n_face), bf16),
            ((part_rows, 3 * n_face), bf16),
        ],
        start_factors, bin_factors, rows, face, inner, weights, tile_speed[0, 0],
        smem=(cells, tile_count, pairs, face_count[0]),
        hbm=True,
        scratch=[
            pltpu.VMEM(bin_factors.shape, bf16),
            pltpu.VMEM(rows.shape, jnp.int32),
            pltpu.VMEM(face.shape, f32),
            pltpu.VMEM(inner.shape, f32),
            pltpu.VMEM(weights.shape, bf16),
            pltpu.VMEM(weights.shape, bf16),
            pltpu.SemaphoreType.DMA((7,)),
        ],
        flops=n_tiles * tile_flops,
    )
    start_whole = gather_rows(start_factors, own_start)
    wide_cat = ((part_rows, 3 * n_face), bf16)
    cat_even, cat_odd = call(
        up_kernel, [wide_cat, wide_cat], face_even, face_odd, scatter_up, down_cat, flops=tile_flops
    )

    counts = face_count[0, 0].astype(f32)
    counts = jnp.where(lax.axis_index("seg") % 2 == 1, counts, counts[::-1])
    counts = jnp.broadcast_to(counts[:, None, None], (2, PAD, width)).reshape(2 * PAD, width)

    cat = ((part_rows, 2 * width), bf16)
    message = ((n_face, width), f32)
    sums = ((PAD, width), f32)

    def main(whole, whole_cat, diagonal, before=None):
        more = [] if before is None else [before]
        return call(
            main_kernel,
            [(rows_shape, f32)] + ([] if before is None else [sums]),
            whole, whole_cat, bins_t, bins_s, gain, inner_cat, diagonal, *more,
            smem=(cells, pairs),
            scratch=[pltpu.VMEM((n_tiles + 2 * n_inner, tile, width), f32)],
            flops=6 * n_tiles * tile_flops,
        )

    counted = ((n_face + PAD, width), f32)
    start_cat, even, odd = call(
        first_pick_kernel, [cat, counted, counted], start_whole, pick_hot, counts
    )
    even, odd = exchange_faces(even, odd)
    (part,) = main(start_whole, start_cat, diag)
    part, diag_all = call(
        first_face_kernel,
        [(rows_shape, f32), (rows_shape, f32)],
        even, odd, cat_even, cat_odd, part, start_whole, diag, rhs,
    )
    first = reduce_all(part)

    first_cat, even, odd = call(pick_kernel, [cat, message, message], first, pick_hot)
    even, odd = exchange_faces(even, odd)
    (part,) = main(first, first_cat, diag_all)
    (part,) = call(face_kernel, [(rows_shape, f32)], even, odd, cat_even, cat_odd, part)
    second = reduce_all(part)

    second_cat, even, odd = call(pick_kernel, [cat, message, message], second, pick_hot)
    even, odd = exchange_faces(even, odd)
    part, early = main(second, second_cat, diag_all, first)
    early = reduce_seg(early)
    part, late, known = call(
        last_face_kernel,
        [(rows_shape, f32), sums, sums],
        even, odd, cat_even, cat_odd, part, first, second, early,
    )
    third, late = reduce_own(part, late)
    (final,) = call(step_kernel, [sums], early, known, late)
    final = reduce_seg(final)
    offset = lax.axis_index("bin") * own_rows
    own = lambda whole: lax.dynamic_slice(whole, (offset, 0), (own_rows, width))
    return tuple(
        call(
            last_kernel,
            [(start_factors.shape, f32), (start_factors.shape, f32)],
            own_start, own(first), own(second), third, early, final,
        )
    )


def solution(mesh):
    return jax.shard_map(
        shards,
        mesh=mesh,
        in_specs=(
            P(("groups", "seg", "bin"), None),
            P(("groups", "bin"), None),
            P(("groups", "seg"), "bin", None, None, None),
            P(("groups", "seg"), "bin", None, None, None),
            P(("groups", "seg"), "bin", None, None),
            P(("groups", "seg"), "bin"),
            P(("groups", "seg"), "bin", None, None),
            P(("groups", "seg"), "bin", None, None, None),
            P(("groups", "seg"), "bin", None, None),
            P(("groups", "seg"), "bin", None),
            P(("groups", "seg"), "bin", None, None),
        ),
        out_specs=(P(("groups", "seg", "bin"), None), P(("groups", "seg", "bin"), None)),
        check_vma=False,
    )
```

time: 82.1 us -> 77.6 us (0.945)
  starting transfers between devices: 32 us -> 20.2 us
  waiting for transfers between devices: 28.4 us -> 33.5 us
  local copies, waits for them, and re-layouts: 4.18 us -> 8.99 us
  Pallas kernels: 14.2 us -> 11.9 us
    ppermute x16, starting transfers between devices: 19.1 us -> 12.5 us  [swap(): return lax.ppermute(x, axis, [(i, i ^ mask) for i in range(n)])]
    ppermute x7 -> x8, starting transfers between devices: 12.9 us -> 7.71 us  [the longest x4 6.93 us: exchange_faces(): got_even = lax.ppermute(message_even, ('seg', 'bin'), face_pairs(0))]
    unnamed x21 -> x36, local copies, waits for them, and re-layouts: 3.91 us -> 8.62 us
    ppermute x16, waiting for transfers between devices: 22.8 us -> 26.1 us  [swap(): return lax.ppermute(x, axis, [(i, i ^ mask) for i in range(n)])]
    pallas_call x13, Pallas kernels: 14.2 us -> 11.9 us  [call(): pl.pallas_call(kernel, out_shape=[jax.ShapeDtypeStruct(shape, kind) for s...]
    ppermute x7 -> x8, waiting for transfers between devices: 5.64 us -> 7.35 us  [the longest x4 7.34 us: exchange_faces(): got_even = lax.ppermute(message_even, ('seg', 'bin'), face_pairs(0))]
    another operation x7, other arithmetic: 0.97 us -> 0.13 us  [ordered(): return jnp.stack([first, second], dim)]
  transfers between devices with their start and end apart: 23 -> 24, of which waited for: 14 -> 18; matrix products, arithmetic and copies ran while one was open for 1% -> 1% of each run, Pallas kernels for 9% -> 9%
where the time goes in v3:
time: 77.6 us; the launch traced here: 77.2 us
  waiting for transfers between devices  33.5 us (43%)
  starting transfers between devices  20.2 us (26%)
  Pallas kernels  11.9 us (15%)
  local copies, waits for them, and re-layouts  8.99 us (12%)
  between operations  1.63 us (2%)
  other arithmetic  1 us (1%)
    ppermute x16, waiting for transfers between devices, swap(): return lax.ppermute(x, axis, [(i, i ^ mask) for i in range(n)])  26.1 us
    ppermute x16, starting transfers between devices, swap(): return lax.ppermute(x, axis, [(i, i ^ mask) for i in range(n)])  12.5 us
    pallas_call x13, Pallas kernels, call(): pl.pallas_call(kernel, out_shape=[jax.ShapeDtypeStruct(shape, kind) for s...  11.9 us
    unnamed x36, local copies, waits for them, and re-layouts  8.62 us
    ppermute x4, waiting for transfers between devices, exchange_faces(): got_even = lax.ppermute(message_even, ('seg', 'bin'), face_pairs(0))  7.34 us
    ppermute x4, starting transfers between devices, exchange_faces(): got_even = lax.ppermute(message_even, ('seg', 'bin'), face_pairs(0))  6.93 us
  transfers between devices with their start and end apart: 24, of which 18 were waited for; matrix products, arithmetic and copies ran while one was open for 1% of the time, Pallas kernels for 9%

profile of v3, /device:TPU:0, one launch (start us, length us, event | category | flops | bytes accessed | tf_op | source)
XLA Modules:
  0.0 77.2 jit_solution(14340767487802638428)
XLA Ops:
  1.2 4.1 %collective-permute-start.4 = (f32[256,256]{1,0:T(8,128)}, f32[256,256]{1,0:T(8,128)}, u32[]{:S(2)}, u32[]{:S(2)}) collective-permute-start(f32[256,256]{1,0:T(8,128)} %bitcast.85), channel_id=1, source_target_pairs={{0,4},{1,5},{2,6},{3,7},{4,0},{5,1},{6,2},{7,3},{8,12},{9,13},{10,... | collective-permute-start | bytes 786440 | tf_op jit(solution)/shard_map/ppermute | solution.py:120
  5.3 1.5 %collective-permute-start = (f32[1,128,128]{2,1,0:T(8,128)}, f32[1,128,128]{2,1,0:T(8,128)S(1)}, u32[]{:S(2)}, u32[]{:S(2)}) collective-permute-start(f32[1,128,128]{2,1,0:T(8,128)} %bitcast.88), channel_id=1, source_target_pairs={{0,2},{1,3},{2,0},{3,1},{4,6},{5,7},{6,4},{7,5},{8,10},{9,11},{10,... | collective-permute-start | bytes 196616 | tf_op jit(solution)/shard_map/ppermute | solution.py:25
  13.9 2.7 %shard_map.122 = (f32[128,128]{1,0:T(8,128)S(1)}, f32[512,128]{1,0:T(8,128)S(1)}, f32[12,128,128]{2,1,0:T(8,128)S(1)}, bf16[8,256,128]{2,1,0:T(8,128)(2,1)S(1)},...) custom-call(s32[2,12]{1,0:T(2,128)S(1)} %bitcast.89, ...), custom_call_target="tpu_custom_call" | custom-call | flops 50331648 | bytes 1509376 | tf_op jit(solution)/shard_map/pallas_call | solution.py:149
  19.7 1.4 %collective-permute-done.1 = f32[2,128,128]{2,1,0:T(8,128)S(1)} collective-permute-done((f32[2,128,128]{2,1,0:T(8,128)}, f32[2,128,128]{2,1,0:T(8,128)S(1)}, u32[]{:S(2)}, u32[]{:S(2)}) %collective-permute-start.1) | collective-permute-done | bytes 131104 | tf_op jit(solution)/shard_map/ppermute | solution.py:25
  21.9 1.4 %shard_map.125.part = f32[512,128]{1,0:T(8,128)S(1)} custom-call(s32[2,12]{1,0:T(2,128)S(1)} %bitcast.90, s32[2,2]{1,0:T(2,128)S(1)} %bitcast.94, f32[512,128]{1,0:T(8,128)S(1)} %bitcast.78, bf16[512,256]{1,0:T(8,128)(2,1)S(1)} %get-tuple-element.38.whole_cat, bf16[8,256,128]{2,1,0:T(8,128)(2,1)S(1)} %get-tuple-element.39.bins_t, ...), custom_call_target="tpu_custom_call" | custom-call | flops 301989888 | bytes 3014656 | tf_op jit(solution)/shard_map/pallas_call | solution.py:149
  23.4 1.4 %shard_map.124 = (bf16[512,768]{1,0:T(8,128)(2,1)S(1)}, bf16[512,768]{1,0:T(8,128)(2,1)S(1)}) custom-call(f32[256,256]{1,0:T(8,128)} %collective-permute-done.4.face_even, f32[256,256]{1,0:T(8,128)S(1)} %collective-permute-done.5.face_odd, bf16[512,256]{1,0:T(8,128)(2,1)S(1)} %copy-done.7, bf16[512,768]{1,0:T(8,128)(2,1)S(1)} %copy-done.1), custom_call_target="tpu_custom_call" | custom-call | flops 4194304 | bytes 1572864 | tf_op jit(solution)/shard_map/pallas_call | solution.py:149
  24.8 2.5 %collective-permute-done.2.even = f32[264,128]{1,0:T(8,128)S(1)} collective-permute-done((f32[264,128]{1,0:T(8,128)S(1)}, f32[264,128]{1,0:T(8,128)S(1)}, u32[]{:S(2)}, u32[]{:S(2)}) %collective-permute-start.2) | collective-permute-done | bytes 135200 | tf_op jit(solution)/shard_map/ppermute | solution.py:120
  28.0 1.3 %collective-permute-done.6 = f32[256,128]{1,0:T(8,128)S(1)} collective-permute-done((f32[256,128]{1,0:T(8,128)S(1)}, f32[256,128]{1,0:T(8,128)S(1)}, u32[]{:S(2)}, u32[]{:S(2)}) %collective-permute-start.6) | collective-permute-done | bytes 131104 | tf_op jit(solution)/shard_map/ppermute | solution.py:25
  30.0 5.0 %collective-permute-done.7 = f32[256,128]{1,0:T(8,128)S(1)} collective-permute-done((f32[256,128]{1,0:T(8,128)S(1)}, f32[256,128]{1,0:T(8,128)S(1)}, u32[]{:S(2)}, u32[]{:S(2)}) %collective-permute-start.7) | collective-permute-done | bytes 131104 | tf_op jit(solution)/shard_map/ppermute | solution.py:25
  35.1 1.3 %collective-permute-done.8 = f32[256,128]{1,0:T(8,128)S(1)} collective-permute-done((f32[256,128]{1,0:T(8,128)S(1)}, f32[256,128]{1,0:T(8,128)S(1)}, u32[]{:S(2)}, u32[]{:S(2)}) %collective-permute-start.8) | collective-permute-done | bytes 131104 | tf_op jit(solution)/shard_map/ppermute | solution.py:25
  36.8 1.8 %collective-permute-start.9 = (f32[256,128]{1,0:T(8,128)S(1)}, f32[256,128]{1,0:T(8,128)S(1)}, u32[]{:S(2)}, u32[]{:S(2)}) collective-permute-start(f32[256,128]{1,0:T(8,128)S(1)} %get-tuple-element.46), channel_id=1, source_target_pairs={{0,4},{1,5},{2,6},{3,7},{4,0},{5,1},{6,2},{7,3},{8,12},{9,13},{10,... | collective-permute-start | bytes 393224 | tf_op jit(solution)/shard_map/ppermute | solution.py:120
  38.6 1.4 %shard_map.128.part = f32[512,128]{1,0:T(8,128)S(1)} custom-call(s32[2,12]{1,0:T(2,128)S(1)} %bitcast.91, s32[2,2]{1,0:T(2,128)S(1)} %bitcast.95, f32[512,128]{1,0:T(8,128)S(1)} %bitcast.69, bf16[512,256]{1,0:T(8,128)(2,1)S(1)} %get-tuple-element.48.whole_cat, bf16[8,256,128]{2,1,0:T(8,128)(2,1)S(1)} %get-tuple-element.39.bins_t, ...), custom_call_target="tpu_custom_call" | custom-call | flops 301989888 | bytes 3014656 | tf_op jit(solution)/shard_map/pallas_call | solution.py:149
  40.0 2.4 %collective-permute-done.9.even = f32[256,128]{1,0:T(8,128)S(1)} collective-permute-done((f32[256,128]{1,0:T(8,128)S(1)}, f32[256,128]{1,0:T(8,128)S(1)}, u32[]{:S(2)}, u32[]{:S(2)}) %collective-permute-start.9) | collective-permute-done | bytes 131104 | tf_op jit(solution)/shard_map/ppermute | solution.py:120
  43.1 1.3 %collective-permute-done.11 = f32[256,128]{1,0:T(8,128)S(1)} collective-permute-done((f32[256,128]{1,0:T(8,128)S(1)}, f32[256,128]{1,0:T(8,128)S(1)}, u32[]{:S(2)}, u32[]{:S(2)}) %collective-permute-start.11) | collective-permute-done | bytes 131104 | tf_op jit(solution)/shard_map/ppermute | solution.py:25
  45.1 5.0 %collective-permute-done.12 = f32[256,128]{1,0:T(8,128)S(1)} collective-permute-done((f32[256,128]{1,0:T(8,128)S(1)}, f32[256,128]{1,0:T(8,128)S(1)}, u32[]{:S(2)}, u32[]{:S(2)}) %collective-permute-start.12) | collective-permute-done | bytes 131104 | tf_op jit(solution)/shard_map/ppermute | solution.py:25
  50.2 1.3 %collective-permute-done.13 = f32[256,128]{1,0:T(8,128)S(1)} collective-permute-done((f32[256,128]{1,0:T(8,128)S(1)}, f32[256,128]{1,0:T(8,128)S(1)}, u32[]{:S(2)}, u32[]{:S(2)}) %collective-permute-start.13) | collective-permute-done | bytes 131104 | tf_op jit(solution)/shard_map/ppermute | solution.py:25
  51.9 1.4 %shard_map.131 = (f32[512,128]{1,0:T(8,128)S(1)}, f32[8,128]{1,0:T(8,128)S(1)}) custom-call(s32[2,12]{1,0:T(2,128)S(1)} %bitcast.92, s32[2,2]{1,0:T(2,128)S(1)} %bitcast.96, f32[512,128]{1,0:T(8,128)S(1)} %bitcast.74, bf16[512,256]{1,0:T(8,128)(2,1)S(1)} %get-tuple-element.52.whole_cat, bf16[8,256,128]{2,1,0:T(8,128)(2,1)S(1)} %get-tuple-element.39.bins_t, ...), custom_call_target="tpu_custom_call" | custom-call | flops 301989888 | bytes 3276800 | tf_op jit(solution)/shard_map/pallas_call | solution.py:149
  53.3 1.4 %collective-permute-start.18 = (f32[8,128]{1,0:T(8,128)S(1)}, f32[8,128]{1,0:T(8,128)S(1)}, u32[]{:S(2)}, u32[]{:S(2)}) collective-permute-start(f32[8,128]{1,0:T(8,128)S(1)} %get-tuple-element.54), channel_id=1, source_target_pairs={{0,12},{4,8},{8,4},{12,0},{1,13},{5,9},{9,5},{13,1},{2,14},{6,10},... | collective-permute-start | bytes 12296 | tf_op jit(solution)/shard_map/ppermute | solution.py:25
  54.7 1.9 %collective-permute-start.17 = (f32[8,128]{1,0:T(8,128)S(1)}, f32[8,128]{1,0:T(8,128)S(1)}, u32[]{:S(2)}, u32[]{:S(2)}) collective-permute-start(f32[8,128]{1,0:T(8,128)S(1)} %get-tuple-element.54), channel_id=1, source_target_pairs={{0,8},{4,12},{8,0},{12,4},{1,9},{5,13},{9,1},{13,5},{2,10},{6,14},... | collective-permute-start | bytes 12296 | tf_op jit(solution)/shard_map/ppermute | solution.py:25
  60.3 2.4 %collective-permute-done.14.even = f32[256,128]{1,0:T(8,128)S(1)} collective-permute-done((f32[256,128]{1,0:T(8,128)S(1)}, f32[256,128]{1,0:T(8,128)S(1)}, u32[]{:S(2)}, u32[]{:S(2)}) %collective-permute-start.14) | collective-permute-done | bytes 131104 | tf_op jit(solution)/shard_map/ppermute | solution.py:120
  63.4 1.3 %collective-permute-done.19 = f32[264,128]{1,0:T(8,128)S(1)} collective-permute-done((f32[264,128]{1,0:T(8,128)S(1)}, f32[264,128]{1,0:T(8,128)S(1)}, u32[]{:S(2)}, u32[]{:S(2)}) %collective-permute-start.19) | collective-permute-done | bytes 135200 | tf_op jit(solution)/shard_map/ppermute | solution.py:25
  65.5 3.8 %collective-permute-done.20 = f32[136,128]{1,0:T(8,128)S(1)} collective-permute-done((f32[136,128]{1,0:T(8,128)S(1)}, f32[136,128]{1,0:T(8,128)S(1)}, u32[]{:S(2)}, u32[]{:S(2)}) %collective-permute-start.20) | collective-permute-done | bytes 69664 | tf_op jit(solution)/shard_map/ppermute | solution.py:25
  69.3 1.4 %collective-permute-start.23 = (f32[8,128]{1,0:T(8,128)S(1)}, f32[8,128]{1,0:T(8,128)S(1)}, u32[]{:S(2)}, u32[]{:S(2)}) collective-permute-start(f32[8,128]{1,0:T(8,128)S(1)} %shard_map.133), channel_id=1, source_target_pairs={{0,12},{4,8},{8,4},{12,0},{1,13},{5,9},{9,5},{13,1},{2,14},{6,10},... | collective-permute-start | bytes 12296 | tf_op jit(solution)/shard_map/ppermute | solution.py:25
  70.7 2.1 %collective-permute-start.22 = (f32[8,128]{1,0:T(8,128)S(1)}, f32[8,128]{1,0:T(8,128)S(1)}, u32[]{:S(2)}, u32[]{:S(2)}) collective-permute-start(f32[8,128]{1,0:T(8,128)S(1)} %shard_map.133), channel_id=1, source_target_pairs={{0,8},{4,12},{8,0},{12,4},{1,9},{5,13},{9,1},{13,5},{2,10},{6,14},... | collective-permute-start | bytes 12296 | tf_op jit(solution)/shard_map/ppermute | solution.py:25
  (107 shorter events, 23.8 us)
Async XLA Ops:
  0.6 22.7 %collective-permute-start.5 = (f32[256,256]{1,0:T(8,128)}, f32[256,256]{1,0:T(8,128)S(1)}, u32[]{:S(2)}, u32[]{:S(2)}) collective-permute-start(f32[256,256]{1,0:T(8,128)} %bitcast.84), channel_id=1, source_target_pairs={{0,1},{1,0},{2,3},{3,2},{4,8},{5,9},{6,10},{7,11},{8,4},{9,5},{10,... | collective-permute-start | bytes 786440 | tf_op jit(solution)/shard_map/ppermute | solution.py:121
  1.2 22.1 %collective-permute-start.4 = (f32[256,256]{1,0:T(8,128)}, f32[256,256]{1,0:T(8,128)}, u32[]{:S(2)}, u32[]{:S(2)}) collective-permute-start(f32[256,256]{1,0:T(8,128)} %bitcast.85), channel_id=1, source_target_pairs={{0,4},{1,5},{2,6},{3,7},{4,0},{5,1},{6,2},{7,3},{8,12},{9,13},{10,... | collective-permute-start | bytes 786440 | tf_op jit(solution)/shard_map/ppermute | solution.py:120
  5.3 12.9 %collective-permute-start = (f32[1,128,128]{2,1,0:T(8,128)}, f32[1,128,128]{2,1,0:T(8,128)S(1)}, u32[]{:S(2)}, u32[]{:S(2)}) collective-permute-start(f32[1,128,128]{2,1,0:T(8,128)} %bitcast.88), channel_id=1, source_target_pairs={{0,2},{1,3},{2,0},{3,1},{4,6},{5,7},{6,4},{7,5},{8,10},{9,11},{10,... | collective-permute-start | bytes 196616 | tf_op jit(solution)/shard_map/ppermute | solution.py:25
  19.6 1.6 %collective-permute-start.1 = (f32[2,128,128]{2,1,0:T(8,128)}, f32[2,128,128]{2,1,0:T(8,128)S(1)}, u32[]{:S(2)}, u32[]{:S(2)}) collective-permute-start(f32[2,128,128]{2,1,0:T(8,128)} %maximum_bitcast_fusion), channel_id=1, source_target_pairs={{0,1},{1,0},{2,3},{3,2},{4,5},{5,4},{6,7},{7,6},{8,9},{9,8},{10,11... | collective-permute-start | bytes 393224 | tf_op jit(solution)/shard_map/ppermute | solution.py:25
  21.6 5.7 %collective-permute-start.2 = (f32[264,128]{1,0:T(8,128)S(1)}, f32[264,128]{1,0:T(8,128)S(1)}, u32[]{:S(2)}, u32[]{:S(2)}) collective-permute-start(f32[264,128]{1,0:T(8,128)S(1)} %get-tuple-element.32), channel_id=1, source_target_pairs={{0,4},{1,5},{2,6},{3,7},{4,0},{5,1},{6,2},{7,3},{8,12},{9,13},{10,... | collective-permute-start | bytes 405512 | tf_op jit(solution)/shard_map/ppermute | solution.py:120
  21.7 5.6 %collective-permute-start.3 = (f32[264,128]{1,0:T(8,128)S(1)}, f32[264,128]{1,0:T(8,128)S(1)}, u32[]{:S(2)}, u32[]{:S(2)}) collective-permute-start(f32[264,128]{1,0:T(8,128)S(1)} %get-tuple-element.33), channel_id=1, source_target_pairs={{0,1},{1,0},{2,3},{3,2},{4,8},{5,9},{6,10},{7,11},{8,4},{9,5},{10,... | collective-permute-start | bytes 405512 | tf_op jit(solution)/shard_map/ppermute | solution.py:121
  27.9 1.4 %collective-permute-start.6 = (f32[256,128]{1,0:T(8,128)S(1)}, f32[256,128]{1,0:T(8,128)S(1)}, u32[]{:S(2)}, u32[]{:S(2)}) collective-permute-start(f32[256,128]{1,0:T(8,128)S(1)} %slice_select_fusion.1), channel_id=1, source_target_pairs={{0,1},{1,0},{2,3},{3,2},{4,5},{5,4},{6,7},{7,6},{8,9},{9,8},{10,11... | collective-permute-start | bytes 393224 | tf_op jit(solution)/shard_map/ppermute | solution.py:25
  29.4 5.6 %collective-permute-start.7 = (f32[256,128]{1,0:T(8,128)S(1)}, f32[256,128]{1,0:T(8,128)S(1)}, u32[]{:S(2)}, u32[]{:S(2)}) collective-permute-start(f32[256,128]{1,0:T(8,128)S(1)} %select_add_fusion.1), channel_id=1, source_target_pairs={{0,2},{1,3},{2,0},{3,1},{4,6},{5,7},{6,4},{7,5},{8,10},{9,11},{10,... | collective-permute-start | bytes 393224 | tf_op jit(solution)/shard_map/ppermute | solution.py:25
  35.0 1.4 %collective-permute-start.8 = (f32[256,128]{1,0:T(8,128)S(1)}, f32[256,128]{1,0:T(8,128)S(1)}, u32[]{:S(2)}, u32[]{:S(2)}) collective-permute-start(f32[256,128]{1,0:T(8,128)S(1)} %add.60), channel_id=1, source_target_pairs={{0,1},{1,0},{2,3},{3,2},{4,5},{5,4},{6,7},{7,6},{8,9},{9,8},{10,11... | collective-permute-start | bytes 393224 | tf_op jit(solution)/shard_map/ppermute | solution.py:25
  36.8 5.6 %collective-permute-start.9 = (f32[256,128]{1,0:T(8,128)S(1)}, f32[256,128]{1,0:T(8,128)S(1)}, u32[]{:S(2)}, u32[]{:S(2)}) collective-permute-start(f32[256,128]{1,0:T(8,128)S(1)} %get-tuple-element.46), channel_id=1, source_target_pairs={{0,4},{1,5},{2,6},{3,7},{4,0},{5,1},{6,2},{7,3},{8,12},{9,13},{10,... | collective-permute-start | bytes 393224 | tf_op jit(solution)/shard_map/ppermute | solution.py:120
  38.6 3.8 %collective-permute-start.10 = (f32[256,128]{1,0:T(8,128)S(1)}, f32[256,128]{1,0:T(8,128)S(1)}, u32[]{:S(2)}, u32[]{:S(2)}) collective-permute-start(f32[256,128]{1,0:T(8,128)S(1)} %get-tuple-element.47), channel_id=1, source_target_pairs={{0,1},{1,0},{2,3},{3,2},{4,8},{5,9},{6,10},{7,11},{8,4},{9,5},{10,... | collective-permute-start | bytes 393224 | tf_op jit(solution)/shard_map/ppermute | solution.py:121
  43.0 1.4 %collective-permute-start.11 = (f32[256,128]{1,0:T(8,128)S(1)}, f32[256,128]{1,0:T(8,128)S(1)}, u32[]{:S(2)}, u32[]{:S(2)}) collective-permute-start(f32[256,128]{1,0:T(8,128)S(1)} %slice_select_fusion), channel_id=1, source_target_pairs={{0,1},{1,0},{2,3},{3,2},{4,5},{5,4},{6,7},{7,6},{8,9},{9,8},{10,11... | collective-permute-start | bytes 393224 | tf_op jit(solution)/shard_map/ppermute | solution.py:25
  44.4 5.6 %collective-permute-start.12 = (f32[256,128]{1,0:T(8,128)S(1)}, f32[256,128]{1,0:T(8,128)S(1)}, u32[]{:S(2)}, u32[]{:S(2)}) collective-permute-start(f32[256,128]{1,0:T(8,128)S(1)} %select_add_fusion), channel_id=1, source_target_pairs={{0,2},{1,3},{2,0},{3,1},{4,6},{5,7},{6,4},{7,5},{8,10},{9,11},{10,... | collective-permute-start | bytes 393224 | tf_op jit(solution)/shard_map/ppermute | solution.py:25
  50.1 1.4 %collective-permute-start.13 = (f32[256,128]{1,0:T(8,128)S(1)}, f32[256,128]{1,0:T(8,128)S(1)}, u32[]{:S(2)}, u32[]{:S(2)}) collective-permute-start(f32[256,128]{1,0:T(8,128)S(1)} %add.63), channel_id=1, source_target_pairs={{0,1},{1,0},{2,3},{3,2},{4,5},{5,4},{6,7},{7,6},{8,9},{9,8},{10,11... | collective-permute-start | bytes 393224 | tf_op jit(solution)/shard_map/ppermute | solution.py:25
  53.3 5.5 %collective-permute-start.18 = (f32[8,128]{1,0:T(8,128)S(1)}, f32[8,128]{1,0:T(8,128)S(1)}, u32[]{:S(2)}, u32[]{:S(2)}) collective-permute-start(f32[8,128]{1,0:T(8,128)S(1)} %get-tuple-element.54), channel_id=1, source_target_pairs={{0,12},{4,8},{8,4},{12,0},{1,13},{5,9},{9,5},{13,1},{2,14},{6,10},... | collective-permute-start | bytes 12296 | tf_op jit(solution)/shard_map/ppermute | solution.py:25
  54.7 4.5 %collective-permute-start.17 = (f32[8,128]{1,0:T(8,128)S(1)}, f32[8,128]{1,0:T(8,128)S(1)}, u32[]{:S(2)}, u32[]{:S(2)}) collective-permute-start(f32[8,128]{1,0:T(8,128)S(1)} %get-tuple-element.54), channel_id=1, source_target_pairs={{0,8},{4,12},{8,0},{12,4},{1,9},{5,13},{9,1},{13,5},{2,10},{6,14},... | collective-permute-start | bytes 12296 | tf_op jit(solution)/shard_map/ppermute | solution.py:25
  56.6 3.7 %collective-permute-start.16 = (f32[8,128]{1,0:T(8,128)S(1)}, f32[8,128]{1,0:T(8,128)S(1)}, u32[]{:S(2)}, u32[]{:S(2)}) collective-permute-start(f32[8,128]{1,0:T(8,128)S(1)} %get-tuple-element.54), channel_id=1, source_target_pairs={{0,4},{4,0},{8,12},{12,8},{1,5},{5,1},{9,13},{13,9},{2,6},{6,2},{1... | collective-permute-start | bytes 12296 | tf_op jit(solution)/shard_map/ppermute | solution.py:25
  57.7 5.0 %collective-permute-start.14 = (f32[256,128]{1,0:T(8,128)S(1)}, f32[256,128]{1,0:T(8,128)S(1)}, u32[]{:S(2)}, u32[]{:S(2)}) collective-permute-start(f32[256,128]{1,0:T(8,128)S(1)} %get-tuple-element.50), channel_id=1, source_target_pairs={{0,4},{1,5},{2,6},{3,7},{4,0},{5,1},{6,2},{7,3},{8,12},{9,13},{10,... | collective-permute-start | bytes 393224 | tf_op jit(solution)/shard_map/ppermute | solution.py:120
  58.6 4.1 %collective-permute-start.15 = (f32[256,128]{1,0:T(8,128)S(1)}, f32[256,128]{1,0:T(8,128)S(1)}, u32[]{:S(2)}, u32[]{:S(2)}) collective-permute-start(f32[256,128]{1,0:T(8,128)S(1)} %get-tuple-element.51), channel_id=1, source_target_pairs={{0,1},{1,0},{2,3},{3,2},{4,8},{5,9},{6,10},{7,11},{8,4},{9,5},{10,... | collective-permute-start | bytes 393224 | tf_op jit(solution)/shard_map/ppermute | solution.py:121
  63.3 1.4 %collective-permute-start.19 = (f32[264,128]{1,0:T(8,128)S(1)}, f32[264,128]{1,0:T(8,128)S(1)}, u32[]{:S(2)}, u32[]{:S(2)}) collective-permute-start(f32[264,128]{1,0:T(8,128)S(1)} %pad_maximum_fusion.3), channel_id=1, source_target_pairs={{0,1},{1,0},{2,3},{3,2},{4,5},{5,4},{6,7},{7,6},{8,9},{9,8},{10,11... | collective-permute-start | bytes 405512 | tf_op jit(solution)/shard_map/ppermute | solution.py:25
  64.8 4.4 %collective-permute-start.20 = (f32[136,128]{1,0:T(8,128)S(1)}, f32[136,128]{1,0:T(8,128)S(1)}, u32[]{:S(2)}, u32[]{:S(2)}) collective-permute-start(f32[136,128]{1,0:T(8,128)S(1)} %pad_maximum_fusion.4), channel_id=1, source_target_pairs={{0,2},{1,3},{2,0},{3,1},{4,6},{5,7},{6,4},{7,5},{8,10},{9,11},{10,... | collective-permute-start | bytes 208904 | tf_op jit(solution)/shard_map/ppermute | solution.py:25
  69.3 5.4 %collective-permute-start.23 = (f32[8,128]{1,0:T(8,128)S(1)}, f32[8,128]{1,0:T(8,128)S(1)}, u32[]{:S(2)}, u32[]{:S(2)}) collective-permute-start(f32[8,128]{1,0:T(8,128)S(1)} %shard_map.133), channel_id=1, source_target_pairs={{0,12},{4,8},{8,4},{12,0},{1,13},{5,9},{9,5},{13,1},{2,14},{6,10},... | collective-permute-start | bytes 12296 | tf_op jit(solution)/shard_map/ppermute | solution.py:25
  70.7 4.5 %collective-permute-start.22 = (f32[8,128]{1,0:T(8,128)S(1)}, f32[8,128]{1,0:T(8,128)S(1)}, u32[]{:S(2)}, u32[]{:S(2)}) collective-permute-start(f32[8,128]{1,0:T(8,128)S(1)} %shard_map.133), channel_id=1, source_target_pairs={{0,8},{4,12},{8,0},{12,4},{1,9},{5,13},{9,1},{13,5},{2,10},{6,14},... | collective-permute-start | bytes 12296 | tf_op jit(solution)/shard_map/ppermute | solution.py:25
  72.8 3.6 %collective-permute-start.21 = (f32[8,128]{1,0:T(8,128)S(1)}, f32[8,128]{1,0:T(8,128)S(1)}, u32[]{:S(2)}, u32[]{:S(2)}) collective-permute-start(f32[8,128]{1,0:T(8,128)S(1)} %shard_map.133), channel_id=1, source_target_pairs={{0,4},{4,0},{8,12},{12,8},{1,5},{5,1},{9,13},{13,9},{2,6},{6,2},{1... | collective-permute-start | bytes 12296 | tf_op jit(solution)/shard_map/ppermute | solution.py:25
  (18 other events, 31.5 us)

commit v4 on v3

--- a/solution.py
+++ b/solution.py
@@ -7,7 +7,7 @@
 from jax.experimental.pallas import tpu as pltpu
 from jax.sharding import PartitionSpec as P
 
-ITERS = 2
+
 PAD = 8
 VMEM_BYTES = 16 << 20
 
@@ -42,7 +42,8 @@
     sent, held = own[None], copy[None]
     mask = n // 2
     while mask:
-        held = ordered(bit_of("bin", mask), held, swap(sent, "bin", mask), 1)
+        got = swap(sent, "bin", mask)
+        held = ordered(bit_of("bin", mask), held, got, 1)
         held = held.reshape((-1,) + own.shape)
         sent = held
         mask //= 2
@@ -141,15 +142,14 @@
     return jnp.concatenate([high, low, high], 0)
 
 
-def call(kernel, outs, *operands, smem=(), hbm=False, scratch=(), flops=0):
+def call(kernel, outs, *operands, smem=(), scratch=(), flops=0):
     in_smem = pl.BlockSpec(memory_space=pltpu.SMEM)
     in_vmem = pl.BlockSpec(memory_space=pltpu.VMEM)
-    given = pl.BlockSpec(memory_space=pltpu.HBM) if hbm else in_vmem
     nbytes = sum(o.size * o.dtype.itemsize for o in operands)
     return pl.pallas_call(
         kernel,
         out_shape=[jax.ShapeDtypeStruct(shape, kind) for shape, kind in outs],
-        in_specs=[in_smem] * len(smem) + [given] * len(operands),
+        in_specs=[in_smem] * len(smem) + [in_vmem] * len(operands),
         out_specs=[in_vmem] * len(outs),
         scratch_shapes=scratch,
         compiler_params=pltpu.CompilerParams(vmem_limit_bytes=VMEM_BYTES),
@@ -161,52 +161,44 @@
     return pl.ds(pl.multiple_of(index * size, size), size)
 
 
-def prep_kernel(n_bin, cells, count, pairs, faces,
-                start_hbm, bins_hbm, rows_hbm, face_hbm, inner_hbm, weights_hbm, speeds_hbm,
-                start, rhs, gain, bins_t, bins_s, inner_cat, diag, pick_hot, scatter_up, down_cat,
-                bins, rows, face, inner, weights, speeds, sems):
-    moves = [
-        pltpu.make_async_copy(source, target, sems.at[i])
-        for i, (source, target) in enumerate([
-            (rows_hbm, rows), (face_hbm, face), (start_hbm, start), (bins_hbm, bins),
-            (inner_hbm, inner), (weights_hbm, weights), (speeds_hbm, speeds),
-        ])
-    ]
-    for move in moves:
-        move.start()
-    n_tiles, tile, _ = weights.shape
-    width = bins.shape[1]
-    part_rows = rhs.shape[0]
-    n_face = rows.shape[1]
+def hot_kernel(faces, rows, own, pick_hot, scatter_low, scatter_up, counts, copy):
+    copy[...] = own[...]
+    part_rows, n_face = scatter_up.shape
     is_odd = lax.axis_index("seg") % 2 == 1
-    is_first = lax.axis_index("seg") == 0
-    rhs[...] = jnp.zeros_like(rhs)
-    diag[...] = jnp.full(diag.shape, ridge_weight / n_bin, f32)
     slots = lax.broadcasted_iota(jnp.int32, (1, n_face), 1)
     ids = lax.broadcasted_iota(jnp.int32, (part_rows, n_face), 0)
-    moves[0].wait()
     hots = []
     for side in range(2):
         listed = jnp.where(slots < faces[0, side], rows[side:side + 1, :], -1)
         hots.append((ids == listed).astype(f32))
+    scatter_low[...] = hots[0].astype(bf16)
     scatter_up[...] = hots[1].astype(bf16)
     low_t, up_t = hots[0].T.astype(bf16), hots[1].T.astype(bf16)
     pick_hot[0:n_face, :] = jnp.where(is_odd, low_t, up_t)
     pick_hot[n_face:, :] = jnp.where(is_odd, up_t, low_t)
-    moves[1].wait()
+    low_count, up_count = faces[0, 0], faces[0, 1]
+    shape = (PAD, counts.shape[1])
+    counts[0:PAD, :] = jnp.full(shape, jnp.where(is_odd, low_count, up_count), jnp.int32).astype(f32)
+    counts[PAD:, :] = jnp.full(shape, jnp.where(is_odd, up_count, low_count), jnp.int32).astype(f32)
+
+
+def prep_kernel(n_bin, cells, count, pairs, bins, face, inner, weights, speeds, scatter_low,
+                rhs, gain, bins_t, bins_s, inner_cat, diag, down_cat):
+    n_tiles, tile, _ = weights.shape
+    width = bins.shape[1]
+    is_first = lax.axis_index("seg") == 0
+    rhs[...] = jnp.zeros_like(rhs)
+    diag[...] = jnp.full(diag.shape, ridge_weight / n_bin, f32)
     high, low = split(jnp.where(is_first, 0.0, face[...]))
-    hot = hots[0].astype(bf16)
+    hot = scatter_low[...]
     high = dot(hot, high).astype(bf16)
     low = dot(hot, low).astype(bf16)
     down_cat[...] = jnp.concatenate([high, high, low], 1)
-    moves[2].wait()
-    moves[3].wait()
     for k in range(bins.shape[0] // tile):
         block = bins[k * tile:(k + 1) * tile, :]
         flipped = block.astype(f32).T.astype(bf16)
         bins_t[k] = jnp.concatenate([flipped, flipped], 0)
         bins_s[k] = jnp.concatenate([block, block], 0)
-    moves[4].wait()
     for j in range(inner.shape[0]):
         block = inner[j]
         flipped = block.T
@@ -215,8 +207,6 @@
         for side, matrix in enumerate((block, flipped)):
             degree = jnp.sum(matrix, axis=1, keepdims=True)
             diag[block_at(pairs[j, side], tile), :] += jnp.broadcast_to(degree, (tile, width))
-    moves[5].wait()
-    moves[6].wait()
     for k in range(n_tiles):
         wide = weights[k].astype(f32)
         live = jnp.where(k < count[0, 0], 1.0, 0.0).astype(f32)
@@ -386,43 +376,39 @@
 
     rows_shape = (part_rows, width)
     tile_flops = 2 * tile * tile * width
-    own_start, rhs, gain, bins_t, bins_s, inner_cat, diag, pick_hot, scatter_up, down_cat = call(
+    pick_hot, scatter_low, scatter_up, counts, own_start = call(
+        hot_kernel,
+        [
+            ((2 * n_face, part_rows), bf16),
+            ((part_rows, n_face), bf16),
+            ((part_rows, n_face), bf16),
+            ((2 * PAD, width), f32),
+            (start_factors.shape, f32),
+        ],
+        rows, start_factors,
+        smem=(face_count[0],),
+        flops=tile_flops,
+    )
+    start_whole = gather_rows(start_factors, own_start)
+    rhs, gain, bins_t, bins_s, inner_cat, diag, down_cat = call(
         functools.partial(prep_kernel, n_bin),
         [
-            (start_factors.shape, f32),
             (rows_shape, f32),
             ((n_tiles, tile, tile), f32),
             ((bin_blocks, 2 * width, tile), bf16),
             ((bin_blocks, 2 * tile, width), bf16),
             ((n_inner, 2, tile, 3 * tile), bf16),
             (rows_shape, f32),
-            ((2 * n_face, part_rows), bf16),
-            ((part_rows, n_face), bf16),
             ((part_rows, 3 * n_face), bf16),
         ],
-        start_factors, bin_factors, rows, face, inner, weights, tile_speed[0, 0],
-        smem=(cells, tile_count, pairs, face_count[0]),
-        hbm=True,
-        scratch=[
-            pltpu.VMEM(bin_factors.shape, bf16),
-            pltpu.VMEM(rows.shape, jnp.int32),
-            pltpu.VMEM(face.shape, f32),
-            pltpu.VMEM(inner.shape, f32),
-            pltpu.VMEM(weights.shape, bf16),
-            pltpu.VMEM(weights.shape, bf16),
-            pltpu.SemaphoreType.DMA((7,)),
-        ],
-        flops=n_tiles * tile_flops,
-    )
-    start_whole = gather_rows(start_factors, own_start)
+        bin_factors, face, inner, weights, tile_speed[0, 0], scatter_low,
+        smem=(cells, tile_count, pairs),
+        flops=3 * n_tiles * tile_flops,
+    )
     wide_cat = ((part_rows, 3 * n_face), bf16)
     cat_even, cat_odd = call(
         up_kernel, [wide_cat, wide_cat], face_even, face_odd, scatter_up, down_cat, flops=tile_flops
     )
-
-    counts = face_count[0, 0].astype(f32)
-    counts = jnp.where(lax.axis_index("seg") % 2 == 1, counts, counts[::-1])
-    counts = jnp.broadcast_to(counts[:, None, None], (2, PAD, width)).reshape(2 * PAD, width)
 
     cat = ((part_rows, 2 * width), bf16)
     message = ((n_face, width), f32)

time: 77.6 us -> 70.3 us (0.906)
  local copies, waits for them, and re-layouts: 8.99 us -> 3.09 us
  starting transfers between devices: 20.2 us -> 24.2 us
  waiting for transfers between devices: 33.5 us -> 30.9 us
  Pallas kernels: 11.9 us -> 9.96 us
    unnamed x36 -> x20, local copies, waits for them, and re-layouts: 8.62 us -> 3.05 us
    ppermute x16, starting transfers between devices: 12.5 us -> 17 us  [swap(): return lax.ppermute(x, axis, [(i, i ^ mask) for i in range(n)])]
    ppermute x16, waiting for transfers between devices: 26.1 us -> 23.1 us  [swap(): return lax.ppermute(x, axis, [(i, i ^ mask) for i in range(n)])]
    pallas_call x13 -> x14, Pallas kernels: 11.9 us -> 9.96 us  [call(): pl.pallas_call(kernel, out_shape=[jax.ShapeDtypeStruct(shape, kind) for s...]
  transfers between devices with their start and end apart: 24 -> 24, of which waited for: 18 -> 16; matrix products, arithmetic and copies ran while one was open for 1% -> 0% of each run, Pallas kernels for 9% -> 8%
where the time goes in v4:
time: 70.3 us; the launch traced here: 70.1 us
  waiting for transfers between devices  30.9 us (44%)
  starting transfers between devices  24.2 us (34%)
  Pallas kernels  9.96 us (14%)
  local copies, waits for them, and re-layouts  3.09 us (4%)
  between operations  1.65 us (2%)
    ppermute x16, waiting for transfers between devices, swap(): return lax.ppermute(x, axis, [(i, i ^ mask) for i in range(n)])  23.1 us
    ppermute x16, starting transfers between devices, swap(): return lax.ppermute(x, axis, [(i, i ^ mask) for i in range(n)])  17 us
    pallas_call x14, Pallas kernels, call(): pl.pallas_call(kernel, out_shape=[jax.ShapeDtypeStruct(shape, kind) for s...  9.96 us
    ppermute x4, waiting for transfers between devices, exchange_faces(): got_even = lax.ppermute(message_even, ('seg', 'bin'), face_pairs(0))  7.76 us
    ppermute x4, starting transfers between devices, exchange_faces(): got_even = lax.ppermute(message_even, ('seg', 'bin'), face_pairs(0))  7.08 us
    unnamed x20, local copies, waits for them, and re-layouts  3.05 us
  transfers between devices with their start and end apart: 24, of which 16 were waited for; matrix products, arithmetic and copies ran while one was open for 0% of the time, Pallas kernels for 8%

profile of v4, /device:TPU:0, one launch (start us, length us, event | category | flops | bytes accessed | tf_op | source)
XLA Modules:
  0.0 70.1 jit_solution(8644874512157840710)
XLA Ops:
  0.6 3.0 %collective-permute-start = (f32[1,128,128]{2,1,0:T(8,128)}, f32[1,128,128]{2,1,0:T(8,128)S(1)}, u32[]{:S(2)}, u32[]{:S(2)}) collective-permute-start(f32[1,128,128]{2,1,0:T(8,128)} %bitcast.84), channel_id=1, source_target_pairs={{0,2},{1,3},{2,0},{3,1},{4,6},{5,7},{6,4},{7,5},{8,10},{9,11},{10,... | collective-permute-start | bytes 196616 | tf_op jit(solution)/shard_map/ppermute | solution.py:25
  7.1 3.7 %collective-permute-start.4 = (f32[256,256]{1,0:T(8,128)S(1)}, f32[256,256]{1,0:T(8,128)S(1)}, u32[]{:S(2)}, u32[]{:S(2)}) collective-permute-start(f32[256,256]{1,0:T(8,128)S(1)} %bitcast.81), channel_id=1, source_target_pairs={{0,4},{1,5},{2,6},{3,7},{4,0},{5,1},{6,2},{7,3},{8,12},{9,13},{10,... | collective-permute-start | bytes 786440 | tf_op jit(solution)/shard_map/ppermute | solution.py:121
  13.8 1.4 %shard_map.126.part = f32[512,128]{1,0:T(8,128)S(1)} custom-call(s32[2,12]{1,0:T(2,128)S(1)} %bitcast.86, s32[2,2]{1,0:T(2,128)S(1)} %bitcast.90, f32[512,128]{1,0:T(8,128)S(1)} %bitcast.74, bf16[512,256]{1,0:T(8,128)(2,1)S(1)} %get-tuple-element.42.whole_cat, bf16[8,256,128]{2,1,0:T(8,128)(2,1)S(1)} %get-tuple-element.43.bins_t, ...), custom_call_target="tpu_custom_call" | custom-call | flops 301989888 | bytes 3014656 | tf_op jit(solution)/shard_map/pallas_call | solution.py:149
  15.2 2.7 %collective-permute-done.4.face_even = f32[256,256]{1,0:T(8,128)S(1)} collective-permute-done((f32[256,256]{1,0:T(8,128)S(1)}, f32[256,256]{1,0:T(8,128)S(1)}, u32[]{:S(2)}, u32[]{:S(2)}) %collective-permute-start.4) | collective-permute-done | bytes 262176 | tf_op jit(solution)/shard_map/ppermute | solution.py:121
  20.2 1.3 %collective-permute-done.6 = f32[256,128]{1,0:T(8,128)S(1)} collective-permute-done((f32[256,128]{1,0:T(8,128)S(1)}, f32[256,128]{1,0:T(8,128)S(1)}, u32[]{:S(2)}, u32[]{:S(2)}) %collective-permute-start.6) | collective-permute-done | bytes 131104 | tf_op jit(solution)/shard_map/ppermute | solution.py:25
  21.6 1.5 %collective-permute-start.7 = (f32[256,128]{1,0:T(8,128)S(1)}, f32[256,128]{1,0:T(8,128)S(1)}, u32[]{:S(2)}, u32[]{:S(2)}) collective-permute-start(f32[256,128]{1,0:T(8,128)S(1)} %select_add_fusion.1), channel_id=1, source_target_pairs={{0,2},{1,3},{2,0},{3,1},{4,6},{5,7},{6,4},{7,5},{8,10},{9,11},{10,... | collective-permute-start | bytes 393224 | tf_op jit(solution)/shard_map/ppermute | solution.py:25
  23.1 4.1 %collective-permute-done.7 = f32[256,128]{1,0:T(8,128)S(1)} collective-permute-done((f32[256,128]{1,0:T(8,128)S(1)}, f32[256,128]{1,0:T(8,128)S(1)}, u32[]{:S(2)}, u32[]{:S(2)}) %collective-permute-start.7) | collective-permute-done | bytes 131104 | tf_op jit(solution)/shard_map/ppermute | solution.py:25
  27.3 1.3 %collective-permute-done.8 = f32[256,128]{1,0:T(8,128)S(1)} collective-permute-done((f32[256,128]{1,0:T(8,128)S(1)}, f32[256,128]{1,0:T(8,128)S(1)}, u32[]{:S(2)}, u32[]{:S(2)}) %collective-permute-start.8) | collective-permute-done | bytes 131104 | tf_op jit(solution)/shard_map/ppermute | solution.py:25
  29.0 1.8 %collective-permute-start.9 = (f32[256,128]{1,0:T(8,128)S(1)}, f32[256,128]{1,0:T(8,128)S(1)}, u32[]{:S(2)}, u32[]{:S(2)}) collective-permute-start(f32[256,128]{1,0:T(8,128)S(1)} %get-tuple-element.50), channel_id=1, source_target_pairs={{0,4},{1,5},{2,6},{3,7},{4,0},{5,1},{6,2},{7,3},{8,12},{9,13},{10,... | collective-permute-start | bytes 393224 | tf_op jit(solution)/shard_map/ppermute | solution.py:121
  30.8 1.4 %shard_map.129.part = f32[512,128]{1,0:T(8,128)S(1)} custom-call(s32[2,12]{1,0:T(2,128)S(1)} %bitcast.87, s32[2,2]{1,0:T(2,128)S(1)} %bitcast.91, f32[512,128]{1,0:T(8,128)S(1)} %bitcast.65, bf16[512,256]{1,0:T(8,128)(2,1)S(1)} %get-tuple-element.52.whole_cat, bf16[8,256,128]{2,1,0:T(8,128)(2,1)S(1)} %get-tuple-element.43.bins_t, ...), custom_call_target="tpu_custom_call" | custom-call | flops 301989888 | bytes 3014656 | tf_op jit(solution)/shard_map/pallas_call | solution.py:149
  32.2 2.4 %collective-permute-done.9.even = f32[256,128]{1,0:T(8,128)S(1)} collective-permute-done((f32[256,128]{1,0:T(8,128)S(1)}, f32[256,128]{1,0:T(8,128)S(1)}, u32[]{:S(2)}, u32[]{:S(2)}) %collective-permute-start.9) | collective-permute-done | bytes 131104 | tf_op jit(solution)/shard_map/ppermute | solution.py:121
  35.3 1.3 %collective-permute-done.11 = f32[256,128]{1,0:T(8,128)S(1)} collective-permute-done((f32[256,128]{1,0:T(8,128)S(1)}, f32[256,128]{1,0:T(8,128)S(1)}, u32[]{:S(2)}, u32[]{:S(2)}) %collective-permute-start.11) | collective-permute-done | bytes 131104 | tf_op jit(solution)/shard_map/ppermute | solution.py:25
  36.6 1.6 %collective-permute-start.12 = (f32[256,128]{1,0:T(8,128)S(1)}, f32[256,128]{1,0:T(8,128)S(1)}, u32[]{:S(2)}, u32[]{:S(2)}) collective-permute-start(f32[256,128]{1,0:T(8,128)S(1)} %select_add_fusion), channel_id=1, source_target_pairs={{0,2},{1,3},{2,0},{3,1},{4,6},{5,7},{6,4},{7,5},{8,10},{9,11},{10,... | collective-permute-start | bytes 393224 | tf_op jit(solution)/shard_map/ppermute | solution.py:25
  38.2 4.1 %collective-permute-done.12 = f32[256,128]{1,0:T(8,128)S(1)} collective-permute-done((f32[256,128]{1,0:T(8,128)S(1)}, f32[256,128]{1,0:T(8,128)S(1)}, u32[]{:S(2)}, u32[]{:S(2)}) %collective-permute-start.12) | collective-permute-done | bytes 131104 | tf_op jit(solution)/shard_map/ppermute | solution.py:25
  42.4 1.3 %collective-permute-done.13 = f32[256,128]{1,0:T(8,128)S(1)} collective-permute-done((f32[256,128]{1,0:T(8,128)S(1)}, f32[256,128]{1,0:T(8,128)S(1)}, u32[]{:S(2)}, u32[]{:S(2)}) %collective-permute-start.13) | collective-permute-done | bytes 131104 | tf_op jit(solution)/shard_map/ppermute | solution.py:25
  44.1 1.4 %shard_map.132 = (f32[512,128]{1,0:T(8,128)S(1)}, f32[8,128]{1,0:T(8,128)S(1)}) custom-call(s32[2,12]{1,0:T(2,128)S(1)} %bitcast.88, s32[2,2]{1,0:T(2,128)S(1)} %bitcast.92, f32[512,128]{1,0:T(8,128)S(1)} %bitcast.70, bf16[512,256]{1,0:T(8,128)(2,1)S(1)} %get-tuple-element.56.whole_cat, bf16[8,256,128]{2,1,0:T(8,128)(2,1)S(1)} %get-tuple-element.43.bins_t, ...), custom_call_target="tpu_custom_call" | custom-call | flops 301989888 | bytes 3276800 | tf_op jit(solution)/shard_map/pallas_call | solution.py:149
  45.4 3.4 %collective-permute-start.18 = (f32[8,128]{1,0:T(8,128)S(1)}, f32[8,128]{1,0:T(8,128)S(1)}, u32[]{:S(2)}, u32[]{:S(2)}) collective-permute-start(f32[8,128]{1,0:T(8,128)S(1)} %get-tuple-element.58), channel_id=1, source_target_pairs={{0,12},{4,8},{8,4},{12,0},{1,13},{5,9},{9,5},{13,1},{2,14},{6,10},... | collective-permute-start | bytes 12296 | tf_op jit(solution)/shard_map/ppermute | solution.py:25
  49.9 1.5 %collective-permute-start.14 = (f32[256,128]{1,0:T(8,128)S(1)}, f32[256,128]{1,0:T(8,128)S(1)}, u32[]{:S(2)}, u32[]{:S(2)}) collective-permute-start(f32[256,128]{1,0:T(8,128)S(1)} %get-tuple-element.54), channel_id=1, source_target_pairs={{0,4},{1,5},{2,6},{3,7},{4,0},{5,1},{6,2},{7,3},{8,12},{9,13},{10,... | collective-permute-start | bytes 393224 | tf_op jit(solution)/shard_map/ppermute | solution.py:121
  51.4 2.0 %collective-permute-done.17 = f32[8,128]{1,0:T(8,128)S(1)} collective-permute-done((f32[8,128]{1,0:T(8,128)S(1)}, f32[8,128]{1,0:T(8,128)S(1)}, u32[]{:S(2)}, u32[]{:S(2)}) %collective-permute-start.17) | collective-permute-done | bytes 4128 | tf_op jit(solution)/shard_map/ppermute | solution.py:25
  53.4 1.5 %collective-permute-done.14.even = f32[256,128]{1,0:T(8,128)S(1)} collective-permute-done((f32[256,128]{1,0:T(8,128)S(1)}, f32[256,128]{1,0:T(8,128)S(1)}, u32[]{:S(2)}, u32[]{:S(2)}) %collective-permute-start.14) | collective-permute-done | bytes 131104 | tf_op jit(solution)/shard_map/ppermute | solution.py:121
  57.0 1.6 %collective-permute-start.20 = (f32[136,128]{1,0:T(8,128)S(1)}, f32[136,128]{1,0:T(8,128)S(1)}, u32[]{:S(2)}, u32[]{:S(2)}) collective-permute-start(f32[136,128]{1,0:T(8,128)S(1)} %pad_maximum_fusion.4), channel_id=1, source_target_pairs={{0,2},{1,3},{2,0},{3,1},{4,6},{5,7},{6,4},{7,5},{8,10},{9,11},{10,... | collective-permute-start | bytes 208904 | tf_op jit(solution)/shard_map/ppermute | solution.py:25
  58.6 2.8 %collective-permute-done.20 = f32[136,128]{1,0:T(8,128)S(1)} collective-permute-done((f32[136,128]{1,0:T(8,128)S(1)}, f32[136,128]{1,0:T(8,128)S(1)}, u32[]{:S(2)}, u32[]{:S(2)}) %collective-permute-start.20) | collective-permute-done | bytes 69664 | tf_op jit(solution)/shard_map/ppermute | solution.py:25
  61.5 3.3 %collective-permute-start.23 = (f32[8,128]{1,0:T(8,128)S(1)}, f32[8,128]{1,0:T(8,128)S(1)}, u32[]{:S(2)}, u32[]{:S(2)}) collective-permute-start(f32[8,128]{1,0:T(8,128)S(1)} %shard_map.134), channel_id=1, source_target_pairs={{0,12},{4,8},{8,4},{12,0},{1,13},{5,9},{9,5},{13,1},{2,14},{6,10},... | collective-permute-start | bytes 12296 | tf_op jit(solution)/shard_map/ppermute | solution.py:25
  66.9 2.4 %collective-permute-done.22 = f32[8,128]{1,0:T(8,128)S(1)} collective-permute-done((f32[8,128]{1,0:T(8,128)S(1)}, f32[8,128]{1,0:T(8,128)S(1)}, u32[]{:S(2)}, u32[]{:S(2)}) %collective-permute-start.22) | collective-permute-done | bytes 4128 | tf_op jit(solution)/shard_map/ppermute | solution.py:25
  (86 shorter events, 15.6 us)
Async XLA Ops:
  0.6 5.5 %collective-permute-start = (f32[1,128,128]{2,1,0:T(8,128)}, f32[1,128,128]{2,1,0:T(8,128)S(1)}, u32[]{:S(2)}, u32[]{:S(2)}) collective-permute-start(f32[1,128,128]{2,1,0:T(8,128)} %bitcast.84), channel_id=1, source_target_pairs={{0,2},{1,3},{2,0},{3,1},{4,6},{5,7},{6,4},{7,5},{8,10},{9,11},{10,... | collective-permute-start | bytes 196616 | tf_op jit(solution)/shard_map/ppermute | solution.py:25
  6.2 4.6 %collective-permute-start.1 = (f32[2,128,128]{2,1,0:T(8,128)S(1)}, f32[2,128,128]{2,1,0:T(8,128)S(1)}, u32[]{:S(2)}, u32[]{:S(2)}) collective-permute-start(f32[2,128,128]{2,1,0:T(8,128)S(1)} %maximum_bitcast_fusion), channel_id=1, source_target_pairs={{0,1},{1,0},{2,3},{3,2},{4,5},{5,4},{6,7},{7,6},{8,9},{9,8},{10,11... | collective-permute-start | bytes 393224 | tf_op jit(solution)/shard_map/ppermute | solution.py:25
  7.1 8.1 %collective-permute-start.5 = (f32[256,256]{1,0:T(8,128)S(1)}, f32[256,256]{1,0:T(8,128)S(1)}, u32[]{:S(2)}, u32[]{:S(2)}) collective-permute-start(f32[256,256]{1,0:T(8,128)S(1)} %bitcast.80), channel_id=1, source_target_pairs={{0,1},{1,0},{2,3},{3,2},{4,8},{5,9},{6,10},{7,11},{8,4},{9,5},{10,... | collective-permute-start | bytes 786440 | tf_op jit(solution)/shard_map/ppermute | solution.py:122
  7.1 10.8 %collective-permute-start.4 = (f32[256,256]{1,0:T(8,128)S(1)}, f32[256,256]{1,0:T(8,128)S(1)}, u32[]{:S(2)}, u32[]{:S(2)}) collective-permute-start(f32[256,256]{1,0:T(8,128)S(1)} %bitcast.81), channel_id=1, source_target_pairs={{0,4},{1,5},{2,6},{3,7},{4,0},{5,1},{6,2},{7,3},{8,12},{9,13},{10,... | collective-permute-start | bytes 786440 | tf_op jit(solution)/shard_map/ppermute | solution.py:121
  11.2 8.3 %collective-permute-start.2 = (f32[264,128]{1,0:T(8,128)S(1)}, f32[264,128]{1,0:T(8,128)S(1)}, u32[]{:S(2)}, u32[]{:S(2)}) collective-permute-start(f32[264,128]{1,0:T(8,128)S(1)} %get-tuple-element.35), channel_id=1, source_target_pairs={{0,4},{1,5},{2,6},{3,7},{4,0},{5,1},{6,2},{7,3},{8,12},{9,13},{10,... | collective-permute-start | bytes 405512 | tf_op jit(solution)/shard_map/ppermute | solution.py:121
  11.3 8.2 %collective-permute-start.3 = (f32[264,128]{1,0:T(8,128)S(1)}, f32[264,128]{1,0:T(8,128)S(1)}, u32[]{:S(2)}, u32[]{:S(2)}) collective-permute-start(f32[264,128]{1,0:T(8,128)S(1)} %get-tuple-element.36), channel_id=1, source_target_pairs={{0,1},{1,0},{2,3},{3,2},{4,8},{5,9},{6,10},{7,11},{8,4},{9,5},{10,... | collective-permute-start | bytes 405512 | tf_op jit(solution)/shard_map/ppermute | solution.py:122
  20.1 1.4 %collective-permute-start.6 = (f32[256,128]{1,0:T(8,128)S(1)}, f32[256,128]{1,0:T(8,128)S(1)}, u32[]{:S(2)}, u32[]{:S(2)}) collective-permute-start(f32[256,128]{1,0:T(8,128)S(1)} %slice_select_fusion.1), channel_id=1, source_target_pairs={{0,1},{1,0},{2,3},{3,2},{4,5},{5,4},{6,7},{7,6},{8,9},{9,8},{10,11... | collective-permute-start | bytes 393224 | tf_op jit(solution)/shard_map/ppermute | solution.py:25
  21.6 5.6 %collective-permute-start.7 = (f32[256,128]{1,0:T(8,128)S(1)}, f32[256,128]{1,0:T(8,128)S(1)}, u32[]{:S(2)}, u32[]{:S(2)}) collective-permute-start(f32[256,128]{1,0:T(8,128)S(1)} %select_add_fusion.1), channel_id=1, source_target_pairs={{0,2},{1,3},{2,0},{3,1},{4,6},{5,7},{6,4},{7,5},{8,10},{9,11},{10,... | collective-permute-start | bytes 393224 | tf_op jit(solution)/shard_map/ppermute | solution.py:25
  27.2 1.4 %collective-permute-start.8 = (f32[256,128]{1,0:T(8,128)S(1)}, f32[256,128]{1,0:T(8,128)S(1)}, u32[]{:S(2)}, u32[]{:S(2)}) collective-permute-start(f32[256,128]{1,0:T(8,128)S(1)} %add.55), channel_id=1, source_target_pairs={{0,1},{1,0},{2,3},{3,2},{4,5},{5,4},{6,7},{7,6},{8,9},{9,8},{10,11... | collective-permute-start | bytes 393224 | tf_op jit(solution)/shard_map/ppermute | solution.py:25
  29.0 5.6 %collective-permute-start.9 = (f32[256,128]{1,0:T(8,128)S(1)}, f32[256,128]{1,0:T(8,128)S(1)}, u32[]{:S(2)}, u32[]{:S(2)}) collective-permute-start(f32[256,128]{1,0:T(8,128)S(1)} %get-tuple-element.50), channel_id=1, source_target_pairs={{0,4},{1,5},{2,6},{3,7},{4,0},{5,1},{6,2},{7,3},{8,12},{9,13},{10,... | collective-permute-start | bytes 393224 | tf_op jit(solution)/shard_map/ppermute | solution.py:121
  30.8 3.8 %collective-permute-start.10 = (f32[256,128]{1,0:T(8,128)S(1)}, f32[256,128]{1,0:T(8,128)S(1)}, u32[]{:S(2)}, u32[]{:S(2)}) collective-permute-start(f32[256,128]{1,0:T(8,128)S(1)} %get-tuple-element.51), channel_id=1, source_target_pairs={{0,1},{1,0},{2,3},{3,2},{4,8},{5,9},{6,10},{7,11},{8,4},{9,5},{10,... | collective-permute-start | bytes 393224 | tf_op jit(solution)/shard_map/ppermute | solution.py:122
  35.2 1.4 %collective-permute-start.11 = (f32[256,128]{1,0:T(8,128)S(1)}, f32[256,128]{1,0:T(8,128)S(1)}, u32[]{:S(2)}, u32[]{:S(2)}) collective-permute-start(f32[256,128]{1,0:T(8,128)S(1)} %slice_select_fusion), channel_id=1, source_target_pairs={{0,1},{1,0},{2,3},{3,2},{4,5},{5,4},{6,7},{7,6},{8,9},{9,8},{10,11... | collective-permute-start | bytes 393224 | tf_op jit(solution)/shard_map/ppermute | solution.py:25
  36.6 5.6 %collective-permute-start.12 = (f32[256,128]{1,0:T(8,128)S(1)}, f32[256,128]{1,0:T(8,128)S(1)}, u32[]{:S(2)}, u32[]{:S(2)}) collective-permute-start(f32[256,128]{1,0:T(8,128)S(1)} %select_add_fusion), channel_id=1, source_target_pairs={{0,2},{1,3},{2,0},{3,1},{4,6},{5,7},{6,4},{7,5},{8,10},{9,11},{10,... | collective-permute-start | bytes 393224 | tf_op jit(solution)/shard_map/ppermute | solution.py:25
  42.3 1.4 %collective-permute-start.13 = (f32[256,128]{1,0:T(8,128)S(1)}, f32[256,128]{1,0:T(8,128)S(1)}, u32[]{:S(2)}, u32[]{:S(2)}) collective-permute-start(f32[256,128]{1,0:T(8,128)S(1)} %add.58), channel_id=1, source_target_pairs={{0,1},{1,0},{2,3},{3,2},{4,5},{5,4},{6,7},{7,6},{8,9},{9,8},{10,11... | collective-permute-start | bytes 393224 | tf_op jit(solution)/shard_map/ppermute | solution.py:25
  45.4 6.0 %collective-permute-start.18 = (f32[8,128]{1,0:T(8,128)S(1)}, f32[8,128]{1,0:T(8,128)S(1)}, u32[]{:S(2)}, u32[]{:S(2)}) collective-permute-start(f32[8,128]{1,0:T(8,128)S(1)} %get-tuple-element.58), channel_id=1, source_target_pairs={{0,12},{4,8},{8,4},{12,0},{1,13},{5,9},{9,5},{13,1},{2,14},{6,10},... | collective-permute-start | bytes 12296 | tf_op jit(solution)/shard_map/ppermute | solution.py:25
  48.8 4.6 %collective-permute-start.17 = (f32[8,128]{1,0:T(8,128)S(1)}, f32[8,128]{1,0:T(8,128)S(1)}, u32[]{:S(2)}, u32[]{:S(2)}) collective-permute-start(f32[8,128]{1,0:T(8,128)S(1)} %get-tuple-element.58), channel_id=1, source_target_pairs={{0,8},{4,12},{8,0},{12,4},{1,9},{5,13},{9,1},{13,5},{2,10},{6,14},... | collective-permute-start | bytes 12296 | tf_op jit(solution)/shard_map/ppermute | solution.py:25
  49.4 4.0 %collective-permute-start.16 = (f32[8,128]{1,0:T(8,128)S(1)}, f32[8,128]{1,0:T(8,128)S(1)}, u32[]{:S(2)}, u32[]{:S(2)}) collective-permute-start(f32[8,128]{1,0:T(8,128)S(1)} %get-tuple-element.58), channel_id=1, source_target_pairs={{0,4},{4,0},{8,12},{12,8},{1,5},{5,1},{9,13},{13,9},{2,6},{6,2},{1... | collective-permute-start | bytes 12296 | tf_op jit(solution)/shard_map/ppermute | solution.py:25
  49.9 5.0 %collective-permute-start.14 = (f32[256,128]{1,0:T(8,128)S(1)}, f32[256,128]{1,0:T(8,128)S(1)}, u32[]{:S(2)}, u32[]{:S(2)}) collective-permute-start(f32[256,128]{1,0:T(8,128)S(1)} %get-tuple-element.54), channel_id=1, source_target_pairs={{0,4},{1,5},{2,6},{3,7},{4,0},{5,1},{6,2},{7,3},{8,12},{9,13},{10,... | collective-permute-start | bytes 393224 | tf_op jit(solution)/shard_map/ppermute | solution.py:121
  51.4 3.5 %collective-permute-start.15 = (f32[256,128]{1,0:T(8,128)S(1)}, f32[256,128]{1,0:T(8,128)S(1)}, u32[]{:S(2)}, u32[]{:S(2)}) collective-permute-start(f32[256,128]{1,0:T(8,128)S(1)} %get-tuple-element.55), channel_id=1, source_target_pairs={{0,1},{1,0},{2,3},{3,2},{4,8},{5,9},{6,10},{7,11},{8,4},{9,5},{10,... | collective-permute-start | bytes 393224 | tf_op jit(solution)/shard_map/ppermute | solution.py:122
  55.5 1.4 %collective-permute-start.19 = (f32[264,128]{1,0:T(8,128)S(1)}, f32[264,128]{1,0:T(8,128)S(1)}, u32[]{:S(2)}, u32[]{:S(2)}) collective-permute-start(f32[264,128]{1,0:T(8,128)S(1)} %pad_maximum_fusion.3), channel_id=1, source_target_pairs={{0,1},{1,0},{2,3},{3,2},{4,5},{5,4},{6,7},{7,6},{8,9},{9,8},{10,11... | collective-permute-start | bytes 405512 | tf_op jit(solution)/shard_map/ppermute | solution.py:25
  57.0 4.4 %collective-permute-start.20 = (f32[136,128]{1,0:T(8,128)S(1)}, f32[136,128]{1,0:T(8,128)S(1)}, u32[]{:S(2)}, u32[]{:S(2)}) collective-permute-start(f32[136,128]{1,0:T(8,128)S(1)} %pad_maximum_fusion.4), channel_id=1, source_target_pairs={{0,2},{1,3},{2,0},{3,1},{4,6},{5,7},{6,4},{7,5},{8,10},{9,11},{10,... | collective-permute-start | bytes 208904 | tf_op jit(solution)/shard_map/ppermute | solution.py:25
  61.5 5.4 %collective-permute-start.23 = (f32[8,128]{1,0:T(8,128)S(1)}, f32[8,128]{1,0:T(8,128)S(1)}, u32[]{:S(2)}, u32[]{:S(2)}) collective-permute-start(f32[8,128]{1,0:T(8,128)S(1)} %shard_map.134), channel_id=1, source_target_pairs={{0,12},{4,8},{8,4},{12,0},{1,13},{5,9},{9,5},{13,1},{2,14},{6,10},... | collective-permute-start | bytes 12296 | tf_op jit(solution)/shard_map/ppermute | solution.py:25
  64.8 4.5 %collective-permute-start.22 = (f32[8,128]{1,0:T(8,128)S(1)}, f32[8,128]{1,0:T(8,128)S(1)}, u32[]{:S(2)}, u32[]{:S(2)}) collective-permute-start(f32[8,128]{1,0:T(8,128)S(1)} %shard_map.134), channel_id=1, source_target_pairs={{0,8},{4,12},{8,0},{12,4},{1,9},{5,13},{9,1},{13,5},{2,10},{6,14},... | collective-permute-start | bytes 12296 | tf_op jit(solution)/shard_map/ppermute | solution.py:25
  65.4 3.9 %collective-permute-start.21 = (f32[8,128]{1,0:T(8,128)S(1)}, f32[8,128]{1,0:T(8,128)S(1)}, u32[]{:S(2)}, u32[]{:S(2)}) collective-permute-start(f32[8,128]{1,0:T(8,128)S(1)} %shard_map.134), channel_id=1, source_target_pairs={{0,4},{4,0},{8,12},{12,8},{1,5},{5,1},{9,13},{13,9},{2,6},{6,2},{1... | collective-permute-start | bytes 12296 | tf_op jit(solution)/shard_map/ppermute | solution.py:25
  (10 other events, 9.9 us)

commit v5 on v4

--- a/solution.py
+++ b/solution.py
@@ -249,22 +249,22 @@
     odd[n_face:, :] = counts[PAD:, :]
 
 
-def pick_kernel(whole, pick_hot, whole_cat, even, odd):
-    picked = pick(whole, pick_hot, whole_cat)
-    n_face = picked.shape[0] // 2
-    even[...] = picked[:n_face]
-    odd[...] = picked[n_face:]
-
-
-def main_kernel(cells, pairs, whole, whole_cat, bins_t, bins_s, gain, inner_cat, diag, *refs):
-    if len(refs) == 4:
-        before, out, sums, terms = refs
+def pick_kernel(whole, pick_hot, *refs):
+    if len(refs) == 5:
+        before, whole_cat, even, odd, sums = refs
         now, old = whole[...], before[...]
         sums[...] = jnp.zeros_like(sums)
         sums[0:1, :] = jnp.sum(old * old, axis=0, keepdims=True)
         sums[1:2, :] = jnp.sum(old * now, axis=0, keepdims=True)
     else:
-        out, terms = refs
+        whole_cat, even, odd = refs
+    picked = pick(whole, pick_hot, whole_cat)
+    n_face = picked.shape[0] // 2
+    even[...] = picked[:n_face]
+    odd[...] = picked[n_face:]
+
+
+def main_kernel(cells, pairs, whole, whole_cat, bins_t, bins_s, gain, inner_cat, diag, out, terms):
     n_tiles, tile, _ = gain.shape
     width = whole.shape[1]
     for k in range(n_tiles):
@@ -414,23 +414,23 @@
     message = ((n_face, width), f32)
     sums = ((PAD, width), f32)
 
-    def main(whole, whole_cat, diagonal, before=None):
-        more = [] if before is None else [before]
-        return call(
+    def main(whole, whole_cat, diagonal):
+        (part,) = call(
             main_kernel,
-            [(rows_shape, f32)] + ([] if before is None else [sums]),
-            whole, whole_cat, bins_t, bins_s, gain, inner_cat, diagonal, *more,
+            [(rows_shape, f32)],
+            whole, whole_cat, bins_t, bins_s, gain, inner_cat, diagonal,
             smem=(cells, pairs),
             scratch=[pltpu.VMEM((n_tiles + 2 * n_inner, tile, width), f32)],
             flops=6 * n_tiles * tile_flops,
         )
+        return part
 
     counted = ((n_face + PAD, width), f32)
     start_cat, even, odd = call(
         first_pick_kernel, [cat, counted, counted], start_whole, pick_hot, counts
     )
     even, odd = exchange_faces(even, odd)
-    (part,) = main(start_whole, start_cat, diag)
+    part = main(start_whole, start_cat, diag)
     part, diag_all = call(
         first_face_kernel,
         [(rows_shape, f32), (rows_shape, f32)],
@@ -440,13 +440,15 @@
 
     first_cat, even, odd = call(pick_kernel, [cat, message, message], first, pick_hot)
     even, odd = exchange_faces(even, odd)
-    (part,) = main(first, first_cat, diag_all)
+    part = main(first, first_cat, diag_all)
     (part,) = call(face_kernel, [(rows_shape, f32)], even, odd, cat_even, cat_odd, part)
     second = reduce_all(part)
 
-    second_cat, even, odd = call(pick_kernel, [cat, message, message], second, pick_hot)
+    second_cat, even, odd, early = call(
+        pick_kernel, [cat, message, message, sums], second, pick_hot, first
+    )
     even, odd = exchange_faces(even, odd)
-    part, early = main(second, second_cat, diag_all, first)
+    part = main(second, second_cat, diag_all)
     early = reduce_seg(early)
     part, late, known = call(
         last_face_kernel,

time: 70.3 us -> 70.5 us (level)
    ppermute x4, waiting for transfers between devices: 7.76 us -> 9.3 us  [exchange_faces(): got_even = lax.ppermute(message_even, ('seg', 'bin'), face_pairs(0))]
    ppermute x16, waiting for transfers between devices: 23.1 us -> 21.6 us  [swap(): return lax.ppermute(x, axis, [(i, i ^ mask) for i in range(n)])]
  transfers between devices with their start and end apart: 24 -> 24, of which waited for: 16 -> 16; matrix products, arithmetic and copies ran while one was open for 0% -> 0% of each run, Pallas kernels for 8% -> 10%
where the time goes in v5:
time: 70.5 us; the launch traced here: 70.2 us
  waiting for transfers between devices  30.9 us (44%)
  starting transfers between devices  24.3 us (34%)
  Pallas kernels  9.99 us (14%)
  local copies, waits for them, and re-layouts  3.09 us (4%)
  between operations  1.65 us (2%)
    ppermute x16, waiting for transfers between devices, swap(): return lax.ppermute(x, axis, [(i, i ^ mask) for i in range(n)])  21.6 us
    ppermute x16, starting transfers between devices, swap(): return lax.ppermute(x, axis, [(i, i ^ mask) for i in range(n)])  17 us
    pallas_call x14, Pallas kernels, call(): pl.pallas_call(kernel, out_shape=[jax.ShapeDtypeStruct(shape, kind) for s...  9.99 us
    ppermute x4, waiting for transfers between devices, exchange_faces(): got_even = lax.ppermute(message_even, ('seg', 'bin'), face_pairs(0))  9.3 us
    ppermute x4, starting transfers between devices, exchange_faces(): got_even = lax.ppermute(message_even, ('seg', 'bin'), face_pairs(0))  7.15 us
    unnamed x20, local copies, waits for them, and re-layouts  3.05 us
  transfers between devices with their start and end apart: 24, of which 16 were waited for; matrix products, arithmetic and copies ran while one was open for 0% of the time, Pallas kernels for 10%

profile of v5, /device:TPU:0, one launch (start us, length us, event | category | flops | bytes accessed | tf_op | source)
XLA Modules:
  0.0 70.2 jit_solution(933274312656808174)
XLA Ops:
  0.6 3.0 %collective-permute-start = (f32[1,128,128]{2,1,0:T(8,128)}, f32[1,128,128]{2,1,0:T(8,128)S(1)}, u32[]{:S(2)}, u32[]{:S(2)}) collective-permute-start(f32[1,128,128]{2,1,0:T(8,128)} %bitcast.84), channel_id=1, source_target_pairs={{0,2},{1,3},{2,0},{3,1},{4,6},{5,7},{6,4},{7,5},{8,10},{9,11},{10,... | collective-permute-start | bytes 196616 | tf_op jit(solution)/shard_map/ppermute | solution.py:25
  7.1 3.7 %collective-permute-start.4 = (f32[256,256]{1,0:T(8,128)S(1)}, f32[256,256]{1,0:T(8,128)S(1)}, u32[]{:S(2)}, u32[]{:S(2)}) collective-permute-start(f32[256,256]{1,0:T(8,128)S(1)} %bitcast.81), channel_id=1, source_target_pairs={{0,4},{1,5},{2,6},{3,7},{4,0},{5,1},{6,2},{7,3},{8,12},{9,13},{10,... | collective-permute-start | bytes 786440 | tf_op jit(solution)/shard_map/ppermute | solution.py:121
  13.8 1.4 %shard_map.126.part = f32[512,128]{1,0:T(8,128)S(1)} custom-call(s32[2,12]{1,0:T(2,128)S(1)} %bitcast.86, s32[2,2]{1,0:T(2,128)S(1)} %bitcast.90, f32[512,128]{1,0:T(8,128)S(1)} %bitcast.74, bf16[512,256]{1,0:T(8,128)(2,1)S(1)} %get-tuple-element.41.whole_cat, bf16[8,256,128]{2,1,0:T(8,128)(2,1)S(1)} %get-tuple-element.42.bins_t, ...), custom_call_target="tpu_custom_call" | custom-call | flops 301989888 | bytes 3014656 | tf_op jit(solution)/shard_map/pallas_call | solution.py:149
  15.2 2.7 %collective-permute-done.4.face_even = f32[256,256]{1,0:T(8,128)S(1)} collective-permute-done((f32[256,256]{1,0:T(8,128)S(1)}, f32[256,256]{1,0:T(8,128)S(1)}, u32[]{:S(2)}, u32[]{:S(2)}) %collective-permute-start.4) | collective-permute-done | bytes 262176 | tf_op jit(solution)/shard_map/ppermute | solution.py:121
  20.2 1.3 %collective-permute-done.6 = f32[256,128]{1,0:T(8,128)S(1)} collective-permute-done((f32[256,128]{1,0:T(8,128)S(1)}, f32[256,128]{1,0:T(8,128)S(1)}, u32[]{:S(2)}, u32[]{:S(2)}) %collective-permute-start.6) | collective-permute-done | bytes 131104 | tf_op jit(solution)/shard_map/ppermute | solution.py:25
  21.6 1.6 %collective-permute-start.7 = (f32[256,128]{1,0:T(8,128)S(1)}, f32[256,128]{1,0:T(8,128)S(1)}, u32[]{:S(2)}, u32[]{:S(2)}) collective-permute-start(f32[256,128]{1,0:T(8,128)S(1)} %select_add_fusion.1), channel_id=1, source_target_pairs={{0,2},{1,3},{2,0},{3,1},{4,6},{5,7},{6,4},{7,5},{8,10},{9,11},{10,... | collective-permute-start | bytes 393224 | tf_op jit(solution)/shard_map/ppermute | solution.py:25
  23.1 4.1 %collective-permute-done.7 = f32[256,128]{1,0:T(8,128)S(1)} collective-permute-done((f32[256,128]{1,0:T(8,128)S(1)}, f32[256,128]{1,0:T(8,128)S(1)}, u32[]{:S(2)}, u32[]{:S(2)}) %collective-permute-start.7) | collective-permute-done | bytes 131104 | tf_op jit(solution)/shard_map/ppermute | solution.py:25
  27.3 1.3 %collective-permute-done.8 = f32[256,128]{1,0:T(8,128)S(1)} collective-permute-done((f32[256,128]{1,0:T(8,128)S(1)}, f32[256,128]{1,0:T(8,128)S(1)}, u32[]{:S(2)}, u32[]{:S(2)}) %collective-permute-start.8) | collective-permute-done | bytes 131104 | tf_op jit(solution)/shard_map/ppermute | solution.py:25
  29.0 1.8 %collective-permute-start.9 = (f32[256,128]{1,0:T(8,128)S(1)}, f32[256,128]{1,0:T(8,128)S(1)}, u32[]{:S(2)}, u32[]{:S(2)}) collective-permute-start(f32[256,128]{1,0:T(8,128)S(1)} %get-tuple-element.49), channel_id=1, source_target_pairs={{0,4},{1,5},{2,6},{3,7},{4,0},{5,1},{6,2},{7,3},{8,12},{9,13},{10,... | collective-permute-start | bytes 393224 | tf_op jit(solution)/shard_map/ppermute | solution.py:121
  30.8 1.4 %shard_map.129.part = f32[512,128]{1,0:T(8,128)S(1)} custom-call(s32[2,12]{1,0:T(2,128)S(1)} %bitcast.87, s32[2,2]{1,0:T(2,128)S(1)} %bitcast.91, f32[512,128]{1,0:T(8,128)S(1)} %bitcast.65, bf16[512,256]{1,0:T(8,128)(2,1)S(1)} %get-tuple-element.51.whole_cat, bf16[8,256,128]{2,1,0:T(8,128)(2,1)S(1)} %get-tuple-element.42.bins_t, ...), custom_call_target="tpu_custom_call" | custom-call | flops 301989888 | bytes 3014656 | tf_op jit(solution)/shard_map/pallas_call | solution.py:149
  32.1 2.4 %collective-permute-done.9.even = f32[256,128]{1,0:T(8,128)S(1)} collective-permute-done((f32[256,128]{1,0:T(8,128)S(1)}, f32[256,128]{1,0:T(8,128)S(1)}, u32[]{:S(2)}, u32[]{:S(2)}) %collective-permute-start.9) | collective-permute-done | bytes 131104 | tf_op jit(solution)/shard_map/ppermute | solution.py:121
  35.3 1.3 %collective-permute-done.11 = f32[256,128]{1,0:T(8,128)S(1)} collective-permute-done((f32[256,128]{1,0:T(8,128)S(1)}, f32[256,128]{1,0:T(8,128)S(1)}, u32[]{:S(2)}, u32[]{:S(2)}) %collective-permute-start.11) | collective-permute-done | bytes 131104 | tf_op jit(solution)/shard_map/ppermute | solution.py:25
  36.6 1.6 %collective-permute-start.12 = (f32[256,128]{1,0:T(8,128)S(1)}, f32[256,128]{1,0:T(8,128)S(1)}, u32[]{:S(2)}, u32[]{:S(2)}) collective-permute-start(f32[256,128]{1,0:T(8,128)S(1)} %select_add_fusion), channel_id=1, source_target_pairs={{0,2},{1,3},{2,0},{3,1},{4,6},{5,7},{6,4},{7,5},{8,10},{9,11},{10,... | collective-permute-start | bytes 393224 | tf_op jit(solution)/shard_map/ppermute | solution.py:25
  38.2 4.1 %collective-permute-done.12 = f32[256,128]{1,0:T(8,128)S(1)} collective-permute-done((f32[256,128]{1,0:T(8,128)S(1)}, f32[256,128]{1,0:T(8,128)S(1)}, u32[]{:S(2)}, u32[]{:S(2)}) %collective-permute-start.12) | collective-permute-done | bytes 131104 | tf_op jit(solution)/shard_map/ppermute | solution.py:25
  42.4 1.3 %collective-permute-done.13 = f32[256,128]{1,0:T(8,128)S(1)} collective-permute-done((f32[256,128]{1,0:T(8,128)S(1)}, f32[256,128]{1,0:T(8,128)S(1)}, u32[]{:S(2)}, u32[]{:S(2)}) %collective-permute-start.13) | collective-permute-done | bytes 131104 | tf_op jit(solution)/shard_map/ppermute | solution.py:25
  44.1 3.4 %collective-permute-start.18 = (f32[8,128]{1,0:T(8,128)S(1)}, f32[8,128]{1,0:T(8,128)S(1)}, u32[]{:S(2)}, u32[]{:S(2)}) collective-permute-start(f32[8,128]{1,0:T(8,128)S(1)} %get-tuple-element.56), channel_id=1, source_target_pairs={{0,12},{4,8},{8,4},{12,0},{1,13},{5,9},{9,5},{13,1},{2,14},{6,10},... | collective-permute-start | bytes 12296 | tf_op jit(solution)/shard_map/ppermute | solution.py:25
  48.6 1.4 %shard_map.132.part = f32[512,128]{1,0:T(8,128)S(1)} custom-call(s32[2,12]{1,0:T(2,128)S(1)} %bitcast.88, s32[2,2]{1,0:T(2,128)S(1)} %bitcast.92, f32[512,128]{1,0:T(8,128)S(1)} %bitcast.70, bf16[512,256]{1,0:T(8,128)(2,1)S(1)} %get-tuple-element.55.whole_cat, bf16[8,256,128]{2,1,0:T(8,128)(2,1)S(1)} %get-tuple-element.42.bins_t, ...), custom_call_target="tpu_custom_call" | custom-call | flops 301989888 | bytes 3014656 | tf_op jit(solution)/shard_map/pallas_call | solution.py:149
  50.0 1.6 %collective-permute-start.14 = (f32[256,128]{1,0:T(8,128)S(1)}, f32[256,128]{1,0:T(8,128)S(1)}, u32[]{:S(2)}, u32[]{:S(2)}) collective-permute-start(f32[256,128]{1,0:T(8,128)S(1)} %get-tuple-element.53), channel_id=1, source_target_pairs={{0,4},{1,5},{2,6},{3,7},{4,0},{5,1},{6,2},{7,3},{8,12},{9,13},{10,... | collective-permute-start | bytes 393224 | tf_op jit(solution)/shard_map/ppermute | solution.py:121
  52.0 3.0 %collective-permute-done.14.even = f32[256,128]{1,0:T(8,128)S(1)} collective-permute-done((f32[256,128]{1,0:T(8,128)S(1)}, f32[256,128]{1,0:T(8,128)S(1)}, u32[]{:S(2)}, u32[]{:S(2)}) %collective-permute-start.14) | collective-permute-done | bytes 131104 | tf_op jit(solution)/shard_map/ppermute | solution.py:121
  55.7 1.3 %collective-permute-done.19 = f32[264,128]{1,0:T(8,128)S(1)} collective-permute-done((f32[264,128]{1,0:T(8,128)S(1)}, f32[264,128]{1,0:T(8,128)S(1)}, u32[]{:S(2)}, u32[]{:S(2)}) %collective-permute-start.19) | collective-permute-done | bytes 135200 | tf_op jit(solution)/shard_map/ppermute | solution.py:25
  57.1 1.6 %collective-permute-start.20 = (f32[136,128]{1,0:T(8,128)S(1)}, f32[136,128]{1,0:T(8,128)S(1)}, u32[]{:S(2)}, u32[]{:S(2)}) collective-permute-start(f32[136,128]{1,0:T(8,128)S(1)} %pad_maximum_fusion.4), channel_id=1, source_target_pairs={{0,2},{1,3},{2,0},{3,1},{4,6},{5,7},{6,4},{7,5},{8,10},{9,11},{10,... | collective-permute-start | bytes 208904 | tf_op jit(solution)/shard_map/ppermute | solution.py:25
  58.7 2.8 %collective-permute-done.20 = f32[136,128]{1,0:T(8,128)S(1)} collective-permute-done((f32[136,128]{1,0:T(8,128)S(1)}, f32[136,128]{1,0:T(8,128)S(1)}, u32[]{:S(2)}, u32[]{:S(2)}) %collective-permute-start.20) | collective-permute-done | bytes 69664 | tf_op jit(solution)/shard_map/ppermute | solution.py:25
  61.6 3.3 %collective-permute-start.23 = (f32[8,128]{1,0:T(8,128)S(1)}, f32[8,128]{1,0:T(8,128)S(1)}, u32[]{:S(2)}, u32[]{:S(2)}) collective-permute-start(f32[8,128]{1,0:T(8,128)S(1)} %shard_map.134), channel_id=1, source_target_pairs={{0,12},{4,8},{8,4},{12,0},{1,13},{5,9},{9,5},{13,1},{2,14},{6,10},... | collective-permute-start | bytes 12296 | tf_op jit(solution)/shard_map/ppermute | solution.py:25
  67.0 2.4 %collective-permute-done.22 = f32[8,128]{1,0:T(8,128)S(1)} collective-permute-done((f32[8,128]{1,0:T(8,128)S(1)}, f32[8,128]{1,0:T(8,128)S(1)}, u32[]{:S(2)}, u32[]{:S(2)}) %collective-permute-start.22) | collective-permute-done | bytes 4128 | tf_op jit(solution)/shard_map/ppermute | solution.py:25
  (86 shorter events, 14.8 us)
Async XLA Ops:
  0.6 5.5 %collective-permute-start = (f32[1,128,128]{2,1,0:T(8,128)}, f32[1,128,128]{2,1,0:T(8,128)S(1)}, u32[]{:S(2)}, u32[]{:S(2)}) collective-permute-start(f32[1,128,128]{2,1,0:T(8,128)} %bitcast.84), channel_id=1, source_target_pairs={{0,2},{1,3},{2,0},{3,1},{4,6},{5,7},{6,4},{7,5},{8,10},{9,11},{10,... | collective-permute-start | bytes 196616 | tf_op jit(solution)/shard_map/ppermute | solution.py:25
  6.2 4.6 %collective-permute-start.1 = (f32[2,128,128]{2,1,0:T(8,128)S(1)}, f32[2,128,128]{2,1,0:T(8,128)S(1)}, u32[]{:S(2)}, u32[]{:S(2)}) collective-permute-start(f32[2,128,128]{2,1,0:T(8,128)S(1)} %maximum_bitcast_fusion), channel_id=1, source_target_pairs={{0,1},{1,0},{2,3},{3,2},{4,5},{5,4},{6,7},{7,6},{8,9},{9,8},{10,11... | collective-permute-start | bytes 393224 | tf_op jit(solution)/shard_map/ppermute | solution.py:25
  7.1 8.1 %collective-permute-start.5 = (f32[256,256]{1,0:T(8,128)S(1)}, f32[256,256]{1,0:T(8,128)S(1)}, u32[]{:S(2)}, u32[]{:S(2)}) collective-permute-start(f32[256,256]{1,0:T(8,128)S(1)} %bitcast.80), channel_id=1, source_target_pairs={{0,1},{1,0},{2,3},{3,2},{4,8},{5,9},{6,10},{7,11},{8,4},{9,5},{10,... | collective-permute-start | bytes 786440 | tf_op jit(solution)/shard_map/ppermute | solution.py:122
  7.1 10.8 %collective-permute-start.4 = (f32[256,256]{1,0:T(8,128)S(1)}, f32[256,256]{1,0:T(8,128)S(1)}, u32[]{:S(2)}, u32[]{:S(2)}) collective-permute-start(f32[256,256]{1,0:T(8,128)S(1)} %bitcast.81), channel_id=1, source_target_pairs={{0,4},{1,5},{2,6},{3,7},{4,0},{5,1},{6,2},{7,3},{8,12},{9,13},{10,... | collective-permute-start | bytes 786440 | tf_op jit(solution)/shard_map/ppermute | solution.py:121
  11.2 8.3 %collective-permute-start.2 = (f32[264,128]{1,0:T(8,128)S(1)}, f32[264,128]{1,0:T(8,128)S(1)}, u32[]{:S(2)}, u32[]{:S(2)}) collective-permute-start(f32[264,128]{1,0:T(8,128)S(1)} %get-tuple-element.34), channel_id=1, source_target_pairs={{0,4},{1,5},{2,6},{3,7},{4,0},{5,1},{6,2},{7,3},{8,12},{9,13},{10,... | collective-permute-start | bytes 405512 | tf_op jit(solution)/shard_map/ppermute | solution.py:121
  11.3 8.2 %collective-permute-start.3 = (f32[264,128]{1,0:T(8,128)S(1)}, f32[264,128]{1,0:T(8,128)S(1)}, u32[]{:S(2)}, u32[]{:S(2)}) collective-permute-start(f32[264,128]{1,0:T(8,128)S(1)} %get-tuple-element.35), channel_id=1, source_target_pairs={{0,1},{1,0},{2,3},{3,2},{4,8},{5,9},{6,10},{7,11},{8,4},{9,5},{10,... | collective-permute-start | bytes 405512 | tf_op jit(solution)/shard_map/ppermute | solution.py:122
  20.1 1.4 %collective-permute-start.6 = (f32[256,128]{1,0:T(8,128)S(1)}, f32[256,128]{1,0:T(8,128)S(1)}, u32[]{:S(2)}, u32[]{:S(2)}) collective-permute-start(f32[256,128]{1,0:T(8,128)S(1)} %slice_select_fusion.1), channel_id=1, source_target_pairs={{0,1},{1,0},{2,3},{3,2},{4,5},{5,4},{6,7},{7,6},{8,9},{9,8},{10,11... | collective-permute-start | bytes 393224 | tf_op jit(solution)/shard_map/ppermute | solution.py:25
  21.6 5.6 %collective-permute-start.7 = (f32[256,128]{1,0:T(8,128)S(1)}, f32[256,128]{1,0:T(8,128)S(1)}, u32[]{:S(2)}, u32[]{:S(2)}) collective-permute-start(f32[256,128]{1,0:T(8,128)S(1)} %select_add_fusion.1), channel_id=1, source_target_pairs={{0,2},{1,3},{2,0},{3,1},{4,6},{5,7},{6,4},{7,5},{8,10},{9,11},{10,... | collective-permute-start | bytes 393224 | tf_op jit(solution)/shard_map/ppermute | solution.py:25
  27.2 1.4 %collective-permute-start.8 = (f32[256,128]{1,0:T(8,128)S(1)}, f32[256,128]{1,0:T(8,128)S(1)}, u32[]{:S(2)}, u32[]{:S(2)}) collective-permute-start(f32[256,128]{1,0:T(8,128)S(1)} %add.55), channel_id=1, source_target_pairs={{0,1},{1,0},{2,3},{3,2},{4,5},{5,4},{6,7},{7,6},{8,9},{9,8},{10,11... | collective-permute-start | bytes 393224 | tf_op jit(solution)/shard_map/ppermute | solution.py:25
  29.0 5.6 %collective-permute-start.9 = (f32[256,128]{1,0:T(8,128)S(1)}, f32[256,128]{1,0:T(8,128)S(1)}, u32[]{:S(2)}, u32[]{:S(2)}) collective-permute-start(f32[256,128]{1,0:T(8,128)S(1)} %get-tuple-element.49), channel_id=1, source_target_pairs={{0,4},{1,5},{2,6},{3,7},{4,0},{5,1},{6,2},{7,3},{8,12},{9,13},{10,... | collective-permute-start | bytes 393224 | tf_op jit(solution)/shard_map/ppermute | solution.py:121
  30.8 3.8 %collective-permute-start.10 = (f32[256,128]{1,0:T(8,128)S(1)}, f32[256,128]{1,0:T(8,128)S(1)}, u32[]{:S(2)}, u32[]{:S(2)}) collective-permute-start(f32[256,128]{1,0:T(8,128)S(1)} %get-tuple-element.50), channel_id=1, source_target_pairs={{0,1},{1,0},{2,3},{3,2},{4,8},{5,9},{6,10},{7,11},{8,4},{9,5},{10,... | collective-permute-start | bytes 393224 | tf_op jit(solution)/shard_map/ppermute | solution.py:122
  35.2 1.4 %collective-permute-start.11 = (f32[256,128]{1,0:T(8,128)S(1)}, f32[256,128]{1,0:T(8,128)S(1)}, u32[]{:S(2)}, u32[]{:S(2)}) collective-permute-start(f32[256,128]{1,0:T(8,128)S(1)} %slice_select_fusion), channel_id=1, source_target_pairs={{0,1},{1,0},{2,3},{3,2},{4,5},{5,4},{6,7},{7,6},{8,9},{9,8},{10,11... | collective-permute-start | bytes 393224 | tf_op jit(solution)/shard_map/ppermute | solution.py:25
  36.6 5.6 %collective-permute-start.12 = (f32[256,128]{1,0:T(8,128)S(1)}, f32[256,128]{1,0:T(8,128)S(1)}, u32[]{:S(2)}, u32[]{:S(2)}) collective-permute-start(f32[256,128]{1,0:T(8,128)S(1)} %select_add_fusion), channel_id=1, source_target_pairs={{0,2},{1,3},{2,0},{3,1},{4,6},{5,7},{6,4},{7,5},{8,10},{9,11},{10,... | collective-permute-start | bytes 393224 | tf_op jit(solution)/shard_map/ppermute | solution.py:25
  42.3 1.4 %collective-permute-start.13 = (f32[256,128]{1,0:T(8,128)S(1)}, f32[256,128]{1,0:T(8,128)S(1)}, u32[]{:S(2)}, u32[]{:S(2)}) collective-permute-start(f32[256,128]{1,0:T(8,128)S(1)} %add.58), channel_id=1, source_target_pairs={{0,1},{1,0},{2,3},{3,2},{4,5},{5,4},{6,7},{7,6},{8,9},{9,8},{10,11... | collective-permute-start | bytes 393224 | tf_op jit(solution)/shard_map/ppermute | solution.py:25
  44.1 7.5 %collective-permute-start.18 = (f32[8,128]{1,0:T(8,128)S(1)}, f32[8,128]{1,0:T(8,128)S(1)}, u32[]{:S(2)}, u32[]{:S(2)}) collective-permute-start(f32[8,128]{1,0:T(8,128)S(1)} %get-tuple-element.56), channel_id=1, source_target_pairs={{0,12},{4,8},{8,4},{12,0},{1,13},{5,9},{9,5},{13,1},{2,14},{6,10},... | collective-permute-start | bytes 12296 | tf_op jit(solution)/shard_map/ppermute | solution.py:25
  47.5 4.5 %collective-permute-start.17 = (f32[8,128]{1,0:T(8,128)S(1)}, f32[8,128]{1,0:T(8,128)S(1)}, u32[]{:S(2)}, u32[]{:S(2)}) collective-permute-start(f32[8,128]{1,0:T(8,128)S(1)} %get-tuple-element.56), channel_id=1, source_target_pairs={{0,8},{4,12},{8,0},{12,4},{1,9},{5,13},{9,1},{13,5},{2,10},{6,14},... | collective-permute-start | bytes 12296 | tf_op jit(solution)/shard_map/ppermute | solution.py:25
  48.1 3.9 %collective-permute-start.16 = (f32[8,128]{1,0:T(8,128)S(1)}, f32[8,128]{1,0:T(8,128)S(1)}, u32[]{:S(2)}, u32[]{:S(2)}) collective-permute-start(f32[8,128]{1,0:T(8,128)S(1)} %get-tuple-element.56), channel_id=1, source_target_pairs={{0,4},{4,0},{8,12},{12,8},{1,5},{5,1},{9,13},{13,9},{2,6},{6,2},{1... | collective-permute-start | bytes 12296 | tf_op jit(solution)/shard_map/ppermute | solution.py:25
  50.0 5.0 %collective-permute-start.14 = (f32[256,128]{1,0:T(8,128)S(1)}, f32[256,128]{1,0:T(8,128)S(1)}, u32[]{:S(2)}, u32[]{:S(2)}) collective-permute-start(f32[256,128]{1,0:T(8,128)S(1)} %get-tuple-element.53), channel_id=1, source_target_pairs={{0,4},{1,5},{2,6},{3,7},{4,0},{5,1},{6,2},{7,3},{8,12},{9,13},{10,... | collective-permute-start | bytes 393224 | tf_op jit(solution)/shard_map/ppermute | solution.py:121
  51.6 3.4 %collective-permute-start.15 = (f32[256,128]{1,0:T(8,128)S(1)}, f32[256,128]{1,0:T(8,128)S(1)}, u32[]{:S(2)}, u32[]{:S(2)}) collective-permute-start(f32[256,128]{1,0:T(8,128)S(1)} %get-tuple-element.54), channel_id=1, source_target_pairs={{0,1},{1,0},{2,3},{3,2},{4,8},{5,9},{6,10},{7,11},{8,4},{9,5},{10,... | collective-permute-start | bytes 393224 | tf_op jit(solution)/shard_map/ppermute | solution.py:122
  55.6 1.4 %collective-permute-start.19 = (f32[264,128]{1,0:T(8,128)S(1)}, f32[264,128]{1,0:T(8,128)S(1)}, u32[]{:S(2)}, u32[]{:S(2)}) collective-permute-start(f32[264,128]{1,0:T(8,128)S(1)} %pad_maximum_fusion.3), channel_id=1, source_target_pairs={{0,1},{1,0},{2,3},{3,2},{4,5},{5,4},{6,7},{7,6},{8,9},{9,8},{10,11... | collective-permute-start | bytes 405512 | tf_op jit(solution)/shard_map/ppermute | solution.py:25
  57.1 4.4 %collective-permute-start.20 = (f32[136,128]{1,0:T(8,128)S(1)}, f32[136,128]{1,0:T(8,128)S(1)}, u32[]{:S(2)}, u32[]{:S(2)}) collective-permute-start(f32[136,128]{1,0:T(8,128)S(1)} %pad_maximum_fusion.4), channel_id=1, source_target_pairs={{0,2},{1,3},{2,0},{3,1},{4,6},{5,7},{6,4},{7,5},{8,10},{9,11},{10,... | collective-permute-start | bytes 208904 | tf_op jit(solution)/shard_map/ppermute | solution.py:25
  61.6 5.4 %collective-permute-start.23 = (f32[8,128]{1,0:T(8,128)S(1)}, f32[8,128]{1,0:T(8,128)S(1)}, u32[]{:S(2)}, u32[]{:S(2)}) collective-permute-start(f32[8,128]{1,0:T(8,128)S(1)} %shard_map.134), channel_id=1, source_target_pairs={{0,12},{4,8},{8,4},{12,0},{1,13},{5,9},{9,5},{13,1},{2,14},{6,10},... | collective-permute-start | bytes 12296 | tf_op jit(solution)/shard_map/ppermute | solution.py:25
  64.9 4.5 %collective-permute-start.22 = (f32[8,128]{1,0:T(8,128)S(1)}, f32[8,128]{1,0:T(8,128)S(1)}, u32[]{:S(2)}, u32[]{:S(2)}) collective-permute-start(f32[8,128]{1,0:T(8,128)S(1)} %shard_map.134), channel_id=1, source_target_pairs={{0,8},{4,12},{8,0},{12,4},{1,9},{5,13},{9,1},{13,5},{2,10},{6,14},... | collective-permute-start | bytes 12296 | tf_op jit(solution)/shard_map/ppermute | solution.py:25
  65.6 3.9 %collective-permute-start.21 = (f32[8,128]{1,0:T(8,128)S(1)}, f32[8,128]{1,0:T(8,128)S(1)}, u32[]{:S(2)}, u32[]{:S(2)}) collective-permute-start(f32[8,128]{1,0:T(8,128)S(1)} %shard_map.134), channel_id=1, source_target_pairs={{0,4},{4,0},{8,12},{12,8},{1,5},{5,1},{9,13},{13,9},{2,6},{6,2},{1... | collective-permute-start | bytes 12296 | tf_op jit(solution)/shard_map/ppermute | solution.py:25
  (10 other events, 9.9 us)
